TPU v7x, 256 devices: a whole 4x4x8 slice. The times are simulated.
256 devices in a mesh: gz: 2 (over core), gx: 16 (over y, x), gy: 8 (over z).
Axes of the slice: x: 4, y: 4, z: 8, core: 2. Of those that a mesh axis runs over, the one named last changes fastest.
Arguments:
- positions: float32 [128, 3, 65536], P(('gz', 'gy'), None, 'gx'), may hold values from -8 to 8
- diffusion_noise: float32 [128, 3, 65536], P(('gz', 'gy'), None, 'gx'), may hold values from -5 to 5
- base_nuclei: float32 [16, 3], replicated, may hold values from -4.15 to 4.15, as said below
- displacements: float32 [8, 16, 3], replicated, may hold values from -0.4375 to 0.4375
- charges: float32 [16], replicated, may hold values from 2 to 14
- orbital_decay: float32 [16], replicated, may hold values from 0.6 to 2
- coefficients: float32 [16], replicated, may hold values from 0.5 to 2
- weights: float32 [65536], P('gx'), may hold values from 0.5 to 2
- counts: int32 [512], P('gx'), may hold values from 1 to 128
- branch_source: int32 [512], replicated, may hold values from 0 to 511, as said below
Outputs:
- local_energy: float32 [8, 65536], P('gz', 'gx')
- energy_estimate: float32 [8], P('gz')
- new_positions: float32 [128, 3, 65536], P(('gz', 'gy'), None, 'gx')
- new_weights: float32 [65536], P('gx')
Inputs may be any that keep to these rules, and one draw needn't show every extreme that they name: `branch_source`: A permutation of the blocks. Of the 32 destination blocks of each aligned group (d // 32 equal), at most 4 have sources in any one aligned group of 32 source blocks, and some pair reaches 4 for every group, as sender and as receiver. `base_nuclei`: any two nuclei lie 1.7 or more apart.
All inputs are finite; a program needn't handle non-finite values.
Results may differ from a plain program's by a relative error of at most 0.0002.
Values sent between devices are 32-bit elements; how exact they have to be, the bound alone decides.
No kernel may reach another device: no remote copies, remote signals or barrier semaphores. Data moves between devices by JAX's collectives and lax.ppermute only.
A program may use at most 64 MiB of HBM per device.

v0:
```python
import functools
import math

import jax
import jax.numpy as jnp
from jax import lax
from jax.sharding import Mesh
from jax.sharding import PartitionSpec as P

NE = 128
BLK = 128
GX = ("gx_0", "gx_1")


soft_square = 0.04
cusp_value = 0.5
jastrow_range = 1.0
time_step = 0.01
step_root = 0.1


def in_blocks(x, dim, peers):
    shape = x.shape
    parts = x.reshape(*shape[:dim], peers, shape[dim] // peers, *shape[dim + 1 :])
    return jnp.moveaxis(parts, dim, 0)


def laid_out(parts, dim):
    shape = list(parts.shape[1:])
    shape[dim] *= parts.shape[0]
    return jnp.moveaxis(parts, 0, dim).reshape(shape)


def turned_blocks(parts, axes, sequence):
    inside = parts.shape[1:]
    out = parts.reshape(*(lax.axis_size(a) for a in axes), *inside)
    for k in sequence:
        out = lax.all_to_all(out, axes[k], k, k, tiled=True)
    return out.reshape(-1, *inside)


def one_axis_at_a_time(x, axes, sequence, split_dim, concat_dim):
    parts = in_blocks(x, split_dim, lax.axis_size(axes))
    return laid_out(turned_blocks(parts, axes, sequence), concat_dim)


def sent_together(arrays, axis, dim, along):
    widths = [a.shape[along] for a in arrays]
    both = jnp.concatenate(arrays, axis=along)
    out = lax.all_gather(both, axis, axis=dim, tiled=True)
    return tuple(jnp.split(out, [sum(widths[:k]) for k in range(1, len(widths))], axis=along))


def over_axes(x, axes):
    return functools.reduce(lax.psum, axes, x)


def side_by_side(arrays, axis, split_dim, concat_dim, along):
    ends, at = ([], 0)
    for a in arrays[:-1]:
        at += a.shape[along]
        ends.append(at)
    both = jnp.concatenate(arrays, axis=along)
    return tuple(
        jnp.split(
            lax.all_to_all(both, axis, split_axis=split_dim, concat_axis=concat_dim, tiled=True),
            ends,
            axis=along,
        )
    )


def orbital_terms(coords, centers, charges, orbital_decay, coefficients):
    offsets = coords[:, None, :, :] - centers[None, :, :, None]
    square_dist = jnp.sum(offsets * offsets, axis=2)
    distance = jnp.sqrt(square_dist + soft_square)
    decay = orbital_decay[None, :, None]
    orbital_part = coefficients[None, :, None] * jnp.exp(-decay * distance)
    orbital = jnp.sum(orbital_part, axis=1)
    grad_orbital = jnp.sum((-decay * orbital_part / distance)[:, :, None, :] * offsets, axis=1)
    lap_orbital = jnp.sum(
        orbital_part
        * (
            decay * decay * square_dist / (distance * distance)
            - decay * (2.0 * distance * distance + soft_square) / (distance * distance * distance)
        ),
        axis=1,
    )
    grad_log = grad_orbital / orbital[:, None, :]
    potential = -jnp.sum(charges[None, :, None] / distance, axis=1)
    return (jnp.log(orbital), grad_log, lap_orbital / orbital, potential)


def pair_terms(coords, others, coord_index, other_index):
    offsets = coords[:, None, :, :] - others[None, :, :, :]
    square_dist = jnp.sum(offsets * offsets, axis=2)
    distance = jnp.sqrt(square_dist + soft_square)
    keeping = (coord_index[:, None] != other_index[None, :]).astype(jnp.float32)[:, :, None]
    denominator = 1.0 + jastrow_range * distance
    slope = keeping * cusp_value / (denominator * denominator)
    bending = (
        keeping * (-2.0 * cusp_value * jastrow_range) / (denominator * denominator * denominator)
    )
    gradient = jnp.sum((slope / distance)[:, :, None, :] * offsets, axis=1)
    laplacian = jnp.sum(
        bending * square_dist / (distance * distance)
        + slope * (2.0 * distance * distance + soft_square) / (distance * distance * distance),
        axis=1,
    )
    coulomb = 0.5 * jnp.sum(keeping / distance, axis=1)
    return (gradient, laplacian, coulomb)


def nuclear_repulsion(centers, charges):
    offsets = centers[:, None, :] - centers[None, :, :]
    identity = jnp.eye(centers.shape[0], dtype=jnp.float32)
    distance = jnp.sqrt(jnp.sum(offsets * offsets, axis=2) + identity)
    return 0.5 * jnp.sum(charges[:, None] * charges[None, :] * (1.0 - identity) / distance)


def electron_energy(grad_log, laplace_ratio, potential, jgrad, jlap, coulomb):
    total_grad = grad_log + jgrad
    kinetic = -0.5 * (
        laplace_ratio
        - jnp.sum(grad_log * grad_log, axis=1)
        + jlap
        + jnp.sum(total_grad * total_grad, axis=1)
    )
    return kinetic + potential + coulomb


def pair_folder(coords, coord_index, totals, shard_rows):
    row_count = shard_rows.shape[0]
    group_size = math.gcd(row_count, 16)

    def one_group(turn, running):
        others = lax.dynamic_slice_in_dim(shard_rows, turn * group_size, group_size, 0)
        other_index = turn * group_size + jnp.arange(group_size, dtype=jnp.int32)
        gradient, laplacian, coulomb = pair_terms(coords, others, coord_index, other_index)
        return (running[0] + gradient, running[1] + laplacian, running[2] + coulomb)

    return lax.fori_loop(0, row_count // group_size, one_group, totals)


def geometry_sums(coords, centers_list, charges, orbital_decay, coefficients, jgrad, jlap, coulomb):
    energies = []
    log_sums = []
    drift_grad = None
    for position, centers in enumerate(centers_list):
        log_orbital, grad_log, laplace_ratio, potential = orbital_terms(
            coords, centers, charges, orbital_decay, coefficients
        )
        energies.append(
            jnp.sum(
                electron_energy(grad_log, laplace_ratio, potential, jgrad, jlap, coulomb), axis=0
            )
        )
        log_sums.append(jnp.sum(log_orbital, axis=0))
        if position == 0:
            drift_grad = grad_log + jgrad
    return (jnp.stack(energies), jnp.stack(log_sums), coords + time_step * drift_grad)


def local(
    positions,
    diffusion_noise,
    base_nuclei,
    displacements,
    charges,
    orbital_decay,
    coefficients,
    weights,
    counts,
    branch_source,
):
    own_count = positions.shape[0]
    walkers = positions.shape[2]
    geometries = displacements.shape[0]
    per_replica = geometries // lax.axis_size("gz")
    replica = lax.axis_index("gz")
    centers = base_nuclei[None, :, :] + displacements
    whole_walkers = one_axis_at_a_time(positions, ("gz", "gy"), (0, 1), 2, 0)
    electron_total = whole_walkers.shape[0]
    few_walkers = whole_walkers.shape[2]
    coord_index = jnp.arange(electron_total, dtype=jnp.int32)
    start_totals = (
        jnp.zeros((electron_total, 3, few_walkers), jnp.float32),
        jnp.zeros((electron_total, few_walkers), jnp.float32),
        jnp.zeros((electron_total, few_walkers), jnp.float32),
    )
    jgrad, jlap, coulomb = pair_folder(whole_walkers, coord_index, start_totals, whole_walkers)
    centers_list = [centers[geometry] for geometry in range(geometries)]
    energies, log_sums, drift_whole = geometry_sums(
        whole_walkers, centers_list, charges, orbital_decay, coefficients, jgrad, jlap, coulomb
    )
    energies, log_sums = sent_together((energies, log_sums), ("gz", "gy"), 1, 0)
    drifted = lax.all_to_all(drift_whole, ("gz", "gy"), split_axis=0, concat_axis=2, tiled=True)
    energies = jnp.concatenate(
        [lax.dynamic_slice_in_dim(energies, replica * per_replica, per_replica, 0), energies[0:1]],
        axis=0,
    )
    log_sums = jnp.concatenate(
        [lax.dynamic_slice_in_dim(log_sums, replica * per_replica, per_replica, 0), log_sums[0:1]],
        axis=0,
    )
    chosen_centers = jnp.concatenate(
        [lax.dynamic_slice_in_dim(centers, replica * per_replica, per_replica, 0), centers[0:1]],
        axis=0,
    )
    nuclear_energy = jnp.stack(
        [
            nuclear_repulsion(chosen_centers[geometry], charges)
            for geometry in range(per_replica + 1)
        ]
    )
    local_energy = (energies + nuclear_energy[:, None]) / NE
    alive_mask = (
        (jnp.arange(BLK, dtype=jnp.int32)[None, :] < counts[:, None])
        .astype(jnp.float32)
        .reshape(walkers)
    )
    weight_ratio = jnp.exp(2.0 * (log_sums - log_sums[-1:]))
    sample_weight = weights[None, :] * weight_ratio * alive_mask[None, :]
    numerator, denominator = (
        over_axes(jnp.sum(sample_weight * local_energy, axis=1), GX),
        over_axes(jnp.sum(sample_weight, axis=1), GX),
    )
    estimate = numerator / denominator
    kept_weights = alive_mask * weights * jnp.exp(-(local_energy[-1] - estimate[-1]))
    moved_positions = drifted + step_root * diffusion_noise
    blocks_here = counts.shape[0]
    block_total = branch_source.shape[0]
    device = lax.axis_index(GX)
    coord_blocks = moved_positions.reshape(own_count * 3, blocks_here, BLK)
    weight_blocks = kept_weights.reshape(1, blocks_here, BLK)
    my_sources = lax.dynamic_slice_in_dim(branch_source, device * blocks_here, blocks_here, 0)
    peers = lax.axis_size(GX)
    capacity = max(2, 2 * blocks_here // peers)
    block_range = jnp.arange(blocks_here, dtype=jnp.int32)
    own_ids = device * blocks_here + block_range
    matches = (branch_source[None, :] == own_ids[:, None]).astype(jnp.int32)
    dest_slot = jnp.sum(matches * jnp.arange(block_total, dtype=jnp.int32)[None, :], axis=1)
    dest_device = dest_slot // blocks_here
    earlier = (
        (dest_device[None, :] == dest_device[:, None]) & (dest_slot[None, :] < dest_slot[:, None])
    ).astype(jnp.int32)
    send_slot = dest_device * capacity + jnp.sum(earlier, axis=1)
    selection = (
        jnp.arange(peers * capacity, dtype=jnp.int32)[:, None] == send_slot[None, :]
    ).astype(jnp.int32)
    picked = jnp.sum(selection * block_range[None, :], axis=1)
    occupied = jnp.sum(selection, axis=1).astype(jnp.float32)
    send_coords = jnp.take(coord_blocks, picked, axis=1) * occupied[None, :, None]
    send_weights = jnp.take(weight_blocks, picked, axis=1) * occupied[None, :, None]
    recv_coords, recv_weights = side_by_side((send_coords, send_weights), GX, 1, 1, 0)
    source_device = my_sources // blocks_here
    before = (
        (source_device[None, :] == source_device[:, None])
        & (block_range[None, :] < block_range[:, None])
    ).astype(jnp.int32)
    slot_index = source_device * capacity + jnp.sum(before, axis=1)
    new_coords = jnp.take(recv_coords, slot_index, axis=1)
    new_weight_blocks = jnp.take(recv_weights, slot_index, axis=1)
    new_positions = new_coords.reshape(own_count, 3, walkers)
    new_weights = new_weight_blocks.reshape(walkers)
    return (local_energy[:-1], estimate[:-1], new_positions, new_weights)


def solution(mesh):
    split = Mesh(
        mesh.devices.reshape(mesh.shape["gz"], 4, 4, mesh.shape["gy"]), ("gz", "gx_0", "gx_1", "gy")
    )
    placed = (
        P(("gz", "gy"), None, GX),
        P(("gz", "gy"), None, GX),
        P(),
        P(),
        P(),
        P(),
        P(),
        P(GX),
        P(GX),
        P(),
    )
    return jax.shard_map(
        local,
        mesh=split,
        in_specs=placed,
        out_specs=(P("gz", GX), P("gz"), P(("gz", "gy"), None, GX), P(GX)),
        check_vma=False,
    )
```

profile of v0, /device:TPU:32, one launch (start us, length us, event | category | flops | bytes accessed | tf_op | source)
XLA Modules:
  0.0 269.8 jit_solution(5065399208477810434)
XLA Ops:
  1.8 4.0 %all_to_all.33 = f32[2,8,8,3,256]{4,2,3,1,0:T(8,128)S(1)} all-to-all(f32[2,8,8,3,256]{4,2,3,1,0:T(8,128)S(1)} %bitcast.96), channel_id=1, replica_groups=mesh['gz'=2,'gx_0'=4,'gx_1'=4,'gy'=8] {'gz'}, dimensions={0} | all-to-all | bytes 786432 | tf_op jit(solution)/shard_map/all_to_all | solution.py:38
  6.6 8.6 %all-to-all-start.1 = ((f32[2,8,8,3,256]{4,2,3,0,1:T(8,128)}), f32[2,8,8,3,256]{4,2,3,0,1:T(8,128)S(1)}, u32[]{:S(2)}, u32[]{:S(2)}) async-start(f32[2,8,8,3,256]{4,2,3,0,1:T(8,128)} %copy.146), calls=%async_computation.1 | async-start | bytes 786432 | tf_op jit(solution)/shard_map/all_to_all | solution.py:38
  23.7 4.9 %all-to-all-done.1 = f32[2,8,8,3,256]{4,2,3,0,1:T(8,128)S(1)} async-done(((f32[2,8,8,3,256]{4,2,3,0,1:T(8,128)}), f32[2,8,8,3,256]{4,2,3,0,1:T(8,128)S(1)}, u32[]{:S(2)}, u32[]{:S(2)}) %all-to-all-start.1) | async-done | bytes 393248 | tf_op jit(solution)/shard_map/all_to_all | solution.py:38
  31.7 73.3 %while.18 = (s32[]{:T(128)}, f32[128,3,256]{2,1,0:T(4,128)S(1)}, f32[128,256]{1,0:T(8,128)}, f32[128,256]{1,0:T(8,128)}, f32[2,8,8,3,256]{4,3,2,1,0:T(4,128)S(1)...) while((s32[]{:T(128)}, f32[128,3,256]{2,1,0:T(4,128)S(1)}, ...), condition=%wide.region_10.0_spmd.clone, body=%wide.region_5.10_spmd.clone.sunk | while | flops 20129812 | bytes 12042598 | solution.py:142
  33.5 3.0 %fusion.145 = (f32[128,256]{1,0:T(8,128)S(1)}, f32[128,256]{1,0:T(8,128)S(1)}, f32[128,16,256]{2,1,0:T(8,128)S(1)}) fusion(f32[128,16,256]{2,1,0:T(8,128)S(1)} %fusion.142, f32[128,16]{1,0:T(8,128)S(1)} %fusion.143, f32[128,16]{1,0:T(8,128)S(1)} %get-tuple-element.422, f32[128,16]{1,0:T(8,128)S(1)} %get-tuple-element.423), kind=kLoop, calls=%fused_computation.24.clone.1 | loop fusion | flops 10944512 | bytes 4481024 | tf_op jit(solution)/shard_map/while/body/eval_jaxpr/reduce_sum | solution.py:110
  41.8 3.0 %fusion.145 = (f32[128,256]{1,0:T(8,128)S(1)}, f32[128,256]{1,0:T(8,128)S(1)}, f32[128,16,256]{2,1,0:T(8,128)S(1)}) fusion(f32[128,16,256]{2,1,0:T(8,128)S(1)} %fusion.142, f32[128,16]{1,0:T(8,128)S(1)} %fusion.143, f32[128,16]{1,0:T(8,128)S(1)} %get-tuple-element.422, f32[128,16]{1,0:T(8,128)S(1)} %get-tuple-element.423), kind=kLoop, calls=%fused_computation.24.clone.1 | loop fusion | flops 10944512 | bytes 4481024 | tf_op jit(solution)/shard_map/while/body/eval_jaxpr/reduce_sum | solution.py:110
  51.1 3.0 %fusion.145 = (f32[128,256]{1,0:T(8,128)S(1)}, f32[128,256]{1,0:T(8,128)S(1)}, f32[128,16,256]{2,1,0:T(8,128)S(1)}) fusion(f32[128,16,256]{2,1,0:T(8,128)S(1)} %fusion.142, f32[128,16]{1,0:T(8,128)S(1)} %fusion.143, f32[128,16]{1,0:T(8,128)S(1)} %get-tuple-element.422, f32[128,16]{1,0:T(8,128)S(1)} %get-tuple-element.423), kind=kLoop, calls=%fused_computation.24.clone.1 | loop fusion | flops 10944512 | bytes 4481024 | tf_op jit(solution)/shard_map/while/body/eval_jaxpr/reduce_sum | solution.py:110
  60.4 3.0 %fusion.145 = (f32[128,256]{1,0:T(8,128)S(1)}, f32[128,256]{1,0:T(8,128)S(1)}, f32[128,16,256]{2,1,0:T(8,128)S(1)}) fusion(f32[128,16,256]{2,1,0:T(8,128)S(1)} %fusion.142, f32[128,16]{1,0:T(8,128)S(1)} %fusion.143, f32[128,16]{1,0:T(8,128)S(1)} %get-tuple-element.422, f32[128,16]{1,0:T(8,128)S(1)} %get-tuple-element.423), kind=kLoop, calls=%fused_computation.24.clone.1 | loop fusion | flops 10944512 | bytes 4481024 | tf_op jit(solution)/shard_map/while/body/eval_jaxpr/reduce_sum | solution.py:110
  69.7 3.0 %fusion.145 = (f32[128,256]{1,0:T(8,128)S(1)}, f32[128,256]{1,0:T(8,128)S(1)}, f32[128,16,256]{2,1,0:T(8,128)S(1)}) fusion(f32[128,16,256]{2,1,0:T(8,128)S(1)} %fusion.142, f32[128,16]{1,0:T(8,128)S(1)} %fusion.143, f32[128,16]{1,0:T(8,128)S(1)} %get-tuple-element.422, f32[128,16]{1,0:T(8,128)S(1)} %get-tuple-element.423), kind=kLoop, calls=%fused_computation.24.clone.1 | loop fusion | flops 10944512 | bytes 4481024 | tf_op jit(solution)/shard_map/while/body/eval_jaxpr/reduce_sum | solution.py:110
  78.9 3.0 %fusion.145 = (f32[128,256]{1,0:T(8,128)S(1)}, f32[128,256]{1,0:T(8,128)S(1)}, f32[128,16,256]{2,1,0:T(8,128)S(1)}) fusion(f32[128,16,256]{2,1,0:T(8,128)S(1)} %fusion.142, f32[128,16]{1,0:T(8,128)S(1)} %fusion.143, f32[128,16]{1,0:T(8,128)S(1)} %get-tuple-element.422, f32[128,16]{1,0:T(8,128)S(1)} %get-tuple-element.423), kind=kLoop, calls=%fused_computation.24.clone.1 | loop fusion | flops 10944512 | bytes 4481024 | tf_op jit(solution)/shard_map/while/body/eval_jaxpr/reduce_sum | solution.py:110
  88.2 3.0 %fusion.145 = (f32[128,256]{1,0:T(8,128)S(1)}, f32[128,256]{1,0:T(8,128)S(1)}, f32[128,16,256]{2,1,0:T(8,128)S(1)}) fusion(f32[128,16,256]{2,1,0:T(8,128)S(1)} %fusion.142, f32[128,16]{1,0:T(8,128)S(1)} %fusion.143, f32[128,16]{1,0:T(8,128)S(1)} %get-tuple-element.422, f32[128,16]{1,0:T(8,128)S(1)} %get-tuple-element.423), kind=kLoop, calls=%fused_computation.24.clone.1 | loop fusion | flops 10944512 | bytes 4481024 | tf_op jit(solution)/shard_map/while/body/eval_jaxpr/reduce_sum | solution.py:110
  97.5 3.0 %fusion.145 = (f32[128,256]{1,0:T(8,128)S(1)}, f32[128,256]{1,0:T(8,128)S(1)}, f32[128,16,256]{2,1,0:T(8,128)S(1)}) fusion(f32[128,16,256]{2,1,0:T(8,128)S(1)} %fusion.142, f32[128,16]{1,0:T(8,128)S(1)} %fusion.143, f32[128,16]{1,0:T(8,128)S(1)} %get-tuple-element.422, f32[128,16]{1,0:T(8,128)S(1)} %get-tuple-element.423), kind=kLoop, calls=%fused_computation.24.clone.1 | loop fusion | flops 10944512 | bytes 4481024 | tf_op jit(solution)/shard_map/while/body/eval_jaxpr/reduce_sum | solution.py:110
  105.0 5.0 %fusion.31 = (f32[128,16,256]{2,1,0:T(8,128)S(1)}, f32[128,16,256]{2,1,0:T(8,128)S(1)}, f32[128,16,256]{2,1,0:T(8,128)S(1)}) fusion(f32[16,3]{0,1:T(4,128)S(1)} %bitcast.116, f32[128,3,256]{2,1,0:T(4,128)} %copy.148, f32[16,3]{0,1:T(4,128)S(1)} %bitcast.118, f32[16,3]{0,1:T(4,128)S(1)} %bitcast.104), kind=kLoop, calls=%fused_computation.65 | loop fusion | flops 12582912 | bytes 6685248 | tf_op jit(solution)/shard_map/reduce_sum | solution.py:75
  110.0 3.1 %multiply_divide_fusion.17 = (f32[128,16,256]{2,1,0:T(8,128)S(1)}, f32[128,16,256]{2,1,0:T(8,128)S(1)}, f32[128,16,256]{2,1,0:T(8,128)S(1)}) fusion(f32[128,16,256]{2,1,0:T(8,128)S(1)} %get-tuple-element.252, f32[16]{0:T(128)S(1)} %get-tuple-element.368, f32[16]{0:T(128)S(1)} %copy-done.40, f32[128,16,256]{2,1,0:T(8,128)S(1)} %get-tuple-element.250, ...), kind=kLoop, calls=%fused_computation.166 | loop fusion | flops 7864320 | bytes 12583040 | tf_op jit(solution)/shard_map/div | solution.py:80
  113.2 13.9 %fusion.32 = (f32[128,3,256]{2,1,0:T(4,128)S(1)}, f32[128,16,256]{2,1,0:T(8,128)S(1)}, f32[128,16,256]{2,1,0:T(8,128)S(1)}, f32[128,16,256]{2,1,0:T(8,128)S(1)},...) fusion(f32[128,16,256]{2,1,0:T(8,128)S(1)} %get-tuple-element.3, ...), kind=kLoop, calls=%fused_computation.66 | loop fusion | flops 34832384 | bytes 18351616 | tf_op jit(solution)/shard_map/reduce_sum | solution.py:80
  127.2 36.6 %fusion.104 = (f32[128,256]{1,0:T(8,128)}, f32[128,256]{1,0:T(8,128)}, f32[128,256]{1,0:T(8,128)}, f32[128,256]{1,0:T(8,128)}, f32[128,256]{1,0:T(8,128)S(1)}, /...) fusion(f32[128,16,256]{2,1,0:T(8,128)S(1)} %get-tuple-element.2, ...), kind=kLoop, calls=%fused_computation.186 | loop fusion | flops 79953920 | bytes 30409024 | tf_op jit(solution)/shard_map/reduce_sum | solution.py:81
  163.8 12.2 %fusion.30 = (f32[128,3,256]{2,1,0:T(4,128)S(1)}, f32[128,3,256]{2,1,0:T(4,128)S(1)}, f32[128,3,256]{2,1,0:T(4,128)S(1)}, f32[128,3,256]{2,1,0:T(4,128)S(1)}, f32[128,3,256]{2,1,0:T(4,128)S(1)}) fusion(f32[128,16,256]{2,1,0:T(8,128)S(1)} %get-tuple-element.330, f32[16,3]{0,1:T(4,128)S(1)} %bitcast.107, f32[128,3,256]{2,1,0:T(4,128)S(1)} %copy-done, ...), kind=kLoop, calls=%fused_computation.64 | loop fusion | flops 23101440 | bytes 12846016 | tf_op jit(solution)/shard_map/reduce_sum | solution.py:80
  176.2 10.3 %multiply_reduce_fusion.7 = (f32[128,256]{1,0:T(8,128)S(1)}, f32[128,256]{1,0:T(8,128)S(1)}, f32[128,256]{1,0:T(8,128)S(1)}, f32[128,256]{1,0:T(8,128)S(1)}, f32...) fusion(f32[128,3,256]{2,1,0:T(4,128)S(1)} %get-tuple-element.25, ...), kind=kLoop, calls=%fused_computation.197 | loop fusion | flops 4390912 | bytes 7471104 | tf_op jit(solution)/shard_map/reduce_sum | solution.py:125
  187.9 25.7 %all_gather.3 = f32[16,4096]{1,0:T(8,128)S(1)} all-gather(f32[16,256]{1,0:T(8,128)S(1)} %concatenate.12), channel_id=1, replica_groups=mesh['gz'=2,'gx_0'=4,'gx_1'=4,'gy'=8] {'gz','gy'}, dimensions={1}, use_global_device_ids=true | all-gather | bytes 278528 | tf_op jit(solution)/shard_map/all_gather | solution.py:50
  213.7 7.5 %all-to-all-start.2 = ((f32[128,3,256]{2,1,0:T(4,128)}), f32[128,3,256]{2,1,0:T(4,128)S(1)}, u32[]{:S(2)}, u32[]{:S(2)}) async-start(f32[128,3,256]{2,1,0:T(4,128)} %get-tuple-element.341), calls=%async_computation.2 | async-start | bytes 1048576 | tf_op jit(solution)/shard_map/all_to_all | solution.py:197
  221.5 10.7 %all-reduce.1 = (f32[5]{0:T(128)S(1)}, f32[5]{0:T(128)S(1)}) all-reduce(f32[5]{0:T(128)S(1)} %get-tuple-element.272, f32[5]{0:T(128)S(1)} %get-tuple-element.271), channel_id=1, replica_groups=mesh['gz'=2,'gx_0'=4,'gx_1'=4,'gy'=8] {'gx_0'}, use_global_device_ids=true, to_apply=%region_89.0 | all-reduce | flops 10 | bytes 80 | tf_op jit(solution)/shard_map/psum | solution.py:55
  232.2 10.5 %all-reduce = (f32[5]{0:T(128)S(1)}, f32[5]{0:T(128)S(1)}) all-reduce(f32[5]{0:T(128)S(1)} %get-tuple-element.318, f32[5]{0:T(128)S(1)} %get-tuple-element.319), channel_id=1, replica_groups=mesh['gz'=2,'gx_0'=4,'gx_1'=4,'gy'=8] {'gx_1'}, use_global_device_ids=true, to_apply=%region_90.0 | all-reduce | flops 10 | bytes 80 | tf_op jit(solution)/shard_map/psum | solution.py:55
  248.1 3.7 %all-to-all-start.3 = ((f32[25,64,128]{2,0,1:T(8,128)}), f32[25,64,128]{2,0,1:T(8,128)S(1)}, u32[]{:S(2)}, u32[]{:S(2)}) async-start(f32[25,64,128]{2,0,1:T(8,128)} %pad_maximum_fusion), calls=%async_computation.3 | async-start | bytes 2097152 | tf_op jit(solution)/shard_map/all_to_all | solution.py:66
  252.7 13.7 %all-to-all-done.3 = f32[25,64,128]{2,0,1:T(8,128)S(1)} async-done(((f32[25,64,128]{2,0,1:T(8,128)}), f32[25,64,128]{2,0,1:T(8,128)S(1)}, u32[]{:S(2)}, u32[]{:S(2)}) %all-to-all-start.3) | async-done | bytes 819232 | tf_op jit(solution)/shard_map/all_to_all | solution.py:66
  (248 shorter events, 70.1 us)
Async XLA Ops:
  0.7 14.6 %copy-start.39 = (s32[512]{0:T(512)S(1)}, s32[512]{0:T(512)}, u32[]{:S(2)}) copy-start(s32[512]{0:T(512)} %param.21) | copy-start | bytes 6148
  0.7 16.0 %copy-start.37 = (f32[16]{0:T(128)S(1)}, f32[16]{0:T(128)}, u32[]{:S(2)}) copy-start(f32[16]{0:T(128)} %param.16) | copy-start | bytes 196
  0.7 22.4 %copy-start.50 = (f32[16]{0:T(128)S(1)}, f32[16]{0:T(128)}, u32[]{:S(2)}) copy-start(f32[16]{0:T(128)} %param.17) | copy-start | bytes 196
  0.7 23.0 %copy-start.45 = (s32[32]{0:T(128)S(1)}, s32[32]{0:T(128)}, u32[]{:S(2)}) copy-start(s32[32]{0:T(128)} %param.20) | copy-start | bytes 388
  6.6 22.1 %all-to-all-start.1 = ((f32[2,8,8,3,256]{4,2,3,0,1:T(8,128)}), f32[2,8,8,3,256]{4,2,3,0,1:T(8,128)S(1)}, u32[]{:S(2)}, u32[]{:S(2)}) async-start(f32[2,8,8,3,256]{4,2,3,0,1:T(8,128)} %copy.146), calls=%async_computation.1 | async-start | bytes 786432 | tf_op jit(solution)/shard_map/all_to_all | solution.py:38
  18.1 95.1 %copy-start.26 = (f32[1,16,3]{1,2,0:T(4,128)}, f32[1,16,3]{1,2,0:T(4,128)S(1)}, u32[]{:S(2)}) copy-start(f32[1,16,3]{1,2,0:T(4,128)S(1)} %copy.182) | copy-start | bytes 580
  18.1 95.0 %copy-start.28 = (f32[1,16,3]{1,2,0:T(4,128)}, f32[1,16,3]{1,2,0:T(4,128)S(1)}, u32[]{:S(2)}) copy-start(f32[1,16,3]{1,2,0:T(4,128)S(1)} %copy.183) | copy-start | bytes 580
  18.1 95.0 %copy-start.30 = (f32[1,16,3]{1,2,0:T(4,128)}, f32[1,16,3]{1,2,0:T(4,128)S(1)}, u32[]{:S(2)}) copy-start(f32[1,16,3]{1,2,0:T(4,128)S(1)} %copy.184) | copy-start | bytes 580
  18.1 95.0 %copy-start.32 = (f32[1,16,3]{1,2,0:T(4,128)}, f32[1,16,3]{1,2,0:T(4,128)S(1)}, u32[]{:S(2)}) copy-start(f32[1,16,3]{1,2,0:T(4,128)S(1)} %copy.185) | copy-start | bytes 580
  18.2 95.0 %copy-start.34 = (f32[1,16,3]{1,2,0:T(4,128)}, f32[1,16,3]{1,2,0:T(4,128)S(1)}, u32[]{:S(2)}) copy-start(f32[1,16,3]{1,2,0:T(4,128)S(1)} %copy.186) | copy-start | bytes 580
  23.7 86.3 %copy-start.43 = (f32[16]{0:T(128)}, f32[16]{0:T(128)S(1)}, u32[]{:S(2)}) copy-start(f32[16]{0:T(128)S(1)} %get-tuple-element.368) | copy-start | bytes 196
  127.1 36.6 %copy-start.27 = (f32[1,16,3]{1,2,0:T(4,128)S(1)}, f32[1,16,3]{1,2,0:T(4,128)}, u32[]{:S(2)}) copy-start(f32[1,16,3]{1,2,0:T(4,128)} %copy-done.26) | copy-start | bytes 580
  127.1 36.6 %copy-start.29 = (f32[1,16,3]{1,2,0:T(4,128)S(1)}, f32[1,16,3]{1,2,0:T(4,128)}, u32[]{:S(2)}) copy-start(f32[1,16,3]{1,2,0:T(4,128)} %copy-done.28) | copy-start | bytes 580
  127.1 36.6 %copy-start.31 = (f32[1,16,3]{1,2,0:T(4,128)S(1)}, f32[1,16,3]{1,2,0:T(4,128)}, u32[]{:S(2)}) copy-start(f32[1,16,3]{1,2,0:T(4,128)} %copy-done.30) | copy-start | bytes 580
  127.2 36.6 %copy-start.33 = (f32[1,16,3]{1,2,0:T(4,128)S(1)}, f32[1,16,3]{1,2,0:T(4,128)}, u32[]{:S(2)}) copy-start(f32[1,16,3]{1,2,0:T(4,128)} %copy-done.32) | copy-start | bytes 580
  127.2 36.6 %copy-start.35 = (f32[1,16,3]{1,2,0:T(4,128)S(1)}, f32[1,16,3]{1,2,0:T(4,128)}, u32[]{:S(2)}) copy-start(f32[1,16,3]{1,2,0:T(4,128)} %copy-done.34) | copy-start | bytes 580
  187.6 33.6 %copy-start.25 = (f32[4096]{0:T(1024)S(1)}, f32[4096]{0:T(1024)}, u32[]{:S(2)}) copy-start(f32[4096]{0:T(1024)} %param.19) | copy-start | bytes 49156
  187.6 33.6 %copy-start.47 = (f32[5]{0:T(128)S(1)}, f32[5]{0:T(128)}, u32[]{:S(2)}) copy-start(f32[5]{0:T(128)} %stack.87) | copy-start | bytes 64
  187.6 56.4 %copy-start.46 = (s32[32]{0:T(128)S(1)}, s32[32]{0:T(128)}, u32[]{:S(2)}) copy-start(s32[32]{0:T(128)} %param.20) | copy-start | bytes 388
  187.6 57.2 %copy-start.41 = (f32[64]{0:T(128)S(1)}, f32[64]{0:T(128)}, u32[]{:S(2)}) copy-start(f32[64]{0:T(128)} %convert_element_type.58) | copy-start | bytes 772
  187.6 57.2 %copy-start.42 = (pred[64]{0:T(512)(128)(4,1)S(1)}, pred[64]{0:T(512)(128)(4,1)}, u32[]{:S(2)}) copy-start(pred[64]{0:T(512)(128)(4,1)} %compare_and_fusion) | copy-start | bytes 196
  187.8 57.3 %copy-start.24 = (f32[8,3,4096]{2,0,1:T(8,128)S(1)}, f32[8,3,4096]{2,0,1:T(8,128)}, u32[]{:S(2)}) copy-start(f32[8,3,4096]{2,0,1:T(8,128)} %param.13) | copy-start | bytes 1179652
  213.7 31.3 %all-to-all-start.2 = ((f32[128,3,256]{2,1,0:T(4,128)}), f32[128,3,256]{2,1,0:T(4,128)S(1)}, u32[]{:S(2)}, u32[]{:S(2)}) async-start(f32[128,3,256]{2,1,0:T(4,128)} %get-tuple-element.341), calls=%async_computation.2 | async-start | bytes 1048576 | tf_op jit(solution)/shard_map/all_to_all | solution.py:197
  248.1 18.3 %all-to-all-start.3 = ((f32[25,64,128]{2,0,1:T(8,128)}), f32[25,64,128]{2,0,1:T(8,128)S(1)}, u32[]{:S(2)}, u32[]{:S(2)}) async-start(f32[25,64,128]{2,0,1:T(8,128)} %pad_maximum_fusion), calls=%async_computation.3 | async-start | bytes 2097152 | tf_op jit(solution)/shard_map/all_to_all | solution.py:66
  (33 other events, 293.9 us)
where the time goes:
time: 271 us; the launch traced here: 270 us
  other arithmetic  156 us (58%)
  blocking collectives  51 us (19%)
  starting transfers between devices  19.8 us (7%)
  local copies, waits for them, and re-layouts  19.3 us (7%)
  waiting for transfers between devices  18.7 us (7%)
  between operations  4.67 us (2%)
    reduce_sum x1, other arithmetic, orbital_terms(): jnp.sum(orbital_part * (decay * decay * square_dist / (distance * distanc...  36.6 us
    reduce_sum x2, other arithmetic, orbital_terms(): jnp.sum((-decay * orbital_part / distance)[:, :, None, :] * offsets, axis=1)  26 us
    all_gather x1, blocking collectives, sent_together(): out = lax.all_gather(both, axis, axis=dim, tiled=True)  25.7 us
    reduce_sum x8, other arithmetic, pair_terms(): coulomb = 0.5 * jnp.sum(keeping / distance, axis=1)  24.2 us
    psum x2, blocking collectives, over_axes(): return functools.reduce(lax.psum, axes, x)  21.2 us
    add x16, other arithmetic, one_group(): return (running[0] + gradient, running[1] + laplacian, running[2] + coulomb)  19 us
    reduce_sum x8, other arithmetic, pair_terms(): gradient = jnp.sum((slope / distance)[:, :, None, :] * offsets, axis=1)  15.7 us
    all_to_all x1, waiting for transfers between devices, side_by_side(): lax.all_to_all(both, axis, split_axis=split_dim, concat_axis=concat_dim,...  13.7 us
  transfers between devices with their start and end apart: 3, of which 2 were waited for; matrix products, arithmetic and copies ran while one was open for 3% of the time, Pallas kernels for 0%

commit v1 on v0

v1 whole, which is shorter than its diff:
```python
import functools
import math

import jax
import jax.numpy as jnp
from jax import lax
from jax.experimental import pallas as pl
from jax.experimental.pallas import tpu as pltpu
from jax.sharding import Mesh
from jax.sharding import PartitionSpec as P

NE = 128
NA = 16
NG = 8
BLK = 128
EB = 16
CAP = 4
SLOT_ROWS = 24
PEER_ROWS = CAP * SLOT_ROWS + 8
GX = ("gx_0", "gx_1")
GZY = ("gz", "gy")

SOFT = 0.04
TIME_STEP = 0.01
STEP_ROOT = 0.1
LN2 = math.log(2.0)
LOG2E = 1.0 / LN2

K_CONST, K_X, K_Y, K_Z, K_R2, K_AMP, K_PHI, K_CX, K_CY, K_CZ, K_SOFT, K_POT = range(12)


def roll8(x, shift):
    shift %= 8
    return x if shift == 0 else pltpu.roll(x, shift, axis=0)


def pair_part(pos, rot, back, grad):
    zero = jnp.zeros((8, BLK), jnp.float32)

    def prepare(p, _):
        for h in range(2):
            for c in range(3):
                x = pos[p, h, c * 8 : c * 8 + 8, :]
                grad[p, h, c * 8 : c * 8 + 8, :] = zero
                for s in range(8):
                    rot[p, h, s, c * 8 : c * 8 + 8, :] = roll8(x, -s)
                    back[p, h, s, c * 8 : c * 8 + 8, :] = zero
        return 0

    lax.fori_loop(0, EB, prepare, 0)

    def terms(xi, xj, sums, half):
        d = [xi[c] - xj[c] for c in range(3)]
        square = (d[0] * d[0] + d[1] * d[1]) + (d[2] * d[2] + SOFT)
        inv = lax.rsqrt(square)
        p = 1.0 / (square * inv + 1.0)
        p2 = p * p
        slope = (0.5 * p2) * inv
        p3 = p2 * p
        first = p + p2 + p3
        second = (inv * inv) * (p3 + slope)
        if half:
            first, second = 0.5 * first, 0.5 * second
        return [slope * d[c] for c in range(3)], (sums[0] + first, sums[1] + second)

    def load3(ref, *at):
        return [ref[(*at, slice(c * 8, c * 8 + 8), slice(None))] for c in range(3)]

    def store3(ref, values, *at):
        for c in range(3):
            ref[(*at, slice(c * 8, c * 8 + 8), slice(None))] = values[c]

    def block_pair(i, j, h, xi, gi, sums):
        for s in range(8):
            f, sums = terms(xi, load3(rot, j, h, s), sums, False)
            gi = [gi[c] + f[c] for c in range(3)]
            b = load3(back, j, h, s)
            store3(back, [b[c] + f[c] for c in range(3)], j, h, s)
        return gi, sums

    def inside(t, sums):
        out = []
        for h in range(2):
            acc = sums[h]
            for i in (2 * t, 2 * t + 1):
                xi, gi = load3(pos, i, h), load3(grad, i, h)
                for s in range(1, 5):
                    f, acc = terms(xi, load3(rot, i, h, s), acc, s == 4)
                    gi = [gi[c] + f[c] for c in range(3)]
                    if s < 4:
                        b = load3(back, i, h, s)
                        store3(back, [b[c] + f[c] for c in range(3)], i, h, s)
                store3(grad, gi, i, h)
            i, j = 2 * t, 2 * t + 1
            gi, acc = block_pair(i, j, h, load3(pos, i, h), load3(grad, i, h), acc)
            store3(grad, gi, i, h)
            out.append(acc)
        return tuple(out)

    def across(u, t, sums):
        out = []
        for h in range(2):
            acc = sums[h]
            for i in (2 * u, 2 * u + 1):
                xi, gi = load3(pos, i, h), load3(grad, i, h)
                for j in (2 * t, 2 * t + 1):
                    gi, acc = block_pair(i, j, h, xi, gi, acc)
                store3(grad, gi, i, h)
            out.append(acc)
        return tuple(out)

    def outer(t, sums):
        sums = inside(t, sums)
        return lax.fori_loop(0, t, lambda u, carry: across(u, t, carry), sums)

    start = ((zero, zero), (zero, zero))
    sums = lax.fori_loop(0, EB // 2, outer, start)

    def finish(p, squares):
        out = []
        for h in range(2):
            acc = squares[h]
            for c in range(3):
                g = grad[p, h, c * 8 : c * 8 + 8, :]
                for s in range(8):
                    g = g - roll8(back[p, h, s, c * 8 : c * 8 + 8, :], s)
                grad[p, h, c * 8 : c * 8 + 8, :] = g
                acc = acc + g * g
            out.append(acc)
        return tuple(out)

    squares = lax.fori_loop(0, EB, finish, (zero, zero))
    totals = []
    for h in range(2):
        t = sums[h][0] - SOFT * sums[h][1] - 0.5 * squares[h]
        totals.append(jnp.broadcast_to(jnp.sum(t, axis=0, keepdims=True), (8, BLK)))
    return totals


def walker_kernel(pos, table, nuclear, live, out, rot, back, grad):
    totals = pair_part(pos, rot, back, grad)
    zero = jnp.zeros((8, BLK), jnp.float32)

    def electrons(p, carry):
        energy, logs, pots = carry
        for e in range(8):
            xs, acc = [], []
            for h in range(2):
                x = [
                    jnp.broadcast_to(pos[p, h, c * 8 + e : c * 8 + e + 1, :], (8, BLK))
                    for c in range(3)
                ]
                xs.append((x[0], x[1], x[2], x[0] * x[0] + x[1] * x[1] + x[2] * x[2]))
                acc.append([zero] * 7)
            pots = list(pots)
            for a in range(NA):
                for h in range(2):
                    x, y, z, r2 = xs[h]
                    square = (r2 * table[K_R2, a] + table[K_CONST, a]) + (
                        (x * table[K_X, a] + y * table[K_Y, a]) + z * table[K_Z, a]
                    )
                    inv = lax.rsqrt(square)
                    amp = jnp.exp2(table[K_AMP, a] - square * inv)
                    u = amp * inv
                    s = acc[h]
                    acc[h] = [
                        s[0] + amp * table[K_PHI, a],
                        s[1] + amp,
                        s[2] + u,
                        s[3] + u * table[K_CX, a],
                        s[4] + u * table[K_CY, a],
                        s[5] + u * table[K_CZ, a],
                        s[6] + (u * inv) * ((inv + LN2) * table[K_SOFT, a]),
                    ]
                    pots[h] = pots[h] + inv * table[K_POT, a]
            new_energy, new_logs = [], []
            for h in range(2):
                phi, amps, us, ux, uy, uz, soft = acc[h]
                x, y, z, _ = xs[h]
                ratio = 1.0 / phi
                g = [(ux - x * us) * ratio, (uy - y * us) * ratio, (uz - z * us) * ratio]
                j = [
                    jnp.broadcast_to(grad[p, h, c * 8 + e : c * 8 + e + 1, :], (8, BLK))
                    for c in range(3)
                ]
                lap = (LN2 * amps - 2.0 * us - soft) * ratio
                dot = g[0] * j[0] + g[1] * j[1] + g[2] * j[2]
                new_energy.append(energy[h] - (0.5 * lap + dot))
                new_logs.append(logs[h] + jnp.log2(phi))
                for c in range(3):
                    out[p, h, c * 8 + e : c * 8 + e + 1, :] = (g[c] + j[c])[0:1, :]
            energy, logs = new_energy, new_logs
        return tuple(energy), tuple(logs), tuple(pots)

    energy, logs, pots = lax.fori_loop(
        0, EB, electrons, ((zero, zero), (zero, zero), (zero, zero))
    )
    row = lax.broadcasted_iota(jnp.int32, (8, BLK), 0)
    lane = lax.broadcasted_iota(jnp.int32, (8, BLK), 1)
    numerator = jnp.zeros((8, 1), jnp.float32)
    denominator = jnp.zeros((8, 1), jnp.float32)
    local = []
    for h in range(2):
        e = (energy[h] - pots[h] + totals[h] + nuclear[...]) * (1.0 / NE)
        weight = jnp.exp2(2.0 * (logs[h] - jnp.broadcast_to(logs[h][0:1, :], (8, BLK))))
        weight = weight * jnp.broadcast_to(live[h : h + 1, :], (8, BLK))
        numerator = numerator + jnp.sum(weight * e, axis=1, keepdims=True)
        denominator = denominator + jnp.sum(weight, axis=1, keepdims=True)
        local.append(e)
    placed = jnp.where(lane == row, numerator, 0.0) + jnp.where(lane == row + 8, denominator, 0.0)
    placed = jnp.broadcast_to(jnp.sum(placed, axis=0, keepdims=True), (8, BLK))
    for h in range(2):
        first = jnp.broadcast_to(local[h][0:1, :], (8, BLK))
        for half in range(2):
            e = local[h] if half == 0 else roll8(local[h], 4)
            tile = jnp.where(row < 4, e, jnp.where(row == 4, first, placed))
            for q in range(8):
                out[half * 8 + q, h, 24:32, :] = tile


def walker_step(whole, table, nuclear, live):
    vmem = pl.BlockSpec(memory_space=pltpu.VMEM)
    return pl.pallas_call(
        walker_kernel,
        out_shape=jax.ShapeDtypeStruct((EB, 2, 32, BLK), jnp.float32),
        in_specs=[vmem] * 4,
        out_specs=vmem,
        scratch_shapes=[
            pltpu.VMEM((EB, 2, 8, 24, BLK), jnp.float32),
            pltpu.VMEM((EB, 2, 8, 24, BLK), jnp.float32),
            pltpu.VMEM((EB, 2, 24, BLK), jnp.float32),
        ],
        name="walker_step",
    )(whole, table, nuclear, live)


def pack_kernel(picked, returned, base, live, send, energy):
    sums = returned[0, 29:30, :]
    for p in range(1, EB):
        sums = sums + returned[2 * p, 29:30, :]
    for b in range(2 * EB):
        energy[:, b * BLK : (b + 1) * BLK] = returned[b, 24:28, :]

    def one_peer(peer, _):
        for k in range(CAP):
            b = picked[peer * CAP + k]
            for c in range(3):
                send[peer, k * 24 + c * 8 : k * 24 + c * 8 + 8, :] = (
                    base[b, c * 8 : c * 8 + 8, :] + TIME_STEP * returned[b, c * 8 : c * 8 + 8, :]
                )
            alive = live[pl.ds(b, 1), :]
            level = returned[b, 28:29, :] - jnp.log(alive)
            send[peer, 96 + k : 97 + k, :] = jnp.where(alive > 0.0, level, 3.0e38)
        send[peer, 100:101, :] = sums
        send[peer, 101:104, :] = jnp.zeros((3, BLK), jnp.float32)
        return 0

    lax.fori_loop(0, send.shape[0], one_peer, 0)


def pack_step(picked, returned, base, live, peers):
    vmem = pl.BlockSpec(memory_space=pltpu.VMEM)
    return pl.pallas_call(
        pack_kernel,
        out_shape=(
            jax.ShapeDtypeStruct((peers, PEER_ROWS, BLK), jnp.float32),
            jax.ShapeDtypeStruct((NG // 2, 2 * EB * BLK), jnp.float32),
        ),
        in_specs=[pl.BlockSpec(memory_space=pltpu.SMEM)] + [vmem] * 3,
        out_specs=(vmem, vmem),
        name="pack_step",
    )(picked, returned, base, live)


def place_kernel(slots, half, received, moved, weights, estimate):
    sums = received[0, 100:101, :]
    for peer in range(1, received.shape[0]):
        sums = sums + received[peer, 100:101, :]
    sums = jnp.broadcast_to(sums, (8, BLK))
    ratio = sums / pltpu.roll(sums, BLK - 8, axis=1)
    lane = lax.broadcasted_iota(jnp.int32, (8, BLK), 1)
    reference = jnp.sum(jnp.where(lane == 0, ratio, 0.0), axis=1, keepdims=True)[0:1, :]
    own = jnp.where(half[0] == 0, ratio, pltpu.roll(ratio, BLK - 4, axis=1))
    estimate[...] = own[0:1, 0:4]
    for d in range(weights.shape[0]):
        peer, k = slots[d] // CAP, slots[d] % CAP
        for e in range(8):
            rows = [received[peer, pl.ds(k * 24 + c * 8 + e, 1), :] for c in range(3)]
            for c in range(3):
                moved[e, c : c + 1, d * BLK : (d + 1) * BLK] = rows[c]
        level = received[peer, pl.ds(96 + k, 1), :]
        weights[d : d + 1, :] = jnp.exp(-(level - reference))


def place_step(slots, half, received):
    vmem = pl.BlockSpec(memory_space=pltpu.VMEM)
    smem = pl.BlockSpec(memory_space=pltpu.SMEM)
    blocks = slots.shape[0]
    return pl.pallas_call(
        place_kernel,
        out_shape=(
            jax.ShapeDtypeStruct((8, 3, blocks * BLK), jnp.float32),
            jax.ShapeDtypeStruct((blocks, BLK), jnp.float32),
            jax.ShapeDtypeStruct((1, NG // 2), jnp.float32),
        ),
        in_specs=[smem, smem, vmem],
        out_specs=(vmem, vmem, vmem),
        name="place_step",
    )(slots, half, received)


def nuclear_repulsion(centers, charges):
    offsets = centers[:, :, None, :] - centers[:, None, :, :]
    identity = jnp.eye(NA, dtype=jnp.float32)
    distance = jnp.sqrt(jnp.sum(offsets * offsets, axis=3) + identity)
    product = charges[:, None] * charges[None, :] * (1.0 - identity)
    return 0.5 * jnp.sum(product / distance, axis=(1, 2))


def nucleus_table(centers, charges, decay, coefficients):
    c = jnp.moveaxis(centers, 1, 0)
    k = (decay * LOG2E)[:, None]
    k2 = k * k
    scale = decay[:, None] * k
    ones = jnp.ones((NA, NG), jnp.float32)
    rows = [
        k2 * (jnp.sum(c * c, axis=2) + SOFT),
        -2.0 * k2 * c[:, :, 0],
        -2.0 * k2 * c[:, :, 1],
        -2.0 * k2 * c[:, :, 2],
        k2 * ones,
        jnp.log2(coefficients[:, None] * scale) * ones,
        ones / scale,
        c[:, :, 0],
        c[:, :, 1],
        c[:, :, 2],
        SOFT * k2 * ones,
        (charges[:, None] * k) * ones,
    ]
    return jnp.broadcast_to(jnp.stack(rows)[..., None], (len(rows), NA, NG, BLK))


def by_blocks(x):
    e, c, w = x.shape
    return x.reshape(e, c, w // BLK, BLK).transpose(2, 1, 0, 3).reshape(w // BLK, c * e, BLK)


def local(
    positions,
    diffusion_noise,
    base_nuclei,
    displacements,
    charges,
    orbital_decay,
    coefficients,
    weights,
    counts,
    branch_source,
):
    blocks_here = counts.shape[0]
    peers = lax.axis_size(GX)
    replica = lax.axis_index("gz")
    member = lax.axis_index(GZY)
    device = lax.axis_index(GX)

    sent = by_blocks(positions)
    whole = lax.all_to_all(sent.reshape(EB, 2, 24, BLK), GZY, 0, 0, tiled=True)

    base = sent + STEP_ROOT * by_blocks(diffusion_noise)
    centers = base_nuclei[None, :, :] + displacements
    table = nucleus_table(centers, charges, orbital_decay, coefficients)
    nuclear = jnp.broadcast_to(nuclear_repulsion(centers, charges)[:, None], (NG, BLK))
    live = jnp.where(
        jnp.arange(BLK, dtype=jnp.int32)[None, :] < counts[:, None],
        weights.reshape(blocks_here, BLK),
        0.0,
    )
    own_live = lax.dynamic_slice_in_dim(live, member * 2, 2, 0)

    block_range = jnp.arange(blocks_here, dtype=jnp.int32)
    total = branch_source.shape[0]
    own_ids = device * blocks_here + block_range
    matches = (branch_source[None, :] == own_ids[:, None]).astype(jnp.int32)
    dest_slot = jnp.sum(matches * jnp.arange(total, dtype=jnp.int32)[None, :], axis=1)
    dest_device = dest_slot // blocks_here
    earlier = (
        (dest_device[None, :] == dest_device[:, None]) & (dest_slot[None, :] < dest_slot[:, None])
    ).astype(jnp.int32)
    send_slot = dest_device * CAP + jnp.sum(earlier, axis=1)
    selection = (
        jnp.arange(peers * CAP, dtype=jnp.int32)[:, None] == send_slot[None, :]
    ).astype(jnp.int32)
    picked = jnp.sum(selection * block_range[None, :], axis=1)
    my_sources = lax.dynamic_slice_in_dim(branch_source, device * blocks_here, blocks_here, 0)
    source_device = my_sources // blocks_here
    before = (
        (source_device[None, :] == source_device[:, None])
        & (block_range[None, :] < block_range[:, None])
    ).astype(jnp.int32)
    slots = source_device * CAP + jnp.sum(before, axis=1)

    out = walker_step(whole, table, nuclear, own_live)
    returned = lax.all_to_all(out, GZY, 0, 0, tiled=True).reshape(blocks_here, 32, BLK)
    send, local_energy = pack_step(picked, returned, base, live, peers)
    received = lax.all_to_all(send, GX, 0, 0, tiled=True)
    moved, new_weights, estimate = place_step(slots, replica.reshape(1), received)
    return (local_energy, estimate.reshape(NG // 2), moved, new_weights.reshape(blocks_here * BLK))


def solution(mesh):
    split = Mesh(
        mesh.devices.reshape(mesh.shape["gz"], 4, 4, mesh.shape["gy"]), ("gz", "gx_0", "gx_1", "gy")
    )
    placed = (
        P(("gz", "gy"), None, GX),
        P(("gz", "gy"), None, GX),
        P(),
        P(),
        P(),
        P(),
        P(),
        P(GX),
        P(GX),
        P(),
    )
    return jax.shard_map(
        local,
        mesh=split,
        in_specs=placed,
        out_specs=(P("gz", GX), P("gz"), P(("gz", "gy"), None, GX), P(GX)),
        check_vma=False,
    )
```

time: 271 us -> 107 us (0.39)
  other arithmetic: 156 us -> 3.12 us
  blocking collectives: 51 us -> 0 us
  Pallas kernels: 0 us -> 35 us
  waiting for transfers between devices: 18.7 us -> 37.9 us
  local copies, waits for them, and re-layouts: 19.3 us -> 10.1 us
  between operations: 4.67 us -> 0.84 us
    reduce_sum x43 -> x7, other arithmetic: 128 us -> 1.43 us  [the longest x1 0.6 us: local(): picked = jnp.sum(selection * block_range[None, :], axis=1)]
    pallas_call x0 -> x3, Pallas kernels: none -> 35 us  [the longest x1 30 us: walker_step(): pl.pallas_call(walker_kernel, out_shape=jax.ShapeDtypeStruct((EB, 2, 32,...]
    all_gather x1 -> x0, blocking collectives: 25.7 us -> none  [sent_together(): out = lax.all_gather(both, axis, axis=dim, tiled=True)]
    psum x2 -> x0, blocking collectives: 21.2 us -> none  [over_axes(): return functools.reduce(lax.psum, axes, x)]
    all_to_all x3, waiting for transfers between devices: 18.7 us -> 37.9 us  [the longest x1 14.5 us: local(): lax.all_to_all(out, GZY, 0, 0, tiled=True).reshape(blocks_here, 32, BLK)]
    add x27 -> x3, other arithmetic: 19.1 us -> 1.41 us  [the longest x1 0.79 us: local(): base = sent + STEP_ROOT * by_blocks(diffusion_noise)]
    dynamic_slice x9 -> x1, local copies, waits for them, and re-layouts: 6.52 us -> 0.6 us  [local(): own_live = lax.dynamic_slice_in_dim(live, member * 2, 2, 0)]
    all_to_all x1 -> x0, blocking collectives: 4.05 us -> none  [turned_blocks(): out = lax.all_to_all(out, axes[k], k, k, tiled=True)]
  transfers between devices with their start and end apart: 3 -> 3, of which waited for: 2 -> 3; matrix products, arithmetic and copies ran while one was open for 3% -> 4% of each run, Pallas kernels for 0% -> 0%
where the time goes in v1:
time: 107 us
  waiting for transfers between devices  37.9 us (35%)
  Pallas kernels  35 us (33%)
  starting transfers between devices  19.7 us (18%)
  local copies, waits for them, and re-layouts  10.1 us (9%)
  other arithmetic  3.12 us (3%)
    pallas_call x1, Pallas kernels, walker_step(): pl.pallas_call(walker_kernel, out_shape=jax.ShapeDtypeStruct((EB, 2, 32,...  30 us
    all_to_all x1, waiting for transfers between devices, local(): lax.all_to_all(out, GZY, 0, 0, tiled=True).reshape(blocks_here, 32, BLK)  14.5 us
    all_to_all x1, waiting for transfers between devices, local(): received = lax.all_to_all(send, GX, 0, 0, tiled=True)  13.2 us
    all_to_all x1, waiting for transfers between devices, local(): whole = lax.all_to_all(sent.reshape(EB, 2, 24, BLK), GZY, 0, 0, tiled=True)  10.2 us
    all_to_all x1, starting transfers between devices, local(): whole = lax.all_to_all(sent.reshape(EB, 2, 24, BLK), GZY, 0, 0, tiled=True)  8.72 us
    all_to_all x1, starting transfers between devices, local(): received = lax.all_to_all(send, GX, 0, 0, tiled=True)  7.04 us
    unnamed x36, local copies, waits for them, and re-layouts  5.79 us
    all_to_all x1, starting transfers between devices, local(): lax.all_to_all(out, GZY, 0, 0, tiled=True).reshape(blocks_here, 32, BLK)  3.97 us
  transfers between devices with their start and end apart: 3, of which 3 were waited for; matrix products, arithmetic and copies ran while one was open for 4% of the time, Pallas kernels for 0%

profile of v1, /device:TPU:32, one launch (start us, length us, event | category | flops | bytes accessed | tf_op | source)
XLA Modules:
  0.0 106.6 jit_solution(7172902785340575861)
XLA Ops:
  0.6 1.8 %copy.20 = f32[8,3,32,128]{3,0,1,2:T(8,128)} copy(f32[8,3,32,128]{3,0,2,1:T(8,128)} %bitcast.47) | data formatting | bytes 786432 | tf_op jit(solution)/shard_map/reshape | solution.py:345
  2.4 8.7 %all-to-all-start = ((f32[16,2,24,128]{3,2,1,0:T(8,128)}), f32[16,2,24,128]{3,2,1,0:T(8,128)S(1)}, u32[]{:S(2)}, u32[]{:S(2)}) async-start(f32[16,2,24,128]{3,2,1,0:T(8,128)} %bitcast.2), calls=%async_computation | async-start | bytes 786432 | tf_op jit(solution)/shard_map/all_to_all | solution.py:367
  11.2 0.7 copy-done.7
  11.8 0.6 copy-done.8
  12.7 0.7 copy-done.6
  13.4 0.6 constant_dynamic-slice_fusion.live
  14.5 10.2 %all-to-all-done.pos = f32[16,2,24,128]{3,2,1,0:T(8,128)S(1)} async-done(((f32[16,2,24,128]{3,2,1,0:T(8,128)}), f32[16,2,24,128]{3,2,1,0:T(8,128)S(1)}, u32[]{:S(2)}, u32[]{:S(2)}) %all-to-all-start) | async-done | bytes 393248 | tf_op jit(solution)/shard_map/all_to_all | solution.py:367
  24.7 1.2 %broadcast_in_dim.10.table = f32[12,16,8,128]{3,2,1,0:T(8,128)} broadcast(f32[12,16,8]{2,1,0:T(8,128)S(1)} %copy.21), dimensions={0,1,2} | broadcast | bytes 792576 | tf_op jit(solution)/shard_map/broadcast_in_dim | solution.py:340
  25.8 0.7 broadcast_in_dim.11.nuclear
  26.5 30.0 %walker_step.1 = f32[16,2,32,128]{3,2,1,0:T(8,128)} custom-call(f32[16,2,24,128]{3,2,1,0:T(8,128)} %copy-done.3, f32[12,16,8,128]{3,2,1,0:T(8,128)} %broadcast_in_dim.10.table, f32[8,128]{1,0:T(8,128)} %broadcast_in_dim.11.nuclear, f32[2,128]{1,0:T(2,128)} %constant_dynamic-slice_fusion.live), custom_call_target="tpu_custom_call" | custom-call | tf_op jit(solution)/shard_map/walker_step/pallas_call | solution.py:223
  56.5 4.0 %all-to-all-start.1 = ((f32[16,2,32,128]{3,2,1,0:T(8,128)}), f32[16,2,32,128]{3,2,1,0:T(8,128)S(1)}, u32[]{:S(2)}, u32[]{:S(2)}) async-start(f32[16,2,32,128]{3,2,1,0:T(8,128)} %walker_step.1), calls=%async_computation.1 | async-start | bytes 1048576 | tf_op jit(solution)/shard_map/all_to_all | solution.py:403
  60.5 0.2 select_reduce_fusion
  60.9 0.6 select_reduce_fusion.1.picked
  61.5 0.8 fusion.base
  62.3 14.5 %all-to-all-done.1 = f32[16,2,32,128]{3,2,1,0:T(8,128)S(1)} async-done(((f32[16,2,32,128]{3,2,1,0:T(8,128)}), f32[16,2,32,128]{3,2,1,0:T(8,128)S(1)}, u32[]{:S(2)}, u32[]{:S(2)}) %all-to-all-start.1) | async-done | bytes 524320 | tf_op jit(solution)/shard_map/all_to_all | solution.py:403
  76.8 0.8 copy-done.1
  77.6 2.5 %pack_step.1 = (f32[16,104,128]{2,1,0:T(8,128)}, f32[4,4096]{1,0:T(4,128)}) custom-call(s32[64]{0:T(128)} %select_reduce_fusion.1.picked, f32[32,32,128]{2,1,0:T(8,128)} %bitcast.46, f32[32,24,128]{2,1,0:T(8,128)} %fusion.base, f32[32,128]{1,0:T(8,128)} %copy-done.5), custom_call_target="tpu_custom_call" | custom-call | tf_op jit(solution)/shard_map/pack_step/pallas_call | solution.py:263
  80.0 7.0 %all-to-all-start.2 = ((f32[16,104,128]{2,1,0:T(8,128)}), f32[16,104,128]{2,1,0:T(8,128)S(1)}, u32[]{:S(2)}, u32[]{:S(2)}) async-start(f32[16,104,128]{2,1,0:T(8,128)} %get-tuple-element.10), calls=%async_computation.2 | async-start | bytes 1703936 | tf_op jit(solution)/shard_map/all_to_all | solution.py:405
  87.2 0.2 convert_reduce_fusion
  87.3 0.6 multiply_add_fusion.slots
  87.9 13.2 %all-to-all-done.2.received = f32[16,104,128]{2,1,0:T(8,128)S(1)} async-done(((f32[16,104,128]{2,1,0:T(8,128)}), f32[16,104,128]{2,1,0:T(8,128)S(1)}, u32[]{:S(2)}, u32[]{:S(2)}) %all-to-all-start.2) | async-done | bytes 852000 | tf_op jit(solution)/shard_map/all_to_all | solution.py:405
  101.1 0.9 copy-done
  102.0 2.5 %place_step.1 = (f32[8,3,4096]{2,1,0:T(4,128)}, f32[32,128]{1,0:T(8,128)}, f32[1,4]{1,0:T(1,128)}) custom-call(s32[32]{0:T(128)} %multiply_add_fusion.slots, s32[1]{0:T(128)} %bitcast.13.half, f32[16,104,128]{2,1,0:T(8,128)} %copy-done), custom_call_target="tpu_custom_call" | custom-call | tf_op jit(solution)/shard_map/place_step/pallas_call | solution.py:299
  104.6 2.0 %copy.25 = f32[8,3,4096]{2,0,1:T(8,128)} copy(f32[8,3,4096]{2,1,0:T(4,128)} %get-tuple-element.20) | data formatting | bytes 786432
  (50 shorter events, 0.9 us)
Async XLA Ops:
  2.4 8.7 %copy-start.10 = (f32[16,3]{0,1:T(4,128)S(1)}, f32[16,3]{0,1:T(4,128)}, u32[]{:S(2)}) copy-start(f32[16,3]{0,1:T(4,128)} %param.12) | copy-start | bytes 580
  2.4 22.3 %all-to-all-start = ((f32[16,2,24,128]{3,2,1,0:T(8,128)}), f32[16,2,24,128]{3,2,1,0:T(8,128)S(1)}, u32[]{:S(2)}, u32[]{:S(2)}) async-start(f32[16,2,24,128]{3,2,1,0:T(8,128)} %bitcast.2), calls=%async_computation | async-start | bytes 786432 | tf_op jit(solution)/shard_map/all_to_all | solution.py:367
  11.1 0.7 copy-start.7
  11.8 0.7 copy-start.8
  11.8 0.7 copy-start.12
  11.8 0.7 copy-start.13
  12.6 0.7 copy-start.6
  12.7 0.7 copy-start.11
  13.4 0.6 copy-start.5
  24.7 1.2 %copy-start.3 = (f32[16,2,24,128]{3,2,1,0:T(8,128)}, f32[16,2,24,128]{3,2,1,0:T(8,128)S(1)}, u32[]{:S(2)}) copy-start(f32[16,2,24,128]{3,2,1,0:T(8,128)S(1)} %all-to-all-done.pos) | copy-start | bytes 1179652
  56.5 4.0 %copy-start.9 = (s32[512]{0:T(512)S(1)}, s32[512]{0:T(512)}, u32[]{:S(2)}) copy-start(s32[512]{0:T(512)} %param.19) | copy-start | bytes 6148
  56.5 5.0 %copy-start.2 = (f32[8,3,4096]{2,0,1:T(8,128)S(1)}, f32[8,3,4096]{2,0,1:T(8,128)}, u32[]{:S(2)}) copy-start(f32[8,3,4096]{2,0,1:T(8,128)} %param.10) | copy-start | bytes 1179652
  56.5 5.0 %copy-start.4 = (f32[8,3,4096]{2,0,1:T(8,128)S(1)}, f32[8,3,4096]{2,0,1:T(8,128)}, u32[]{:S(2)}) copy-start(f32[8,3,4096]{2,0,1:T(8,128)} %param.11) | copy-start | bytes 1179652
  56.5 20.3 %all-to-all-start.1 = ((f32[16,2,32,128]{3,2,1,0:T(8,128)}), f32[16,2,32,128]{3,2,1,0:T(8,128)S(1)}, u32[]{:S(2)}, u32[]{:S(2)}) async-start(f32[16,2,32,128]{3,2,1,0:T(8,128)} %walker_step.1), calls=%async_computation.1 | async-start | bytes 1048576 | tf_op jit(solution)/shard_map/all_to_all | solution.py:403
  76.8 0.8 copy-start.1
  80.0 21.1 %all-to-all-start.2 = ((f32[16,104,128]{2,1,0:T(8,128)}), f32[16,104,128]{2,1,0:T(8,128)S(1)}, u32[]{:S(2)}, u32[]{:S(2)}) async-start(f32[16,104,128]{2,1,0:T(8,128)} %get-tuple-element.10), calls=%async_computation.2 | async-start | bytes 1703936 | tf_op jit(solution)/shard_map/all_to_all | solution.py:405
  101.1 0.9 copy-start

commit v2 on v1

--- a/solution.py
+++ b/solution.py
@@ -55,13 +55,11 @@
         inv = lax.rsqrt(square)
         p = 1.0 / (square * inv + 1.0)
         p2 = p * p
-        slope = (0.5 * p2) * inv
-        p3 = p2 * p
-        first = p + p2 + p3
-        second = (inv * inv) * (p3 + slope)
+        slope = p2 * inv
+        parts = (inv, slope, p2 * p, (inv * inv) * inv)
         if half:
-            first, second = 0.5 * first, 0.5 * second
-        return [slope * d[c] for c in range(3)], (sums[0] + first, sums[1] + second)
+            parts = tuple(0.5 * part for part in parts)
+        return [slope * d[c] for c in range(3)], tuple(a + b for a, b in zip(sums, parts))
 
     def load3(ref, *at):
         return [ref[(*at, slice(c * 8, c * 8 + 8), slice(None))] for c in range(3)]
@@ -113,7 +111,7 @@
         sums = inside(t, sums)
         return lax.fori_loop(0, t, lambda u, carry: across(u, t, carry), sums)
 
-    start = ((zero, zero), (zero, zero))
+    start = ((zero,) * 4, (zero,) * 4)
     sums = lax.fori_loop(0, EB // 2, outer, start)
 
     def finish(p, squares):
@@ -124,6 +122,7 @@
                 g = grad[p, h, c * 8 : c * 8 + 8, :]
                 for s in range(8):
                     g = g - roll8(back[p, h, s, c * 8 : c * 8 + 8, :], s)
+                g = 0.5 * g
                 grad[p, h, c * 8 : c * 8 + 8, :] = g
                 acc = acc + g * g
             out.append(acc)
@@ -132,7 +131,9 @@
     squares = lax.fori_loop(0, EB, finish, (zero, zero))
     totals = []
     for h in range(2):
-        t = sums[h][0] - SOFT * sums[h][1] - 0.5 * squares[h]
+        inv, slope, cube, inv3 = sums[h]
+        t = inv - (1.0 - 1.5 * SOFT) * slope + (1.0 - SOFT) * cube - (0.5 * SOFT) * inv3
+        t = t - 0.5 * squares[h]
         totals.append(jnp.broadcast_to(jnp.sum(t, axis=0, keepdims=True), (8, BLK)))
     return totals
 
@@ -230,6 +231,7 @@
             pltpu.VMEM((EB, 2, 8, 24, BLK), jnp.float32),
             pltpu.VMEM((EB, 2, 24, BLK), jnp.float32),
         ],
+        compiler_params=pltpu.CompilerParams(vmem_limit_bytes=24 * 1024 * 1024),
         name="walker_step",
     )(whole, table, nuclear, live)
 
@@ -268,6 +270,7 @@
         ),
         in_specs=[pl.BlockSpec(memory_space=pltpu.SMEM)] + [vmem] * 3,
         out_specs=(vmem, vmem),
+        compiler_params=pltpu.CompilerParams(vmem_limit_bytes=8 * 1024 * 1024),
         name="pack_step",
     )(picked, returned, base, live)
 
@@ -284,10 +287,9 @@
     estimate[...] = own[0:1, 0:4]
     for d in range(weights.shape[0]):
         peer, k = slots[d] // CAP, slots[d] % CAP
-        for e in range(8):
-            rows = [received[peer, pl.ds(k * 24 + c * 8 + e, 1), :] for c in range(3)]
-            for c in range(3):
-                moved[e, c : c + 1, d * BLK : (d + 1) * BLK] = rows[c]
+        for c in range(3):
+            at = pl.multiple_of(k * 24 + c * 8, 8)
+            moved[c, :, d * BLK : (d + 1) * BLK] = received[peer, pl.ds(at, 8), :]
         level = received[peer, pl.ds(96 + k, 1), :]
         weights[d : d + 1, :] = jnp.exp(-(level - reference))
 
@@ -299,12 +301,13 @@
     return pl.pallas_call(
         place_kernel,
         out_shape=(
-            jax.ShapeDtypeStruct((8, 3, blocks * BLK), jnp.float32),
+            jax.ShapeDtypeStruct((3, 8, blocks * BLK), jnp.float32),
             jax.ShapeDtypeStruct((blocks, BLK), jnp.float32),
             jax.ShapeDtypeStruct((1, NG // 2), jnp.float32),
         ),
         in_specs=[smem, smem, vmem],
         out_specs=(vmem, vmem, vmem),
+        compiler_params=pltpu.CompilerParams(vmem_limit_bytes=8 * 1024 * 1024),
         name="place_step",
     )(slots, half, received)
 
@@ -404,7 +407,7 @@
     send, local_energy = pack_step(picked, returned, base, live, peers)
     received = lax.all_to_all(send, GX, 0, 0, tiled=True)
     moved, new_weights, estimate = place_step(slots, replica.reshape(1), received)
-    return (local_energy, estimate.reshape(NG // 2), moved, new_weights.reshape(blocks_here * BLK))
+    return (local_energy, estimate.reshape(NG // 2), moved.transpose(1, 0, 2), new_weights.reshape(blocks_here * BLK))
 
 
 def solution(mesh):

time: 107 us -> 98.7 us (0.922)
  local copies, waits for them, and re-layouts: 10.1 us -> 4.26 us
  Pallas kernels: 35 us -> 31.7 us
  waiting for transfers between devices: 37.9 us -> 40.2 us
  other arithmetic: 3.12 us -> 1.35 us
    unnamed x36 -> x27, local copies, waits for them, and re-layouts: 5.79 us -> 2.07 us
    pallas_call x1, Pallas kernels: 30 us -> 28.3 us  [walker_step(): pl.pallas_call(walker_kernel, out_shape=jax.ShapeDtypeStruct((EB, 2, 32,...]
    all_to_all x1, waiting for transfers between devices: 14.5 us -> 15.7 us  [local(): lax.all_to_all(out, GZY, 0, 0, tiled=True).reshape(blocks_here, 32, BLK)]
  transfers between devices with their start and end apart: 3 -> 3, of which waited for: 3 -> 3; matrix products, arithmetic and copies ran while one was open for 4% -> 1% of each run, Pallas kernels for 0% -> 0%
where the time goes in v2:
time: 98.7 us; the launch traced here: 98.2 us
  waiting for transfers between devices  40.2 us (41%)
  Pallas kernels  31.7 us (32%)
  starting transfers between devices  19.7 us (20%)
  local copies, waits for them, and re-layouts  4.26 us (4%)
  other arithmetic  1.35 us (1%)
    pallas_call x1, Pallas kernels, walker_step(): pl.pallas_call(walker_kernel, out_shape=jax.ShapeDtypeStruct((EB, 2, 32,...  28.3 us
    all_to_all x1, waiting for transfers between devices, local(): lax.all_to_all(out, GZY, 0, 0, tiled=True).reshape(blocks_here, 32, BLK)  15.7 us
    all_to_all x1, waiting for transfers between devices, local(): received = lax.all_to_all(send, GX, 0, 0, tiled=True)  13.7 us
    all_to_all x1, waiting for transfers between devices, local(): whole = lax.all_to_all(sent.reshape(EB, 2, 24, BLK), GZY, 0, 0, tiled=True)  10.8 us
    all_to_all x1, starting transfers between devices, local(): whole = lax.all_to_all(sent.reshape(EB, 2, 24, BLK), GZY, 0, 0, tiled=True)  8.72 us
    all_to_all x1, starting transfers between devices, local(): received = lax.all_to_all(send, GX, 0, 0, tiled=True)  7.04 us
    all_to_all x1, starting transfers between devices, local(): lax.all_to_all(out, GZY, 0, 0, tiled=True).reshape(blocks_here, 32, BLK)  3.97 us
    unnamed x27, local copies, waits for them, and re-layouts  2.07 us
  transfers between devices with their start and end apart: 3, of which 3 were waited for; matrix products, arithmetic and copies ran while one was open for 1% of the time, Pallas kernels for 0%

profile of v2, /device:TPU:32, one launch (start us, length us, event | category | flops | bytes accessed | tf_op | source)
XLA Modules:
  0.0 98.2 jit_solution(4092256607448252542)
XLA Ops:
  0.6 1.8 %copy.19 = f32[8,3,32,128]{3,0,1,2:T(8,128)} copy(f32[8,3,32,128]{3,0,2,1:T(8,128)} %bitcast.48) | data formatting | bytes 786432 | tf_op jit(solution)/shard_map/reshape | solution.py:348
  2.4 8.7 %all-to-all-start = ((f32[16,2,24,128]{3,2,1,0:T(8,128)}), f32[16,2,24,128]{3,2,1,0:T(8,128)S(1)}, u32[]{:S(2)}, u32[]{:S(2)}) async-start(f32[16,2,24,128]{3,2,1,0:T(8,128)} %bitcast.2), calls=%async_computation | async-start | bytes 786432 | tf_op jit(solution)/shard_map/all_to_all | solution.py:370
  11.2 0.7 copy-done.3
  11.8 0.6 copy-done.4
  12.7 0.7 copy-done.2
  13.5 0.1 copy.20
  13.5 0.1 multiply_reduce_fusion
  13.7 0.1 subtract_multiply_fusion
  13.8 0.2 multiply_reduce_fusion.1
  13.9 10.8 %all-to-all-done.pos = f32[16,2,24,128]{3,2,1,0:T(8,128)S(1)} async-done(((f32[16,2,24,128]{3,2,1,0:T(8,128)}), f32[16,2,24,128]{3,2,1,0:T(8,128)S(1)}, u32[]{:S(2)}, u32[]{:S(2)}) %all-to-all-start) | async-done | bytes 393248 | tf_op jit(solution)/shard_map/all_to_all | solution.py:370
  24.7 0.3 broadcast_in_dim.10.table
  25.0 28.3 %walker_step.1 = f32[16,2,32,128]{3,2,1,0:T(8,128)} custom-call(f32[16,2,24,128]{3,2,1,0:T(8,128)S(1)} %all-to-all-done.pos, f32[12,16,8,128]{3,2,1,0:T(8,128)S(1)} %broadcast_in_dim.10.table, f32[8,128]{1,0:T(8,128)S(1)} %broadcast_in_dim.11.nuclear, f32[2,128]{1,0:T(2,128)S(1)} %constant_dynamic-slice_fusion.live), custom_call_target="tpu_custom_call" | custom-call | tf_op jit(solution)/shard_map/walker_step/pallas_call | solution.py:224
  53.3 4.0 %all-to-all-start.1 = ((f32[16,2,32,128]{3,2,1,0:T(8,128)}), f32[16,2,32,128]{3,2,1,0:T(8,128)S(1)}, u32[]{:S(2)}, u32[]{:S(2)}) async-start(f32[16,2,32,128]{3,2,1,0:T(8,128)} %walker_step.1), calls=%async_computation.1 | async-start | bytes 1048576 | tf_op jit(solution)/shard_map/all_to_all | solution.py:406
  57.3 0.2 select_reduce_fusion
  57.5 0.2 convert_reduce_fusion.1
  57.7 0.1 select_reduce_fusion.1.picked
  57.8 15.7 %all-to-all-done.1 = f32[16,2,32,128]{3,2,1,0:T(8,128)S(1)} async-done(((f32[16,2,32,128]{3,2,1,0:T(8,128)}), f32[16,2,32,128]{3,2,1,0:T(8,128)S(1)}, u32[]{:S(2)}, u32[]{:S(2)}) %all-to-all-start.1) | async-done | bytes 524320 | tf_op jit(solution)/shard_map/all_to_all | solution.py:406
  73.6 1.8 %pack_step.1 = (f32[16,104,128]{2,1,0:T(8,128)}, f32[4,4096]{1,0:T(4,128)}) custom-call(s32[64]{0:T(128)S(1)} %select_reduce_fusion.1.picked, f32[32,32,128]{2,1,0:T(8,128)S(1)} %bitcast.47, f32[32,24,128]{2,1,0:T(8,128)S(1)} %fusion.base, f32[32,128]{1,0:T(8,128)S(1)} %bitcast_select_fusion.live), custom_call_target="tpu_custom_call" | custom-call | tf_op jit(solution)/shard_map/pack_step/pallas_call | solution.py:265
  75.4 7.0 %all-to-all-start.2 = ((f32[16,104,128]{2,1,0:T(8,128)}), f32[16,104,128]{2,1,0:T(8,128)S(1)}, u32[]{:S(2)}, u32[]{:S(2)}) async-start(f32[16,104,128]{2,1,0:T(8,128)} %get-tuple-element.10), calls=%async_computation.2 | async-start | bytes 1703936 | tf_op jit(solution)/shard_map/all_to_all | solution.py:408
  82.5 0.1 and_select_fusion
  82.5 0.2 convert_reduce_fusion
  82.7 0.1 multiply_add_fusion.slots
  82.8 13.7 %all-to-all-done.2.received = f32[16,104,128]{2,1,0:T(8,128)S(1)} async-done(((f32[16,104,128]{2,1,0:T(8,128)}), f32[16,104,128]{2,1,0:T(8,128)S(1)}, u32[]{:S(2)}, u32[]{:S(2)}) %all-to-all-start.2) | async-done | bytes 852000 | tf_op jit(solution)/shard_map/all_to_all | solution.py:408
  96.5 1.6 %place_step.1 = (f32[3,8,4096]{2,1,0:T(8,128)}, f32[32,128]{1,0:T(8,128)}, f32[1,4]{1,0:T(1,128)}) custom-call(s32[32]{0:T(128)S(1)} %multiply_add_fusion.slots, s32[1]{0:T(128)} %bitcast.13.half, f32[16,104,128]{2,1,0:T(8,128)S(1)} %all-to-all-done.2.received), custom_call_target="tpu_custom_call" | custom-call | tf_op jit(solution)/shard_map/place_step/pallas_call | solution.py:301
  (41 shorter events, 0.4 us)
Async XLA Ops:
  2.4 8.7 %copy-start.6 = (f32[16,3]{0,1:T(4,128)S(1)}, f32[16,3]{0,1:T(4,128)}, u32[]{:S(2)}) copy-start(f32[16,3]{0,1:T(4,128)} %param.12) | copy-start | bytes 580
  2.4 22.3 %all-to-all-start = ((f32[16,2,24,128]{3,2,1,0:T(8,128)}), f32[16,2,24,128]{3,2,1,0:T(8,128)S(1)}, u32[]{:S(2)}, u32[]{:S(2)}) async-start(f32[16,2,24,128]{3,2,1,0:T(8,128)} %bitcast.2), calls=%async_computation | async-start | bytes 786432 | tf_op jit(solution)/shard_map/all_to_all | solution.py:370
  11.1 0.7 copy-start.3
  11.8 0.7 copy-start.4
  11.8 0.7 copy-start.8
  11.8 0.7 copy-start.9
  12.6 0.7 copy-start.2
  12.7 0.7 copy-start.7
  53.3 4.0 %copy-start.5 = (s32[512]{0:T(512)S(1)}, s32[512]{0:T(512)}, u32[]{:S(2)}) copy-start(s32[512]{0:T(512)} %param.19) | copy-start | bytes 6148
  53.3 4.5 %copy-start = (f32[8,3,4096]{2,0,1:T(8,128)S(1)}, f32[8,3,4096]{2,0,1:T(8,128)}, u32[]{:S(2)}) copy-start(f32[8,3,4096]{2,0,1:T(8,128)} %param.10) | copy-start | bytes 1179652
  53.3 4.5 %copy-start.1 = (f32[8,3,4096]{2,0,1:T(8,128)S(1)}, f32[8,3,4096]{2,0,1:T(8,128)}, u32[]{:S(2)}) copy-start(f32[8,3,4096]{2,0,1:T(8,128)} %param.11) | copy-start | bytes 1179652
  53.3 20.3 %all-to-all-start.1 = ((f32[16,2,32,128]{3,2,1,0:T(8,128)}), f32[16,2,32,128]{3,2,1,0:T(8,128)S(1)}, u32[]{:S(2)}, u32[]{:S(2)}) async-start(f32[16,2,32,128]{3,2,1,0:T(8,128)} %walker_step.1), calls=%async_computation.1 | async-start | bytes 1048576 | tf_op jit(solution)/shard_map/all_to_all | solution.py:406
  75.4 21.1 %all-to-all-start.2 = ((f32[16,104,128]{2,1,0:T(8,128)}), f32[16,104,128]{2,1,0:T(8,128)S(1)}, u32[]{:S(2)}, u32[]{:S(2)}) async-start(f32[16,104,128]{2,1,0:T(8,128)} %get-tuple-element.10), calls=%async_computation.2 | async-start | bytes 1703936 | tf_op jit(solution)/shard_map/all_to_all | solution.py:408

commit v3 on v2

--- a/solution.py
+++ b/solution.py
@@ -14,6 +14,7 @@
 NG = 8
 BLK = 128
 EB = 16
+GROUP = 4
 CAP = 4
 SLOT_ROWS = 24
 PEER_ROWS = CAP * SLOT_ROWS + 8
@@ -25,9 +26,6 @@
 STEP_ROOT = 0.1
 LN2 = math.log(2.0)
 LOG2E = 1.0 / LN2
-
-K_CONST, K_X, K_Y, K_Z, K_R2, K_AMP, K_PHI, K_CX, K_CY, K_CZ, K_SOFT, K_POT = range(12)
-
 
 def roll8(x, shift):
     shift %= 8
@@ -138,64 +136,119 @@
     return totals
 
 
-def walker_kernel(pos, table, nuclear, live, out, rot, back, grad):
+def split3(x):
+    high = x.astype(jnp.bfloat16).astype(jnp.float32)
+    rest = x - high
+    middle = rest.astype(jnp.bfloat16).astype(jnp.float32)
+    return high, middle, rest - middle
+
+
+def walker_kernel(
+    pos, spread, sums, table, nuclear, live, out, rot, back, grad,
+    left, right, square0, square1, parts0, parts1, held0, held1,
+):
     totals = pair_part(pos, rot, back, grad)
     zero = jnp.zeros((8, BLK), jnp.float32)
-
-    def electrons(p, carry):
-        energy, logs, pots = carry
-        for e in range(8):
-            xs, acc = [], []
+    one = jnp.ones((8, BLK), jnp.float32)
+    wide = jnp.zeros((16, BLK), jnp.float32)
+
+    column = lax.broadcasted_iota(jnp.int32, (8 * NA, 2 * BLK), 1)
+    for e in range(8):
+        weights = jnp.where(column % 8 == e, spread[...], 0.0)
+        left[e * 128 : e * 128 + 128, :] = weights
+    for row in range(24, 32):
+        right[row * 8 : row * 8 + 8, :] = jnp.full((8, 2 * BLK), 1.0 if row < 27 else 0.0)
+
+    def features(p):
+        for h in range(2):
+            lanes = slice(h * BLK, h * BLK + BLK)
+            x = [pos[p, h, c * 8 : c * 8 + 8, :] for c in range(3)]
+            x.append(x[0] * x[0] + x[1] * x[1] + x[2] * x[2])
+            tiles = []
+            for value in x:
+                high, middle, low = split3(value)
+                tiles += [high, high, high, middle, middle, low]
+            for row, tile in enumerate(tiles):
+                right[row * 8 : row * 8 + 8, lanes] = tile
+
+    def squares(square, first, count):
+        rows = slice(first * 128, (first + count) * 128)
+        square[rows, :] = jnp.dot(left[rows, :], right[...], preferred_element_type=jnp.float32)
+
+    def orbitals(square, parts, held, pots, first, count):
+        pots = list(pots)
+        pair = jnp.zeros((16, BLK), jnp.float32)
+        acc = {(e, h): [pair] * 2 for e in range(first, first + count) for h in range(2)}
+        for a in range(0, NA * 8, 16):
+            logs, phis, charge = (table[k, a : a + 16, :] for k in range(3))
             for h in range(2):
-                x = [
-                    jnp.broadcast_to(pos[p, h, c * 8 + e : c * 8 + e + 1, :], (8, BLK))
-                    for c in range(3)
-                ]
-                xs.append((x[0], x[1], x[2], x[0] * x[0] + x[1] * x[1] + x[2] * x[2]))
-                acc.append([zero] * 7)
-            pots = list(pots)
-            for a in range(NA):
-                for h in range(2):
-                    x, y, z, r2 = xs[h]
-                    square = (r2 * table[K_R2, a] + table[K_CONST, a]) + (
-                        (x * table[K_X, a] + y * table[K_Y, a]) + z * table[K_Z, a]
-                    )
-                    inv = lax.rsqrt(square)
-                    amp = jnp.exp2(table[K_AMP, a] - square * inv)
+                lanes = slice(h * BLK, h * BLK + BLK)
+                near = []
+                for e in range(first, first + count):
+                    sq = square[e * 128 + a : e * 128 + a + 16, lanes]
+                    inv = lax.rsqrt(sq)
+                    amp = jnp.exp2(logs - sq * inv)
                     u = amp * inv
-                    s = acc[h]
-                    acc[h] = [
-                        s[0] + amp * table[K_PHI, a],
-                        s[1] + amp,
-                        s[2] + u,
-                        s[3] + u * table[K_CX, a],
-                        s[4] + u * table[K_CY, a],
-                        s[5] + u * table[K_CZ, a],
-                        s[6] + (u * inv) * ((inv + LN2) * table[K_SOFT, a]),
-                    ]
-                    pots[h] = pots[h] + inv * table[K_POT, a]
-            new_energy, new_logs = [], []
+                    s = acc[e, h]
+                    acc[e, h] = [s[0] + amp * phis, s[1] + amp]
+                    parts[e, 256 + a : 272 + a, lanes] = (u * inv) * (inv + LN2)
+                    near.append(inv)
+                    high = u.astype(jnp.bfloat16).astype(jnp.float32)
+                    parts[e, a : a + 16, lanes] = high
+                    parts[e, 128 + a : 144 + a, lanes] = u - high
+                pots[h] = pots[h] + functools.reduce(jnp.add, near) * charge
+        for (e, h), s in acc.items():
+            for k in range(2):
+                held[e, h, k] = s[k][0:8, :] + s[k][8:16, :]
+        return tuple(pots)
+
+    def gather(p, parts, held, energy, logs, first, count):
+        energy, logs = list(energy), list(logs)
+        for e in range(first, first + count):
+            got = jnp.dot(sums[...], parts[e], preferred_element_type=jnp.float32)
             for h in range(2):
-                phi, amps, us, ux, uy, uz, soft = acc[h]
-                x, y, z, _ = xs[h]
+                lanes = slice(h * BLK, h * BLK + BLK)
+                o = [got[k * 8 : k * 8 + 8, lanes] for k in range(9)]
+                us, u = o[0], [o[1] + o[2], o[3] + o[4], o[5] + o[6]]
+                phi, amps, soft = held[e, h, 0], held[e, h, 1], o[7] + o[8]
                 ratio = 1.0 / phi
-                g = [(ux - x * us) * ratio, (uy - y * us) * ratio, (uz - z * us) * ratio]
-                j = [
-                    jnp.broadcast_to(grad[p, h, c * 8 + e : c * 8 + e + 1, :], (8, BLK))
-                    for c in range(3)
-                ]
+                at = [slice(c * 8 + e, c * 8 + e + 1) for c in range(3)]
+                x = [jnp.broadcast_to(pos[p, h, at[c], :], (8, BLK)) for c in range(3)]
+                j = [jnp.broadcast_to(grad[p, h, at[c], :], (8, BLK)) for c in range(3)]
+                g = [(u[c] - x[c] * us) * ratio for c in range(3)]
                 lap = (LN2 * amps - 2.0 * us - soft) * ratio
                 dot = g[0] * j[0] + g[1] * j[1] + g[2] * j[2]
-                new_energy.append(energy[h] - (0.5 * lap + dot))
-                new_logs.append(logs[h] + jnp.log2(phi))
+                energy[h] = energy[h] - (0.5 * lap + dot)
+                logs[h] = logs[h] + jnp.log2(phi)
                 for c in range(3):
-                    out[p, h, c * 8 + e : c * 8 + e + 1, :] = (g[c] + j[c])[0:1, :]
-            energy, logs = new_energy, new_logs
-        return tuple(energy), tuple(logs), tuple(pots)
+                    out[p, h, at[c], :] = (g[c] + j[c])[0:1, :]
+        return tuple(energy), tuple(logs)
+
+    parts1[...] = jnp.zeros_like(parts1)
+    for e in range(8):
+        for h in range(2):
+            held1[e, h, 0], held1[e, h, 1] = one, zero
+    features(0)
+    squares(square0, 0, 8)
+
+    def one_block(p, now, later, parts, held, before, kept, carry):
+        energy, logs, pots = carry
+        features(jnp.minimum(p + 1, EB - 1))
+        for first in range(0, 8, GROUP):
+            squares(later, first, GROUP)
+            pots = orbitals(now, parts, held, pots, first, GROUP)
+            energy, logs = gather(jnp.maximum(p - 1, 0), before, kept, energy, logs, first, GROUP)
+        return energy, logs, pots
+
+    def two_blocks(t, carry):
+        carry = one_block(2 * t, square0, square1, parts0, held0, parts1, held1, carry)
+        return one_block(2 * t + 1, square1, square0, parts1, held1, parts0, held0, carry)
 
     energy, logs, pots = lax.fori_loop(
-        0, EB, electrons, ((zero, zero), (zero, zero), (zero, zero))
+        0, EB // 2, two_blocks, ((zero, zero), (zero, zero), (wide, wide))
     )
+    pots = [q[0:8, :] + q[8:16, :] for q in pots]
+    energy, logs = gather(EB - 1, parts1, held1, energy, logs, 0, 8)
     row = lax.broadcasted_iota(jnp.int32, (8, BLK), 0)
     lane = lax.broadcasted_iota(jnp.int32, (8, BLK), 1)
     numerator = jnp.zeros((8, 1), jnp.float32)
@@ -219,21 +272,30 @@
                 out[half * 8 + q, h, 24:32, :] = tile
 
 
-def walker_step(whole, table, nuclear, live):
+def walker_step(whole, spread, sums, table, nuclear, live):
     vmem = pl.BlockSpec(memory_space=pltpu.VMEM)
+    rows, width = 8 * NA * 8, 2 * BLK
     return pl.pallas_call(
         walker_kernel,
         out_shape=jax.ShapeDtypeStruct((EB, 2, 32, BLK), jnp.float32),
-        in_specs=[vmem] * 4,
+        in_specs=[vmem] * 6,
         out_specs=vmem,
         scratch_shapes=[
             pltpu.VMEM((EB, 2, 8, 24, BLK), jnp.float32),
             pltpu.VMEM((EB, 2, 8, 24, BLK), jnp.float32),
             pltpu.VMEM((EB, 2, 24, BLK), jnp.float32),
+            pltpu.VMEM((rows, width), jnp.float32),
+            pltpu.VMEM((width, width), jnp.float32),
+            pltpu.VMEM((rows, width), jnp.float32),
+            pltpu.VMEM((rows, width), jnp.float32),
+            pltpu.VMEM((8, 3 * 8 * NA, width), jnp.float32),
+            pltpu.VMEM((8, 3 * 8 * NA, width), jnp.float32),
+            pltpu.VMEM((8, 2, 2, 8, BLK), jnp.float32),
+            pltpu.VMEM((8, 2, 2, 8, BLK), jnp.float32),
         ],
         compiler_params=pltpu.CompilerParams(vmem_limit_bytes=24 * 1024 * 1024),
         name="walker_step",
-    )(whole, table, nuclear, live)
+    )(whole, spread, sums, table, nuclear, live)
 
 
 def pack_kernel(picked, returned, base, live, send, energy):
@@ -320,27 +382,51 @@
     return 0.5 * jnp.sum(product / distance, axis=(1, 2))
 
 
-def nucleus_table(centers, charges, decay, coefficients):
+def nucleus_tables(centers, charges, decay, coefficients):
     c = jnp.moveaxis(centers, 1, 0)
     k = (decay * LOG2E)[:, None]
     k2 = k * k
     scale = decay[:, None] * k
     ones = jnp.ones((NA, NG), jnp.float32)
-    rows = [
-        k2 * (jnp.sum(c * c, axis=2) + SOFT),
-        -2.0 * k2 * c[:, :, 0],
-        -2.0 * k2 * c[:, :, 1],
-        -2.0 * k2 * c[:, :, 2],
-        k2 * ones,
-        jnp.log2(coefficients[:, None] * scale) * ones,
-        ones / scale,
-        c[:, :, 0],
-        c[:, :, 1],
-        c[:, :, 2],
-        SOFT * k2 * ones,
-        (charges[:, None] * k) * ones,
+
+    def thirds(x):
+        high = lax.reduce_precision(x, 8, 7)
+        rest = x - high
+        middle = lax.reduce_precision(rest, 8, 7)
+        return high, middle, rest - middle
+
+    rows = []
+    for value in [-2.0 * k2 * c[:, :, d] for d in range(3)] + [k2 * ones]:
+        high, middle, low = thirds(value)
+        rows += [high, middle, low, high, middle, high]
+    rows += list(thirds(k2 * (jnp.sum(c * c, axis=2) + SOFT)))
+    rows += [jnp.zeros_like(ones)] * (2 * BLK // 8 - len(rows))
+    spread = jnp.stack(rows, axis=-1).reshape(NA * NG, len(rows), 1)
+    spread = jnp.broadcast_to(spread, (NA * NG, len(rows), 8)).reshape(NA * NG, 2 * BLK)
+
+    def halves(x):
+        high = lax.reduce_precision(x, 8, 7)
+        return [high, x - high]
+
+    none = [0.0 * ones]
+    weights = [ones] + sum((halves(c[:, :, d]) for d in range(3)), []) + 2 * none
+    softs = 7 * none + halves(SOFT * k2 * ones)
+    same = jnp.eye(NG, dtype=jnp.float32)
+
+    def matrix(rows):
+        full = jnp.stack(rows)[:, None, :, :] * same[None, :, None, :]
+        return full.reshape(len(rows) * NG, NA * NG)
+
+    sums = jnp.concatenate([matrix(weights), matrix(weights), matrix(softs)], axis=1)
+
+    factors = [
+        jnp.log2(coefficients * scale[:, 0]),
+        1.0 / scale[:, 0],
+        charges * k[:, 0],
     ]
-    return jnp.broadcast_to(jnp.stack(rows)[..., None], (len(rows), NA, NG, BLK))
+    factors = jnp.stack(factors)[:, :, None, None]
+    factors = jnp.broadcast_to(factors, (3, NA, NG, BLK)).reshape(3, NA * NG, BLK)
+    return spread, sums, factors
 
 
 def by_blocks(x):
@@ -371,7 +457,7 @@
 
     base = sent + STEP_ROOT * by_blocks(diffusion_noise)
     centers = base_nuclei[None, :, :] + displacements
-    table = nucleus_table(centers, charges, orbital_decay, coefficients)
+    spread, sums, table = nucleus_tables(centers, charges, orbital_decay, coefficients)
     nuclear = jnp.broadcast_to(nuclear_repulsion(centers, charges)[:, None], (NG, BLK))
     live = jnp.where(
         jnp.arange(BLK, dtype=jnp.int32)[None, :] < counts[:, None],
@@ -402,7 +488,7 @@
     ).astype(jnp.int32)
     slots = source_device * CAP + jnp.sum(before, axis=1)
 
-    out = walker_step(whole, table, nuclear, own_live)
+    out = walker_step(whole, spread, sums, table, nuclear, own_live)
     returned = lax.all_to_all(out, GZY, 0, 0, tiled=True).reshape(blocks_here, 32, BLK)
     send, local_energy = pack_step(picked, returned, base, live, peers)
     received = lax.all_to_all(send, GX, 0, 0, tiled=True)

time: 98.7 us -> 96.9 us (0.982)
  waiting for transfers between devices: 40.2 us -> 36.5 us
  local copies, waits for them, and re-layouts: 4.26 us -> 7.57 us
  Pallas kernels: 31.7 us -> 30.3 us
    all_to_all x1, waiting for transfers between devices: 10.8 us -> 7 us  [local(): whole = lax.all_to_all(sent.reshape(EB, 2, 24, BLK), GZY, 0, 0, tiled=True)]
    pallas_call x1, Pallas kernels: 28.3 us -> 26.8 us  [walker_step(): pl.pallas_call(walker_kernel, out_shape=jax.ShapeDtypeStruct((EB, 2, 32,...]
    another operation x2 -> x20, local copies, waits for them, and re-layouts: 0.08 us -> 1.46 us  [the longest x18 1.38 us: nucleus_tables(): spread = jnp.stack(rows, axis=-1).reshape(NA * NG, len(rows), 1)]
    unnamed x27 -> x31, local copies, waits for them, and re-layouts: 2.07 us -> 2.11 us
  transfers between devices with their start and end apart: 3 -> 3, of which waited for: 3 -> 3; matrix products, arithmetic and copies ran while one was open for 1% -> 5% of each run, Pallas kernels for 0% -> 0%
where the time goes in v3:
time: 96.9 us; the launch traced here: 96.4 us
  waiting for transfers between devices  36.5 us (38%)
  Pallas kernels  30.3 us (31%)
  starting transfers between devices  19.6 us (20%)
  local copies, waits for them, and re-layouts  7.57 us (8%)
  other arithmetic  1.51 us (2%)
  between operations  0.98 us (1%)
    pallas_call x1, Pallas kernels, walker_step(): pl.pallas_call(walker_kernel, out_shape=jax.ShapeDtypeStruct((EB, 2, 32,...  26.8 us
    all_to_all x1, waiting for transfers between devices, local(): lax.all_to_all(out, GZY, 0, 0, tiled=True).reshape(blocks_here, 32, BLK)  15.7 us
    all_to_all x1, waiting for transfers between devices, local(): received = lax.all_to_all(send, GX, 0, 0, tiled=True)  13.7 us
    all_to_all x1, starting transfers between devices, local(): whole = lax.all_to_all(sent.reshape(EB, 2, 24, BLK), GZY, 0, 0, tiled=True)  8.59 us
    all_to_all x1, starting transfers between devices, local(): received = lax.all_to_all(send, GX, 0, 0, tiled=True)  7.04 us
    all_to_all x1, waiting for transfers between devices, local(): whole = lax.all_to_all(sent.reshape(EB, 2, 24, BLK), GZY, 0, 0, tiled=True)  7 us
    all_to_all x1, starting transfers between devices, local(): lax.all_to_all(out, GZY, 0, 0, tiled=True).reshape(blocks_here, 32, BLK)  3.97 us
    unnamed x31, local copies, waits for them, and re-layouts  2.11 us
  transfers between devices with their start and end apart: 3, of which 3 were waited for; matrix products, arithmetic and copies ran while one was open for 5% of the time, Pallas kernels for 0%

profile of v3, /device:TPU:32, one launch (start us, length us, event | category | flops | bytes accessed | tf_op | source)
XLA Modules:
  0.0 96.4 jit_solution(9296139210645901347)
XLA Ops:
  0.6 1.8 %copy.155 = f32[8,3,32,128]{3,0,1,2:T(8,128)} copy(f32[8,3,32,128]{3,0,2,1:T(8,128)} %bitcast.90) | data formatting | bytes 786432 | tf_op jit(solution)/shard_map/reshape | solution.py:434
  2.4 8.6 %all-to-all-start = ((f32[16,2,24,128]{3,2,1,0:T(8,128)}), f32[16,2,24,128]{3,2,1,0:T(8,128)S(1)}, u32[]{:S(2)}, u32[]{:S(2)}) async-start(f32[16,2,24,128]{3,2,1,0:T(8,128)} %bitcast.2), calls=%async_computation | async-start | bytes 786432 | tf_op jit(solution)/shard_map/all_to_all | solution.py:456
  11.1 0.7 copy-done.3
  11.8 0.6 copy-done.4
  14.3 0.1 stack.116
  15.4 0.1 broadcast_multiply_fusion.1
  15.5 0.3 mul.242
  15.8 0.3 mul.246
  16.1 0.7 copy-done.2
  16.9 0.1 copy.201.spread
  17.2 0.1 multiply_reduce_fusion
  17.4 0.2 multiply_reduce_fusion.1
  17.5 7.0 %all-to-all-done.pos = f32[16,2,24,128]{3,2,1,0:T(8,128)S(1)} async-done(((f32[16,2,24,128]{3,2,1,0:T(8,128)}), f32[16,2,24,128]{3,2,1,0:T(8,128)S(1)}, u32[]{:S(2)}, u32[]{:S(2)}) %all-to-all-start) | async-done | bytes 393248 | tf_op jit(solution)/shard_map/all_to_all | solution.py:456
  24.5 0.1 broadcast_in_dim.19.table
  24.7 26.8 %walker_step.1 = f32[16,2,32,128]{3,2,1,0:T(8,128)} custom-call(f32[16,2,24,128]{3,2,1,0:T(8,128)S(1)} %all-to-all-done.pos, f32[128,256]{1,0:T(8,128)S(1)} %copy.201.spread, f32[72,384]{1,0:T(8,128)S(1)} %pad_maximum_fusion.sums, f32[3,128,128]{2,1,0:T(8,128)S(1)} %broadcast_in_dim.19.table, f32[8,128]{1,0:T(8,128)S(1)} %broadcast_in_dim.20.nuclear, ...), custom_call_target="tpu_custom_call" | custom-call | tf_op jit(solution)/shard_map/walker_step/pallas_call | solution.py:278
  51.5 4.0 %all-to-all-start.1 = ((f32[16,2,32,128]{3,2,1,0:T(8,128)}), f32[16,2,32,128]{3,2,1,0:T(8,128)S(1)}, u32[]{:S(2)}, u32[]{:S(2)}) async-start(f32[16,2,32,128]{3,2,1,0:T(8,128)} %walker_step.1), calls=%async_computation.1 | async-start | bytes 1048576 | tf_op jit(solution)/shard_map/all_to_all | solution.py:492
  55.5 0.2 select_reduce_fusion
  55.7 0.2 convert_reduce_fusion.1
  56.1 15.7 %all-to-all-done.1 = f32[16,2,32,128]{3,2,1,0:T(8,128)S(1)} async-done(((f32[16,2,32,128]{3,2,1,0:T(8,128)}), f32[16,2,32,128]{3,2,1,0:T(8,128)S(1)}, u32[]{:S(2)}, u32[]{:S(2)}) %all-to-all-start.1) | async-done | bytes 524320 | tf_op jit(solution)/shard_map/all_to_all | solution.py:492
  71.8 1.8 %pack_step.1 = (f32[16,104,128]{2,1,0:T(8,128)}, f32[4,4096]{1,0:T(4,128)}) custom-call(s32[64]{0:T(128)S(1)} %select_reduce_fusion.1.picked, f32[32,32,128]{2,1,0:T(8,128)S(1)} %bitcast.89, f32[32,24,128]{2,1,0:T(8,128)S(1)} %fusion.base, f32[32,128]{1,0:T(8,128)S(1)} %bitcast_select_fusion.live), custom_call_target="tpu_custom_call" | custom-call | tf_op jit(solution)/shard_map/pack_step/pallas_call | solution.py:327
  73.7 7.0 %all-to-all-start.2 = ((f32[16,104,128]{2,1,0:T(8,128)}), f32[16,104,128]{2,1,0:T(8,128)S(1)}, u32[]{:S(2)}, u32[]{:S(2)}) async-start(f32[16,104,128]{2,1,0:T(8,128)} %get-tuple-element.10), calls=%async_computation.2 | async-start | bytes 1703936 | tf_op jit(solution)/shard_map/all_to_all | solution.py:494
  80.8 0.2 convert_reduce_fusion
  81.0 13.7 %all-to-all-done.2.received = f32[16,104,128]{2,1,0:T(8,128)S(1)} async-done(((f32[16,104,128]{2,1,0:T(8,128)}), f32[16,104,128]{2,1,0:T(8,128)S(1)}, u32[]{:S(2)}, u32[]{:S(2)}) %all-to-all-start.2) | async-done | bytes 852000 | tf_op jit(solution)/shard_map/all_to_all | solution.py:494
  94.8 1.6 %place_step.1 = (f32[3,8,4096]{2,1,0:T(8,128)}, f32[32,128]{1,0:T(8,128)}, f32[1,4]{1,0:T(1,128)}) custom-call(s32[32]{0:T(128)S(1)} %multiply_add_fusion.slots, s32[1]{0:T(128)} %bitcast.32.half, f32[16,104,128]{2,1,0:T(8,128)S(1)} %all-to-all-done.2.received), custom_call_target="tpu_custom_call" | custom-call | tf_op jit(solution)/shard_map/place_step/pallas_call | solution.py:363
  (90 shorter events, 3.6 us)
Async XLA Ops:
  2.4 22.1 %all-to-all-start = ((f32[16,2,24,128]{3,2,1,0:T(8,128)}), f32[16,2,24,128]{3,2,1,0:T(8,128)S(1)}, u32[]{:S(2)}, u32[]{:S(2)}) async-start(f32[16,2,24,128]{3,2,1,0:T(8,128)} %bitcast.2), calls=%async_computation | async-start | bytes 786432 | tf_op jit(solution)/shard_map/all_to_all | solution.py:456
  11.0 0.7 copy-start.3
  11.0 0.7 copy-start.6
  11.7 0.7 copy-start.4
  11.7 0.7 copy-start.8
  11.7 0.7 copy-start.9
  16.1 0.7 copy-start.2
  16.1 0.7 copy-start.7
  51.5 4.0 %copy-start.5 = (s32[512]{0:T(512)S(1)}, s32[512]{0:T(512)}, u32[]{:S(2)}) copy-start(s32[512]{0:T(512)} %param.19) | copy-start | bytes 6148
  51.5 4.5 %copy-start = (f32[8,3,4096]{2,0,1:T(8,128)S(1)}, f32[8,3,4096]{2,0,1:T(8,128)}, u32[]{:S(2)}) copy-start(f32[8,3,4096]{2,0,1:T(8,128)} %param.10) | copy-start | bytes 1179652
  51.5 4.5 %copy-start.1 = (f32[8,3,4096]{2,0,1:T(8,128)S(1)}, f32[8,3,4096]{2,0,1:T(8,128)}, u32[]{:S(2)}) copy-start(f32[8,3,4096]{2,0,1:T(8,128)} %param.11) | copy-start | bytes 1179652
  51.5 20.3 %all-to-all-start.1 = ((f32[16,2,32,128]{3,2,1,0:T(8,128)}), f32[16,2,32,128]{3,2,1,0:T(8,128)S(1)}, u32[]{:S(2)}, u32[]{:S(2)}) async-start(f32[16,2,32,128]{3,2,1,0:T(8,128)} %walker_step.1), calls=%async_computation.1 | async-start | bytes 1048576 | tf_op jit(solution)/shard_map/all_to_all | solution.py:492
  73.7 21.1 %all-to-all-start.2 = ((f32[16,104,128]{2,1,0:T(8,128)}), f32[16,104,128]{2,1,0:T(8,128)S(1)}, u32[]{:S(2)}, u32[]{:S(2)}) async-start(f32[16,104,128]{2,1,0:T(8,128)} %get-tuple-element.10), calls=%async_computation.2 | async-start | bytes 1703936 | tf_op jit(solution)/shard_map/all_to_all | solution.py:494

commit v4 on v3

--- a/solution.py
+++ b/solution.py
@@ -143,11 +143,15 @@
     return high, middle, rest - middle
 
 
-def walker_kernel(
-    pos, spread, sums, table, nuclear, live, out, rot, back, grad,
+def pair_kernel(pos, grad, totals, rot, back):
+    for h, total in enumerate(pair_part(pos, rot, back, grad)):
+        totals[h] = total
+
+
+def orbital_kernel(
+    pos, grad, totals, spread, sums, table, nuclear, live, out,
     left, right, square0, square1, parts0, parts1, held0, held1,
 ):
-    totals = pair_part(pos, rot, back, grad)
     zero = jnp.zeros((8, BLK), jnp.float32)
     one = jnp.ones((8, BLK), jnp.float32)
     wide = jnp.zeros((16, BLK), jnp.float32)
@@ -155,7 +159,7 @@
     column = lax.broadcasted_iota(jnp.int32, (8 * NA, 2 * BLK), 1)
     for e in range(8):
         weights = jnp.where(column % 8 == e, spread[...], 0.0)
-        left[e * 128 : e * 128 + 128, :] = weights
+        left[e * 128 : e * 128 + 128, :] = weights.astype(jnp.bfloat16)
     for row in range(24, 32):
         right[row * 8 : row * 8 + 8, :] = jnp.full((8, 2 * BLK), 1.0 if row < 27 else 0.0)
 
@@ -173,7 +177,8 @@
 
     def squares(square, first, count):
         rows = slice(first * 128, (first + count) * 128)
-        square[rows, :] = jnp.dot(left[rows, :], right[...], preferred_element_type=jnp.float32)
+        factor = right[...].astype(jnp.bfloat16)
+        square[rows, :] = jnp.dot(left[rows, :], factor, preferred_element_type=jnp.float32)
 
     def orbitals(square, parts, held, pots, first, count):
         pots = list(pots)
@@ -205,7 +210,8 @@
     def gather(p, parts, held, energy, logs, first, count):
         energy, logs = list(energy), list(logs)
         for e in range(first, first + count):
-            got = jnp.dot(sums[...], parts[e], preferred_element_type=jnp.float32)
+            factor = parts[e].astype(jnp.bfloat16)
+            got = jnp.dot(sums[...], factor, preferred_element_type=jnp.float32)
             for h in range(2):
                 lanes = slice(h * BLK, h * BLK + BLK)
                 o = [got[k * 8 : k * 8 + 8, lanes] for k in range(9)]
@@ -220,8 +226,6 @@
                 dot = g[0] * j[0] + g[1] * j[1] + g[2] * j[2]
                 energy[h] = energy[h] - (0.5 * lap + dot)
                 logs[h] = logs[h] + jnp.log2(phi)
-                for c in range(3):
-                    out[p, h, at[c], :] = (g[c] + j[c])[0:1, :]
         return tuple(energy), tuple(logs)
 
     parts1[...] = jnp.zeros_like(parts1)
@@ -263,28 +267,43 @@
         local.append(e)
     placed = jnp.where(lane == row, numerator, 0.0) + jnp.where(lane == row + 8, denominator, 0.0)
     placed = jnp.broadcast_to(jnp.sum(placed, axis=0, keepdims=True), (8, BLK))
-    for h in range(2):
-        first = jnp.broadcast_to(local[h][0:1, :], (8, BLK))
-        for half in range(2):
-            e = local[h] if half == 0 else roll8(local[h], 4)
-            tile = jnp.where(row < 4, e, jnp.where(row == 4, first, placed))
-            for q in range(8):
-                out[half * 8 + q, h, 24:32, :] = tile
-
-
-def walker_step(whole, spread, sums, table, nuclear, live):
+    firsts = [jnp.broadcast_to(local[h][0:1, :], (8, BLK)) for h in range(2)]
+    rest = jnp.where(row == 0, firsts[0], jnp.where(row == 1, firsts[1], placed))
+    for q in range(EB):
+        low, high = local if q < EB // 2 else (roll8(local[0], 4), roll8(local[1], 4))
+        out[q, 0:8, :] = jnp.where(row < 4, low, roll8(high, 4))
+        out[q, 8:16, :] = rest
+
+
+def pair_step(whole):
+    vmem = pl.BlockSpec(memory_space=pltpu.VMEM)
+    return pl.pallas_call(
+        pair_kernel,
+        out_shape=(
+            jax.ShapeDtypeStruct((EB, 2, 24, BLK), jnp.float32),
+            jax.ShapeDtypeStruct((2, 8, BLK), jnp.float32),
+        ),
+        in_specs=[vmem],
+        out_specs=(vmem, vmem),
+        scratch_shapes=[pltpu.VMEM((EB, 2, 8, 24, BLK), jnp.float32)] * 2,
+        compiler_params=pltpu.CompilerParams(vmem_limit_bytes=16 * 1024 * 1024),
+        cost_estimate=pl.CostEstimate(
+            flops=EB * EB * BLK * 2 * 32 * 32, transcendentals=0, bytes_accessed=1 << 20
+        ),
+        name="pair_step",
+    )(whole)
+
+
+def orbital_step(whole, grad, totals, spread, sums, table, nuclear, live):
     vmem = pl.BlockSpec(memory_space=pltpu.VMEM)
     rows, width = 8 * NA * 8, 2 * BLK
     return pl.pallas_call(
-        walker_kernel,
-        out_shape=jax.ShapeDtypeStruct((EB, 2, 32, BLK), jnp.float32),
-        in_specs=[vmem] * 6,
+        orbital_kernel,
+        out_shape=jax.ShapeDtypeStruct((EB, 16, BLK), jnp.float32),
+        in_specs=[vmem] * 8,
         out_specs=vmem,
         scratch_shapes=[
-            pltpu.VMEM((EB, 2, 8, 24, BLK), jnp.float32),
-            pltpu.VMEM((EB, 2, 8, 24, BLK), jnp.float32),
-            pltpu.VMEM((EB, 2, 24, BLK), jnp.float32),
-            pltpu.VMEM((rows, width), jnp.float32),
+            pltpu.VMEM((rows, width), jnp.bfloat16),
             pltpu.VMEM((width, width), jnp.float32),
             pltpu.VMEM((rows, width), jnp.float32),
             pltpu.VMEM((rows, width), jnp.float32),
@@ -293,17 +312,60 @@
             pltpu.VMEM((8, 2, 2, 8, BLK), jnp.float32),
             pltpu.VMEM((8, 2, 2, 8, BLK), jnp.float32),
         ],
-        compiler_params=pltpu.CompilerParams(vmem_limit_bytes=24 * 1024 * 1024),
-        name="walker_step",
-    )(whole, spread, sums, table, nuclear, live)
-
-
-def pack_kernel(picked, returned, base, live, send, energy):
-    sums = returned[0, 29:30, :]
+        compiler_params=pltpu.CompilerParams(vmem_limit_bytes=20 * 1024 * 1024),
+        cost_estimate=pl.CostEstimate(
+            flops=EB * 8 * NA * NG * BLK * 2 * 32 * 2, transcendentals=0, bytes_accessed=1 << 20
+        ),
+        name="orbital_step",
+    )(whole, grad, totals, spread, sums, table, nuclear, live)
+
+
+def own_kernel(scalars, positions, noise, base):
+    wide = 4 * BLK
+
+    def four(t, _):
+        at = pl.multiple_of(t * wide, wide)
+        r = [positions[c, :, pl.ds(at, wide)] for c in range(3)]
+        phi = jnp.zeros((8, wide), jnp.float32)
+        grad = [phi, phi, phi]
+        for a in range(NA):
+            v = [r[c] - scalars[c, a] for c in range(3)]
+            square = (v[0] * v[0] + v[1] * v[1]) + (v[2] * v[2] + SOFT)
+            inv = lax.rsqrt(square)
+            amp = jnp.exp2(scalars[4, a] - scalars[3, a] * (square * inv))
+            u = amp * inv
+            phi = phi + amp * scalars[5, a]
+            grad = [grad[c] + u * v[c] for c in range(3)]
+        step = TIME_STEP / phi
+        for c in range(3):
+            moved = r[c] + STEP_ROOT * noise[c, :, pl.ds(at, wide)] - step * grad[c]
+            for k in range(4):
+                base[t * 4 + k, c * 8 : c * 8 + 8, :] = moved[:, k * BLK : (k + 1) * BLK]
+        return 0
+
+    lax.fori_loop(0, base.shape[0] // 4, four, 0)
+
+
+def own_step(scalars, positions, noise):
+    vmem = pl.BlockSpec(memory_space=pltpu.VMEM)
+    blocks = positions.shape[2] // BLK
+    return pl.pallas_call(
+        own_kernel,
+        out_shape=jax.ShapeDtypeStruct((blocks, 24, BLK), jnp.float32),
+        in_specs=[pl.BlockSpec(memory_space=pltpu.SMEM), vmem, vmem],
+        out_specs=vmem,
+        compiler_params=pltpu.CompilerParams(vmem_limit_bytes=8 * 1024 * 1024),
+        name="own_step",
+    )(scalars, positions, noise)
+
+
+def pack_kernel(picked, returned, energies, base, live, send, energy):
+    sums = energies[0, 10:11, :]
     for p in range(1, EB):
-        sums = sums + returned[2 * p, 29:30, :]
+        sums = sums + energies[p, 10:11, :]
     for b in range(2 * EB):
-        energy[:, b * BLK : (b + 1) * BLK] = returned[b, 24:28, :]
+        at = (b % 2) * 4
+        energy[:, b * BLK : (b + 1) * BLK] = energies[b // 2, at : at + 4, :]
 
     def one_peer(peer, _):
         for k in range(CAP):
@@ -313,7 +375,7 @@
                     base[b, c * 8 : c * 8 + 8, :] + TIME_STEP * returned[b, c * 8 : c * 8 + 8, :]
                 )
             alive = live[pl.ds(b, 1), :]
-            level = returned[b, 28:29, :] - jnp.log(alive)
+            level = energies[b // 2, pl.ds(8 + b % 2, 1), :] - jnp.log(alive)
             send[peer, 96 + k : 97 + k, :] = jnp.where(alive > 0.0, level, 3.0e38)
         send[peer, 100:101, :] = sums
         send[peer, 101:104, :] = jnp.zeros((3, BLK), jnp.float32)
@@ -322,7 +384,7 @@
     lax.fori_loop(0, send.shape[0], one_peer, 0)
 
 
-def pack_step(picked, returned, base, live, peers):
+def pack_step(picked, returned, energies, base, live, peers):
     vmem = pl.BlockSpec(memory_space=pltpu.VMEM)
     return pl.pallas_call(
         pack_kernel,
@@ -330,11 +392,11 @@
             jax.ShapeDtypeStruct((peers, PEER_ROWS, BLK), jnp.float32),
             jax.ShapeDtypeStruct((NG // 2, 2 * EB * BLK), jnp.float32),
         ),
-        in_specs=[pl.BlockSpec(memory_space=pltpu.SMEM)] + [vmem] * 3,
+        in_specs=[pl.BlockSpec(memory_space=pltpu.SMEM)] + [vmem] * 4,
         out_specs=(vmem, vmem),
         compiler_params=pltpu.CompilerParams(vmem_limit_bytes=8 * 1024 * 1024),
         name="pack_step",
-    )(picked, returned, base, live)
+    )(picked, returned, energies, base, live)
 
 
 def place_kernel(slots, half, received, moved, weights, estimate):
@@ -418,6 +480,7 @@
         return full.reshape(len(rows) * NG, NA * NG)
 
     sums = jnp.concatenate([matrix(weights), matrix(weights), matrix(softs)], axis=1)
+    sums = sums.astype(jnp.bfloat16)
 
     factors = [
         jnp.log2(coefficients * scale[:, 0]),
@@ -455,8 +518,12 @@
     sent = by_blocks(positions)
     whole = lax.all_to_all(sent.reshape(EB, 2, 24, BLK), GZY, 0, 0, tiled=True)
 
-    base = sent + STEP_ROOT * by_blocks(diffusion_noise)
     centers = base_nuclei[None, :, :] + displacements
+    first = centers[0]
+    rate = orbital_decay * LOG2E
+    level = jnp.log2(coefficients * orbital_decay)
+    scalars = jnp.stack([first[:, 0], first[:, 1], first[:, 2], rate, level, 1.0 / orbital_decay])
+    base = own_step(scalars, positions.transpose(1, 0, 2), diffusion_noise.transpose(1, 0, 2))
     spread, sums, table = nucleus_tables(centers, charges, orbital_decay, coefficients)
     nuclear = jnp.broadcast_to(nuclear_repulsion(centers, charges)[:, None], (NG, BLK))
     live = jnp.where(
@@ -488,9 +555,15 @@
     ).astype(jnp.int32)
     slots = source_device * CAP + jnp.sum(before, axis=1)
 
-    out = walker_step(whole, spread, sums, table, nuclear, own_live)
-    returned = lax.all_to_all(out, GZY, 0, 0, tiled=True).reshape(blocks_here, 32, BLK)
-    send, local_energy = pack_step(picked, returned, base, live, peers)
+    whole, base, spread, sums, table, nuclear, own_live, picked = lax.optimization_barrier(
+        (whole, base, spread, sums, table, nuclear, own_live, picked)
+    )
+    grad, totals = pair_step(whole)
+    returned = lax.all_to_all(grad, GZY, 0, 0, tiled=True).reshape(blocks_here, 24, BLK)
+    out = orbital_step(whole, grad, totals, spread, sums, table, nuclear, own_live)
+    returned, out = lax.optimization_barrier((returned, out))
+    energies = lax.all_to_all(out, GZY, 0, 0, tiled=True)
+    send, local_energy = pack_step(picked, returned, energies, base, live, peers)
     received = lax.all_to_all(send, GX, 0, 0, tiled=True)
     moved, new_weights, estimate = place_step(slots, replica.reshape(1), received)
     return (local_energy, estimate.reshape(NG // 2), moved.transpose(1, 0, 2), new_weights.reshape(blocks_here * BLK))

time: 96.9 us -> 96.1 us (level)
  waiting for transfers between devices: 36.5 us -> 18.4 us
  blocking collectives: 0 us -> 15.2 us
  Pallas kernels: 30.3 us -> 32.4 us
    all_to_all x1, waiting for transfers between devices: 15.7 us -> 0.01 us  [local(): lax.all_to_all(grad, GZY, 0, 0, tiled=True).reshape(blocks_here, 24, BLK)]
    all_to_all x0 -> x1, blocking collectives: none -> 15.2 us  [local(): energies = lax.all_to_all(out, GZY, 0, 0, tiled=True)]
    all_to_all x1, waiting for transfers between devices: 7 us -> 4.09 us  [local(): whole = lax.all_to_all(sent.reshape(EB, 2, 24, BLK), GZY, 0, 0, tiled=True)]
    pallas_call x1 -> x3, Pallas kernels: 26.8 us -> 28.7 us  [the longest x1 15.6 us: orbital_step(): pl.pallas_call(orbital_kernel, out_shape=jax.ShapeDtypeStruct((EB, 16, BL...]
    unnamed x31 -> x32, local copies, waits for them, and re-layouts: 2.11 us -> 2.04 us
  transfers between devices with their start and end apart: 3 -> 3, of which waited for: 3 -> 2; matrix products, arithmetic and copies ran while one was open for 5% -> 5% of each run, Pallas kernels for 0% -> 19%
where the time goes in v4:
time: 96.1 us; the launch traced here: 95.5 us
  Pallas kernels  32.4 us (34%)
  starting transfers between devices  19.4 us (20%)
  waiting for transfers between devices  18.4 us (19%)
  blocking collectives  15.2 us (16%)
  local copies, waits for them, and re-layouts  7.57 us (8%)
  other arithmetic  1.47 us (2%)
  between operations  1.05 us (1%)
    pallas_call x1, Pallas kernels, orbital_step(): pl.pallas_call(orbital_kernel, out_shape=jax.ShapeDtypeStruct((EB, 16, BL...  15.6 us
    all_to_all x1, blocking collectives, local(): energies = lax.all_to_all(out, GZY, 0, 0, tiled=True)  15.2 us
    all_to_all x1, waiting for transfers between devices, local(): received = lax.all_to_all(send, GX, 0, 0, tiled=True)  14.3 us
    pallas_call x1, Pallas kernels, pair_step(): pl.pallas_call(pair_kernel, out_shape=(jax.ShapeDtypeStruct((EB, 2, 24, B...  10.6 us
    all_to_all x1, starting transfers between devices, local(): whole = lax.all_to_all(sent.reshape(EB, 2, 24, BLK), GZY, 0, 0, tiled=True)  8.59 us
    all_to_all x1, starting transfers between devices, local(): received = lax.all_to_all(send, GX, 0, 0, tiled=True)  7.02 us
    all_to_all x1, waiting for transfers between devices, local(): whole = lax.all_to_all(sent.reshape(EB, 2, 24, BLK), GZY, 0, 0, tiled=True)  4.09 us
    all_to_all x1, starting transfers between devices, local(): lax.all_to_all(grad, GZY, 0, 0, tiled=True).reshape(blocks_here, 24, BLK)  3.83 us
  transfers between devices with their start and end apart: 3, of which 2 were waited for; matrix products, arithmetic and copies ran while one was open for 5% of the time, Pallas kernels for 19%

profile of v4, /device:TPU:32, one launch (start us, length us, event | category | flops | bytes accessed | tf_op | source)
XLA Modules:
  0.0 95.5 jit_solution(13821639819359734278)
XLA Ops:
  0.6 1.8 %copy.152 = f32[8,3,32,128]{3,0,1,2:T(8,128)} copy(f32[8,3,32,128]{3,0,2,1:T(8,128)} %bitcast.95) | data formatting | bytes 786432 | tf_op jit(solution)/shard_map/reshape | solution.py:497
  2.4 8.6 %all-to-all-start = ((f32[16,2,24,128]{3,2,1,0:T(8,128)}), f32[16,2,24,128]{3,2,1,0:T(8,128)S(1)}, u32[]{:S(2)}, u32[]{:S(2)}) async-start(f32[16,2,24,128]{3,2,1,0:T(8,128)} %bitcast.2), calls=%async_computation | async-start | bytes 786432 | tf_op jit(solution)/shard_map/all_to_all | solution.py:519
  11.1 0.7 copy-done.3
  11.8 0.6 copy-done.4
  12.5 0.6 copy-done.8
  13.9 0.1 multiply_convert_fusion.1
  14.1 0.3 mul.231
  14.4 0.3 reshape.396
  14.8 0.2 select_reduce_fusion
  14.9 0.2 convert_reduce_fusion.1
  17.6 2.4 %own_step.1.base = f32[32,24,128]{2,1,0:T(8,128)S(1)} custom-call(f32[6,16]{1,0:T(8,128)S(1)} %stack.119.scalars, f32[3,8,4096]{2,1,0:T(8,128)S(1)} %bitcast.96, f32[3,8,4096]{2,1,0:T(8,128)S(1)} %bitcast.97), custom_call_target="tpu_custom_call" | custom-call | tf_op jit(solution)/shard_map/own_step/pallas_call | solution.py:352
  20.1 0.1 multiply_reduce_fusion
  20.3 0.2 multiply_reduce_fusion.1
  20.4 4.1 %all-to-all-done.pos = f32[16,2,24,128]{3,2,1,0:T(8,128)S(1)} async-done(((f32[16,2,24,128]{3,2,1,0:T(8,128)}), f32[16,2,24,128]{3,2,1,0:T(8,128)S(1)}, u32[]{:S(2)}, u32[]{:S(2)}) %all-to-all-start) | async-done | bytes 393248 | tf_op jit(solution)/shard_map/all_to_all | solution.py:519
  24.5 0.1 broadcast_in_dim.19.table
  24.7 10.6 %pair_step.1 = (f32[16,2,24,128]{3,2,1,0:T(8,128)}, f32[2,8,128]{2,1,0:T(8,128)S(1)}) custom-call(f32[16,2,24,128]{3,2,1,0:T(8,128)S(1)} %all-to-all-done.pos), custom_call_target="tpu_custom_call" | custom-call | flops 67108864 | bytes 1048576 | tf_op jit(solution)/shard_map/pair_step/pallas_call | solution.py:280
  35.4 3.8 %all-to-all-start.1 = ((f32[16,2,24,128]{3,2,1,0:T(8,128)}), f32[16,2,24,128]{3,2,1,0:T(8,128)S(1)}, u32[]{:S(2)}, u32[]{:S(2)}) async-start(f32[16,2,24,128]{3,2,1,0:T(8,128)} %get-tuple-element.23.grad), calls=%async_computation.1 | async-start | bytes 786432 | tf_op jit(solution)/shard_map/all_to_all | solution.py:562
  39.3 15.6 %orbital_step.1 = f32[16,16,128]{2,1,0:T(8,128)S(1)} custom-call(f32[16,2,24,128]{3,2,1,0:T(8,128)S(1)} %all-to-all-done.pos, f32[16,2,24,128]{3,2,1,0:T(8,128)} %get-tuple-element.23.grad, f32[2,8,128]{2,1,0:T(8,128)S(1)} %get-tuple-element.24.totals, f32[128,256]{1,0:T(8,128)S(1)} %copy.198.spread, bf16[72,384]{1,0:T(8,128)(2,1)S(1)} %pad_maximum_fusion.sums, ...), custom_call_target="tpu_custom_call" | custom-call | flops 268435456 | bytes 1048576 | tf_op jit(solution)/shard_map/orbital_step/pallas_call | solution.py:300
  54.9 15.2 %all_to_all.20.energies = f32[16,16,128]{2,1,0:T(8,128)S(1)} all-to-all(f32[16,16,128]{2,1,0:T(8,128)S(1)} %orbital_step.1), channel_id=1, replica_groups=mesh['gz'=2,'gx_0'=4,'gx_1'=4,'gy'=8] {'gz','gy'}, dimensions={0} | all-to-all | bytes 262144 | tf_op jit(solution)/shard_map/all_to_all | solution.py:565
  70.1 2.1 %pack_step.1 = (f32[16,104,128]{2,1,0:T(8,128)}, f32[4,4096]{1,0:T(4,128)}) custom-call(s32[64]{0:T(128)S(1)} %select_reduce_fusion.1.picked, f32[32,24,128]{2,1,0:T(8,128)S(1)} %bitcast.94, f32[16,16,128]{2,1,0:T(8,128)S(1)} %all_to_all.20.energies, f32[32,24,128]{2,1,0:T(8,128)S(1)} %own_step.1.base, f32[32,128]{1,0:T(8,128)S(1)} %bitcast_select_fusion.live), custom_call_target="tpu_custom_call" | custom-call | tf_op jit(solution)/shard_map/pack_step/pallas_call | solution.py:389
  72.2 7.0 %all-to-all-start.3 = ((f32[16,104,128]{2,1,0:T(8,128)}), f32[16,104,128]{2,1,0:T(8,128)S(1)}, u32[]{:S(2)}, u32[]{:S(2)}) async-start(f32[16,104,128]{2,1,0:T(8,128)} %get-tuple-element.34), calls=%async_computation.3 | async-start | bytes 1703936 | tf_op jit(solution)/shard_map/all_to_all | solution.py:567
  79.3 0.2 convert_reduce_fusion
  79.6 14.3 %all-to-all-done.3.received = f32[16,104,128]{2,1,0:T(8,128)S(1)} async-done(((f32[16,104,128]{2,1,0:T(8,128)}), f32[16,104,128]{2,1,0:T(8,128)S(1)}, u32[]{:S(2)}, u32[]{:S(2)}) %all-to-all-start.3) | async-done | bytes 852000 | tf_op jit(solution)/shard_map/all_to_all | solution.py:567
  93.9 1.6 %place_step.1 = (f32[3,8,4096]{2,1,0:T(8,128)}, f32[32,128]{1,0:T(8,128)}, f32[1,4]{1,0:T(1,128)}) custom-call(s32[32]{0:T(128)S(1)} %multiply_add_fusion.slots, s32[1]{0:T(128)} %bitcast.37.half, f32[16,104,128]{2,1,0:T(8,128)S(1)} %all-to-all-done.3.received), custom_call_target="tpu_custom_call" | custom-call | tf_op jit(solution)/shard_map/place_step/pallas_call | solution.py:425
  (96 shorter events, 3.8 us)
Async XLA Ops:
  2.4 22.1 %all-to-all-start = ((f32[16,2,24,128]{3,2,1,0:T(8,128)}), f32[16,2,24,128]{3,2,1,0:T(8,128)S(1)}, u32[]{:S(2)}, u32[]{:S(2)}) async-start(f32[16,2,24,128]{3,2,1,0:T(8,128)} %bitcast.2), calls=%async_computation | async-start | bytes 786432 | tf_op jit(solution)/shard_map/all_to_all | solution.py:519
  11.0 0.7 copy-start.3
  11.0 0.7 copy-start.6
  11.7 0.7 copy-start.4
  12.4 0.7 copy-start.8
  12.4 0.7 copy-start.9
  14.1 0.7 copy-start.5
  14.1 1.2 %copy-start.2 = (f32[4096]{0:T(1024)S(1)}, f32[4096]{0:T(1024)}, u32[]{:S(2)}) copy-start(f32[4096]{0:T(1024)} %param.17) | copy-start | bytes 49156
  14.1 1.2 %copy-start.7 = (s32[32]{0:T(128)S(1)}, s32[32]{0:T(128)}, u32[]{:S(2)}) copy-start(s32[32]{0:T(128)} %param.18) | copy-start | bytes 388
  14.4 3.2 %copy-start = (f32[8,3,4096]{2,0,1:T(8,128)S(1)}, f32[8,3,4096]{2,0,1:T(8,128)}, u32[]{:S(2)}) copy-start(f32[8,3,4096]{2,0,1:T(8,128)} %param.10) | copy-start | bytes 1179652
  14.4 3.2 %copy-start.1 = (f32[8,3,4096]{2,0,1:T(8,128)S(1)}, f32[8,3,4096]{2,0,1:T(8,128)}, u32[]{:S(2)}) copy-start(f32[8,3,4096]{2,0,1:T(8,128)} %param.11) | copy-start | bytes 1179652
  35.4 19.6 %all-to-all-start.1 = ((f32[16,2,24,128]{3,2,1,0:T(8,128)}), f32[16,2,24,128]{3,2,1,0:T(8,128)S(1)}, u32[]{:S(2)}, u32[]{:S(2)}) async-start(f32[16,2,24,128]{3,2,1,0:T(8,128)} %get-tuple-element.23.grad), calls=%async_computation.1 | async-start | bytes 786432 | tf_op jit(solution)/shard_map/all_to_all | solution.py:562
  72.2 21.7 %all-to-all-start.3 = ((f32[16,104,128]{2,1,0:T(8,128)}), f32[16,104,128]{2,1,0:T(8,128)S(1)}, u32[]{:S(2)}, u32[]{:S(2)}) async-start(f32[16,104,128]{2,1,0:T(8,128)} %get-tuple-element.34), calls=%async_computation.3 | async-start | bytes 1703936 | tf_op jit(solution)/shard_map/all_to_all | solution.py:567

commit v5 on v3

--- a/solution.py
+++ b/solution.py
@@ -144,18 +144,16 @@
 
 
 def walker_kernel(
-    pos, spread, sums, table, nuclear, live, out, rot, back, grad,
-    left, right, square0, square1, parts0, parts1, held0, held1,
+    pos, spread, table, nuclear, live, out,
+    rot, back, grad, left, right, square0, square1, reaches, firsts,
 ):
     totals = pair_part(pos, rot, back, grad)
     zero = jnp.zeros((8, BLK), jnp.float32)
-    one = jnp.ones((8, BLK), jnp.float32)
-    wide = jnp.zeros((16, BLK), jnp.float32)
 
     column = lax.broadcasted_iota(jnp.int32, (8 * NA, 2 * BLK), 1)
     for e in range(8):
         weights = jnp.where(column % 8 == e, spread[...], 0.0)
-        left[e * 128 : e * 128 + 128, :] = weights
+        left[e * 128 : e * 128 + 128, :] = weights.astype(jnp.bfloat16)
     for row in range(24, 32):
         right[row * 8 : row * 8 + 8, :] = jnp.full((8, 2 * BLK), 1.0 if row < 27 else 0.0)
 
@@ -173,82 +171,89 @@
 
     def squares(square, first, count):
         rows = slice(first * 128, (first + count) * 128)
-        square[rows, :] = jnp.dot(left[rows, :], right[...], preferred_element_type=jnp.float32)
-
-    def orbitals(square, parts, held, pots, first, count):
-        pots = list(pots)
-        pair = jnp.zeros((16, BLK), jnp.float32)
-        acc = {(e, h): [pair] * 2 for e in range(first, first + count) for h in range(2)}
-        for a in range(0, NA * 8, 16):
-            logs, phis, charge = (table[k, a : a + 16, :] for k in range(3))
+        factor = right[...].astype(jnp.bfloat16)
+        square[rows, :] = jnp.dot(left[rows, :], factor, preferred_element_type=jnp.float32)
+
+    def orbitals(p, square, carry, first):
+        energy, logs, pots = (list(part) for part in carry)
+        group = range(first, first + GROUP)
+        acc = {(e, h): [zero] * 7 for e in group for h in range(2)}
+        for a in range(NA):
+            level, share, soft, cx, cy, cz, charge = (table[k, a] for k in range(7))
             for h in range(2):
                 lanes = slice(h * BLK, h * BLK + BLK)
                 near = []
-                for e in range(first, first + count):
-                    sq = square[e * 128 + a : e * 128 + a + 16, lanes]
+                for e in group:
+                    at = (e * NA + a) * 8
+                    sq = square[at : at + 8, lanes]
                     inv = lax.rsqrt(sq)
-                    amp = jnp.exp2(logs - sq * inv)
+                    amp = jnp.exp2(level - sq * inv)
                     u = amp * inv
                     s = acc[e, h]
-                    acc[e, h] = [s[0] + amp * phis, s[1] + amp]
-                    parts[e, 256 + a : 272 + a, lanes] = (u * inv) * (inv + LN2)
+                    acc[e, h] = [
+                        s[0] + amp * share,
+                        s[1] + amp,
+                        s[2] + (u * inv) * ((inv + LN2) * soft),
+                        s[3] + u,
+                        s[4] + u * cx,
+                        s[5] + u * cy,
+                        s[6] + u * cz,
+                    ]
                     near.append(inv)
-                    high = u.astype(jnp.bfloat16).astype(jnp.float32)
-                    parts[e, a : a + 16, lanes] = high
-                    parts[e, 128 + a : 144 + a, lanes] = u - high
                 pots[h] = pots[h] + functools.reduce(jnp.add, near) * charge
-        for (e, h), s in acc.items():
-            for k in range(2):
-                held[e, h, k] = s[k][0:8, :] + s[k][8:16, :]
-        return tuple(pots)
-
-    def gather(p, parts, held, energy, logs, first, count):
-        energy, logs = list(energy), list(logs)
-        for e in range(first, first + count):
-            got = jnp.dot(sums[...], parts[e], preferred_element_type=jnp.float32)
+        for e in group:
             for h in range(2):
-                lanes = slice(h * BLK, h * BLK + BLK)
-                o = [got[k * 8 : k * 8 + 8, lanes] for k in range(9)]
-                us, u = o[0], [o[1] + o[2], o[3] + o[4], o[5] + o[6]]
-                phi, amps, soft = held[e, h, 0], held[e, h, 1], o[7] + o[8]
+                phi, amps, soft, us = acc[e, h][:4]
+                u = acc[e, h][4:]
                 ratio = 1.0 / phi
                 at = [slice(c * 8 + e, c * 8 + e + 1) for c in range(3)]
-                x = [jnp.broadcast_to(pos[p, h, at[c], :], (8, BLK)) for c in range(3)]
                 j = [jnp.broadcast_to(grad[p, h, at[c], :], (8, BLK)) for c in range(3)]
-                g = [(u[c] - x[c] * us) * ratio for c in range(3)]
-                lap = (LN2 * amps - 2.0 * us - soft) * ratio
-                dot = g[0] * j[0] + g[1] * j[1] + g[2] * j[2]
-                energy[h] = energy[h] - (0.5 * lap + dot)
+                reach = jnp.broadcast_to(reaches[p, h, e : e + 1, :], (8, BLK))
+                part = (0.5 * LN2) * amps - soft - us * reach
+                part = part + (u[0] * j[0] + u[1] * j[1] + u[2] * j[2])
+                energy[h] = energy[h] - part * ratio
                 logs[h] = logs[h] + jnp.log2(phi)
-                for c in range(3):
-                    out[p, h, at[c], :] = (g[c] + j[c])[0:1, :]
-        return tuple(energy), tuple(logs)
-
-    parts1[...] = jnp.zeros_like(parts1)
-    for e in range(8):
-        for h in range(2):
-            held1[e, h, 0], held1[e, h, 1] = one, zero
+                for k, value in enumerate((*u, us, ratio)):
+                    firsts[h, k, e : e + 1, :] = value[0:1, :]
+        return tuple(energy), tuple(logs), tuple(pots)
+
+    def reaching(p, _):
+        for h in range(2):
+            dots = [
+                pos[p, h, c * 8 : c * 8 + 8, :] * grad[p, h, c * 8 : c * 8 + 8, :] for c in range(3)
+            ]
+            reaches[p, h] = (1.0 + dots[0]) + (dots[1] + dots[2])
+        return 0
+
+    lax.fori_loop(0, EB, reaching, 0)
+
+    def drift(p):
+        for h in range(2):
+            for c in range(3):
+                rows = slice(c * 8, c * 8 + 8)
+                own = (firsts[h, c] - pos[p, h, rows, :] * firsts[h, 3]) * firsts[h, 4]
+                out[p, h, rows, :] = own + grad[p, h, rows, :]
+
     features(0)
     squares(square0, 0, 8)
 
-    def one_block(p, now, later, parts, held, before, kept, carry):
-        energy, logs, pots = carry
+    def one_block(p, now, later, carry):
         features(jnp.minimum(p + 1, EB - 1))
         for first in range(0, 8, GROUP):
             squares(later, first, GROUP)
-            pots = orbitals(now, parts, held, pots, first, GROUP)
-            energy, logs = gather(jnp.maximum(p - 1, 0), before, kept, energy, logs, first, GROUP)
-        return energy, logs, pots
-
-    def two_blocks(t, carry):
-        carry = one_block(2 * t, square0, square1, parts0, held0, parts1, held1, carry)
-        return one_block(2 * t + 1, square1, square0, parts1, held1, parts0, held0, carry)
+            carry = orbitals(p, now, carry, first)
+        drift(p)
+        return carry
+
+    def some_blocks(t, carry):
+        for k in range(0, 4, 2):
+            carry = one_block(4 * t + k, square0, square1, carry)
+            carry = one_block(4 * t + k + 1, square1, square0, carry)
+        return carry
 
     energy, logs, pots = lax.fori_loop(
-        0, EB // 2, two_blocks, ((zero, zero), (zero, zero), (wide, wide))
+        0, EB // 4, some_blocks, ((zero, zero), (zero, zero), (zero, zero))
     )
-    pots = [q[0:8, :] + q[8:16, :] for q in pots]
-    energy, logs = gather(EB - 1, parts1, held1, energy, logs, 0, 8)
     row = lax.broadcasted_iota(jnp.int32, (8, BLK), 0)
     lane = lax.broadcasted_iota(jnp.int32, (8, BLK), 1)
     numerator = jnp.zeros((8, 1), jnp.float32)
@@ -272,30 +277,28 @@
                 out[half * 8 + q, h, 24:32, :] = tile
 
 
-def walker_step(whole, spread, sums, table, nuclear, live):
+def walker_step(whole, spread, table, nuclear, live):
     vmem = pl.BlockSpec(memory_space=pltpu.VMEM)
     rows, width = 8 * NA * 8, 2 * BLK
     return pl.pallas_call(
         walker_kernel,
         out_shape=jax.ShapeDtypeStruct((EB, 2, 32, BLK), jnp.float32),
-        in_specs=[vmem] * 6,
+        in_specs=[vmem] * 5,
         out_specs=vmem,
         scratch_shapes=[
             pltpu.VMEM((EB, 2, 8, 24, BLK), jnp.float32),
             pltpu.VMEM((EB, 2, 8, 24, BLK), jnp.float32),
             pltpu.VMEM((EB, 2, 24, BLK), jnp.float32),
-            pltpu.VMEM((rows, width), jnp.float32),
+            pltpu.VMEM((rows, width), jnp.bfloat16),
             pltpu.VMEM((width, width), jnp.float32),
             pltpu.VMEM((rows, width), jnp.float32),
             pltpu.VMEM((rows, width), jnp.float32),
-            pltpu.VMEM((8, 3 * 8 * NA, width), jnp.float32),
-            pltpu.VMEM((8, 3 * 8 * NA, width), jnp.float32),
-            pltpu.VMEM((8, 2, 2, 8, BLK), jnp.float32),
-            pltpu.VMEM((8, 2, 2, 8, BLK), jnp.float32),
+            pltpu.VMEM((EB, 2, 8, BLK), jnp.float32),
+            pltpu.VMEM((2, 5, 8, BLK), jnp.float32),
         ],
         compiler_params=pltpu.CompilerParams(vmem_limit_bytes=24 * 1024 * 1024),
         name="walker_step",
-    )(whole, spread, sums, table, nuclear, live)
+    )(whole, spread, table, nuclear, live)
 
 
 def pack_kernel(picked, returned, base, live, send, energy):
@@ -404,29 +407,17 @@
     spread = jnp.stack(rows, axis=-1).reshape(NA * NG, len(rows), 1)
     spread = jnp.broadcast_to(spread, (NA * NG, len(rows), 8)).reshape(NA * NG, 2 * BLK)
 
-    def halves(x):
-        high = lax.reduce_precision(x, 8, 7)
-        return [high, x - high]
-
-    none = [0.0 * ones]
-    weights = [ones] + sum((halves(c[:, :, d]) for d in range(3)), []) + 2 * none
-    softs = 7 * none + halves(SOFT * k2 * ones)
-    same = jnp.eye(NG, dtype=jnp.float32)
-
-    def matrix(rows):
-        full = jnp.stack(rows)[:, None, :, :] * same[None, :, None, :]
-        return full.reshape(len(rows) * NG, NA * NG)
-
-    sums = jnp.concatenate([matrix(weights), matrix(weights), matrix(softs)], axis=1)
-
     factors = [
-        jnp.log2(coefficients * scale[:, 0]),
-        1.0 / scale[:, 0],
-        charges * k[:, 0],
+        jnp.log2(coefficients[:, None] * scale) * ones,
+        ones / scale,
+        (0.5 * SOFT) * k2 * ones,
+        c[:, :, 0],
+        c[:, :, 1],
+        c[:, :, 2],
+        (charges[:, None] * k) * ones,
     ]
-    factors = jnp.stack(factors)[:, :, None, None]
-    factors = jnp.broadcast_to(factors, (3, NA, NG, BLK)).reshape(3, NA * NG, BLK)
-    return spread, sums, factors
+    table = jnp.broadcast_to(jnp.stack(factors)[..., None], (len(factors), NA, NG, BLK))
+    return spread, table
 
 
 def by_blocks(x):
@@ -457,7 +448,7 @@
 
     base = sent + STEP_ROOT * by_blocks(diffusion_noise)
     centers = base_nuclei[None, :, :] + displacements
-    spread, sums, table = nucleus_tables(centers, charges, orbital_decay, coefficients)
+    spread, table = nucleus_tables(centers, charges, orbital_decay, coefficients)
     nuclear = jnp.broadcast_to(nuclear_repulsion(centers, charges)[:, None], (NG, BLK))
     live = jnp.where(
         jnp.arange(BLK, dtype=jnp.int32)[None, :] < counts[:, None],
@@ -488,7 +479,7 @@
     ).astype(jnp.int32)
     slots = source_device * CAP + jnp.sum(before, axis=1)
 
-    out = walker_step(whole, spread, sums, table, nuclear, own_live)
+    out = walker_step(whole, spread, table, nuclear, own_live)
     returned = lax.all_to_all(out, GZY, 0, 0, tiled=True).reshape(blocks_here, 32, BLK)
     send, local_energy = pack_step(picked, returned, base, live, peers)
     received = lax.all_to_all(send, GX, 0, 0, tiled=True)

time: 96.9 us -> 95.7 us (0.988)
  Pallas kernels: 30.3 us -> 28.8 us
  waiting for transfers between devices: 36.5 us -> 37.8 us
  local copies, waits for them, and re-layouts: 7.57 us -> 6.48 us
    pallas_call x1, Pallas kernels: 26.8 us -> 25.3 us  [walker_step(): pl.pallas_call(walker_kernel, out_shape=jax.ShapeDtypeStruct((EB, 2, 32,...]
    all_to_all x1, waiting for transfers between devices: 7 us -> 8.39 us  [local(): whole = lax.all_to_all(sent.reshape(EB, 2, 24, BLK), GZY, 0, 0, tiled=True)]
    unnamed x31 -> x26, local copies, waits for them, and re-layouts: 2.11 us -> 2.07 us
  transfers between devices with their start and end apart: 3 -> 3, of which waited for: 3 -> 3; matrix products, arithmetic and copies ran while one was open for 5% -> 4% of each run, Pallas kernels for 0% -> 0%
where the time goes in v5:
time: 95.7 us; the launch traced here: 95.1 us
  waiting for transfers between devices  37.8 us (39%)
  Pallas kernels  28.8 us (30%)
  starting transfers between devices  19.7 us (21%)
  local copies, waits for them, and re-layouts  6.48 us (7%)
  other arithmetic  1.37 us (1%)
    pallas_call x1, Pallas kernels, walker_step(): pl.pallas_call(walker_kernel, out_shape=jax.ShapeDtypeStruct((EB, 2, 32,...  25.3 us
    all_to_all x1, waiting for transfers between devices, local(): lax.all_to_all(out, GZY, 0, 0, tiled=True).reshape(blocks_here, 32, BLK)  15.7 us
    all_to_all x1, waiting for transfers between devices, local(): received = lax.all_to_all(send, GX, 0, 0, tiled=True)  13.7 us
    all_to_all x1, starting transfers between devices, local(): whole = lax.all_to_all(sent.reshape(EB, 2, 24, BLK), GZY, 0, 0, tiled=True)  8.72 us
    all_to_all x1, waiting for transfers between devices, local(): whole = lax.all_to_all(sent.reshape(EB, 2, 24, BLK), GZY, 0, 0, tiled=True)  8.39 us
    all_to_all x1, starting transfers between devices, local(): received = lax.all_to_all(send, GX, 0, 0, tiled=True)  7.03 us
    all_to_all x1, starting transfers between devices, local(): lax.all_to_all(out, GZY, 0, 0, tiled=True).reshape(blocks_here, 32, BLK)  3.98 us
    unnamed x26, local copies, waits for them, and re-layouts  2.07 us
  transfers between devices with their start and end apart: 3, of which 3 were waited for; matrix products, arithmetic and copies ran while one was open for 4% of the time, Pallas kernels for 0%

profile of v5, /device:TPU:32, one launch (start us, length us, event | category | flops | bytes accessed | tf_op | source)
XLA Modules:
  0.0 95.1 jit_solution(13286743639134391096)
XLA Ops:
  0.6 1.8 %copy.140 = f32[8,3,32,128]{3,0,1,2:T(8,128)} copy(f32[8,3,32,128]{3,0,2,1:T(8,128)} %bitcast.71) | data formatting | bytes 786432 | tf_op jit(solution)/shard_map/reshape | solution.py:425
  2.4 8.7 %all-to-all-start = ((f32[16,2,24,128]{3,2,1,0:T(8,128)}), f32[16,2,24,128]{3,2,1,0:T(8,128)S(1)}, u32[]{:S(2)}, u32[]{:S(2)}) async-start(f32[16,2,24,128]{3,2,1,0:T(8,128)} %bitcast.2), calls=%async_computation | async-start | bytes 786432 | tf_op jit(solution)/shard_map/all_to_all | solution.py:447
  11.2 0.7 copy-done.3
  11.8 0.6 copy-done.4
  12.8 0.1 stack.85
  12.9 0.1 stack.86
  14.4 0.1 stack.90
  14.6 0.1 stack.92
  14.9 0.7 copy-done.2
  15.7 0.1 copy.181.spread
  15.9 0.1 multiply_reduce_fusion
  16.1 0.2 multiply_reduce_fusion.1
  16.3 8.4 %all-to-all-done.pos = f32[16,2,24,128]{3,2,1,0:T(8,128)S(1)} async-done(((f32[16,2,24,128]{3,2,1,0:T(8,128)}), f32[16,2,24,128]{3,2,1,0:T(8,128)S(1)}, u32[]{:S(2)}, u32[]{:S(2)}) %all-to-all-start) | async-done | bytes 393248 | tf_op jit(solution)/shard_map/all_to_all | solution.py:447
  24.7 0.2 broadcast_in_dim.16.table
  24.9 25.3 %walker_step.1 = f32[16,2,32,128]{3,2,1,0:T(8,128)} custom-call(f32[16,2,24,128]{3,2,1,0:T(8,128)S(1)} %all-to-all-done.pos, f32[128,256]{1,0:T(8,128)S(1)} %copy.181.spread, f32[7,16,8,128]{3,2,1,0:T(8,128)S(1)} %broadcast_in_dim.16.table, f32[8,128]{1,0:T(8,128)S(1)} %broadcast_in_dim.17.nuclear, f32[2,128]{1,0:T(2,128)S(1)} %constant_dynamic-slice_fusion.live), custom_call_target="tpu_custom_call" | custom-call | tf_op jit(solution)/shard_map/walker_step/pallas_call | solution.py:283
  50.3 4.0 %all-to-all-start.1 = ((f32[16,2,32,128]{3,2,1,0:T(8,128)}), f32[16,2,32,128]{3,2,1,0:T(8,128)S(1)}, u32[]{:S(2)}, u32[]{:S(2)}) async-start(f32[16,2,32,128]{3,2,1,0:T(8,128)} %walker_step.1), calls=%async_computation.1 | async-start | bytes 1048576 | tf_op jit(solution)/shard_map/all_to_all | solution.py:483
  54.3 0.2 select_reduce_fusion
  54.5 0.2 convert_reduce_fusion.1
  54.8 15.7 %all-to-all-done.1 = f32[16,2,32,128]{3,2,1,0:T(8,128)S(1)} async-done(((f32[16,2,32,128]{3,2,1,0:T(8,128)}), f32[16,2,32,128]{3,2,1,0:T(8,128)S(1)}, u32[]{:S(2)}, u32[]{:S(2)}) %all-to-all-start.1) | async-done | bytes 524320 | tf_op jit(solution)/shard_map/all_to_all | solution.py:483
  70.6 1.8 %pack_step.1 = (f32[16,104,128]{2,1,0:T(8,128)}, f32[4,4096]{1,0:T(4,128)}) custom-call(s32[64]{0:T(128)S(1)} %select_reduce_fusion.1.picked, f32[32,32,128]{2,1,0:T(8,128)S(1)} %bitcast.70, f32[32,24,128]{2,1,0:T(8,128)S(1)} %fusion.base, f32[32,128]{1,0:T(8,128)S(1)} %bitcast_select_fusion.live), custom_call_target="tpu_custom_call" | custom-call | tf_op jit(solution)/shard_map/pack_step/pallas_call | solution.py:330
  72.4 7.0 %all-to-all-start.2 = ((f32[16,104,128]{2,1,0:T(8,128)}), f32[16,104,128]{2,1,0:T(8,128)S(1)}, u32[]{:S(2)}, u32[]{:S(2)}) async-start(f32[16,104,128]{2,1,0:T(8,128)} %get-tuple-element.10), calls=%async_computation.2 | async-start | bytes 1703936 | tf_op jit(solution)/shard_map/all_to_all | solution.py:485
  79.5 0.2 convert_reduce_fusion
  79.8 13.7 %all-to-all-done.2.received = f32[16,104,128]{2,1,0:T(8,128)S(1)} async-done(((f32[16,104,128]{2,1,0:T(8,128)}), f32[16,104,128]{2,1,0:T(8,128)S(1)}, u32[]{:S(2)}, u32[]{:S(2)}) %all-to-all-start.2) | async-done | bytes 852000 | tf_op jit(solution)/shard_map/all_to_all | solution.py:485
  93.5 1.6 %place_step.1 = (f32[3,8,4096]{2,1,0:T(8,128)}, f32[32,128]{1,0:T(8,128)}, f32[1,4]{1,0:T(1,128)}) custom-call(s32[32]{0:T(128)S(1)} %multiply_add_fusion.slots, s32[1]{0:T(128)} %bitcast.29.half, f32[16,104,128]{2,1,0:T(8,128)S(1)} %all-to-all-done.2.received), custom_call_target="tpu_custom_call" | custom-call | tf_op jit(solution)/shard_map/place_step/pallas_call | solution.py:366
  (70 shorter events, 2.6 us)
Async XLA Ops:
  2.4 8.7 %copy-start.6 = (f32[16,3]{0,1:T(4,128)S(1)}, f32[16,3]{0,1:T(4,128)}, u32[]{:S(2)}) copy-start(f32[16,3]{0,1:T(4,128)} %param.12) | copy-start | bytes 580
  2.4 22.3 %all-to-all-start = ((f32[16,2,24,128]{3,2,1,0:T(8,128)}), f32[16,2,24,128]{3,2,1,0:T(8,128)S(1)}, u32[]{:S(2)}, u32[]{:S(2)}) async-start(f32[16,2,24,128]{3,2,1,0:T(8,128)} %bitcast.2), calls=%async_computation | async-start | bytes 786432 | tf_op jit(solution)/shard_map/all_to_all | solution.py:447
  11.1 0.7 copy-start.3
  11.8 0.7 copy-start.4
  11.8 0.7 copy-start.8
  11.8 0.7 copy-start.9
  14.9 0.7 copy-start.2
  14.9 0.7 copy-start.7
  50.3 4.0 %copy-start.5 = (s32[512]{0:T(512)S(1)}, s32[512]{0:T(512)}, u32[]{:S(2)}) copy-start(s32[512]{0:T(512)} %param.19) | copy-start | bytes 6148
  50.3 4.5 %copy-start = (f32[8,3,4096]{2,0,1:T(8,128)S(1)}, f32[8,3,4096]{2,0,1:T(8,128)}, u32[]{:S(2)}) copy-start(f32[8,3,4096]{2,0,1:T(8,128)} %param.10) | copy-start | bytes 1179652
  50.3 4.5 %copy-start.1 = (f32[8,3,4096]{2,0,1:T(8,128)S(1)}, f32[8,3,4096]{2,0,1:T(8,128)}, u32[]{:S(2)}) copy-start(f32[8,3,4096]{2,0,1:T(8,128)} %param.11) | copy-start | bytes 1179652
  50.3 20.3 %all-to-all-start.1 = ((f32[16,2,32,128]{3,2,1,0:T(8,128)}), f32[16,2,32,128]{3,2,1,0:T(8,128)S(1)}, u32[]{:S(2)}, u32[]{:S(2)}) async-start(f32[16,2,32,128]{3,2,1,0:T(8,128)} %walker_step.1), calls=%async_computation.1 | async-start | bytes 1048576 | tf_op jit(solution)/shard_map/all_to_all | solution.py:483
  72.4 21.1 %all-to-all-start.2 = ((f32[16,104,128]{2,1,0:T(8,128)}), f32[16,104,128]{2,1,0:T(8,128)S(1)}, u32[]{:S(2)}, u32[]{:S(2)}) async-start(f32[16,104,128]{2,1,0:T(8,128)} %get-tuple-element.10), calls=%async_computation.2 | async-start | bytes 1703936 | tf_op jit(solution)/shard_map/all_to_all | solution.py:485

commit v6 on v5

--- a/solution.py
+++ b/solution.py
@@ -39,10 +39,8 @@
         for h in range(2):
             for c in range(3):
                 x = pos[p, h, c * 8 : c * 8 + 8, :]
-                grad[p, h, c * 8 : c * 8 + 8, :] = zero
-                for s in range(8):
-                    rot[p, h, s, c * 8 : c * 8 + 8, :] = roll8(x, -s)
-                    back[p, h, s, c * 8 : c * 8 + 8, :] = zero
+                for s in range(1, 8):
+                    rot[p, h, s - 1, c * 8 : c * 8 + 8, :] = roll8(x, -s)
         return 0
 
     lax.fori_loop(0, EB, prepare, 0)
@@ -66,30 +64,39 @@
         for c in range(3):
             ref[(*at, slice(c * 8, c * 8 + 8), slice(None))] = values[c]
 
-    def block_pair(i, j, h, xi, gi, sums):
+    def turned(j, h, s):
+        return load3(pos, j, h) if s == 0 else load3(rot, j, h, s - 1)
+
+    def block_pair(i, j, h, xi, gi, sums, fresh=()):
         for s in range(8):
-            f, sums = terms(xi, load3(rot, j, h, s), sums, False)
+            f, sums = terms(xi, turned(j, h, s), sums, False)
             gi = [gi[c] + f[c] for c in range(3)]
-            b = load3(back, j, h, s)
-            store3(back, [b[c] + f[c] for c in range(3)], j, h, s)
+            if s not in fresh:
+                b = load3(back, j, h, s)
+                f = [b[c] + f[c] for c in range(3)]
+            store3(back, f, j, h, s)
         return gi, sums
 
     def inside(t, sums):
         out = []
+        untouched = (0, 4, 5, 6, 7)
         for h in range(2):
             acc = sums[h]
+            own = []
             for i in (2 * t, 2 * t + 1):
-                xi, gi = load3(pos, i, h), load3(grad, i, h)
+                xi, gi = load3(pos, i, h), [zero] * 3
                 for s in range(1, 5):
-                    f, acc = terms(xi, load3(rot, i, h, s), acc, s == 4)
+                    f, acc = terms(xi, turned(i, h, s), acc, s == 4)
                     gi = [gi[c] + f[c] for c in range(3)]
                     if s < 4:
-                        b = load3(back, i, h, s)
-                        store3(back, [b[c] + f[c] for c in range(3)], i, h, s)
-                store3(grad, gi, i, h)
+                        store3(back, f, i, h, s)
+                own.append(gi)
             i, j = 2 * t, 2 * t + 1
-            gi, acc = block_pair(i, j, h, load3(pos, i, h), load3(grad, i, h), acc)
+            for s in untouched:
+                store3(back, [zero] * 3, i, h, s)
+            gi, acc = block_pair(i, j, h, load3(pos, i, h), own[0], acc, untouched)
             store3(grad, gi, i, h)
+            store3(grad, own[1], j, h)
             out.append(acc)
         return tuple(out)
 
@@ -143,11 +150,15 @@
     return high, middle, rest - middle
 
 
-def walker_kernel(
-    pos, spread, table, nuclear, live, out,
-    rot, back, grad, left, right, square0, square1, reaches, firsts,
+def pair_kernel(pos, grad, totals, rot, back):
+    for h, total in enumerate(pair_part(pos, rot, back, grad)):
+        totals[h] = total
+
+
+def orbital_kernel(
+    pos, grad, totals, spread, table, nuclear, live, out,
+    left, right, square0, square1, reaches,
 ):
-    totals = pair_part(pos, rot, back, grad)
     zero = jnp.zeros((8, BLK), jnp.float32)
 
     column = lax.broadcasted_iota(jnp.int32, (8 * NA, 2 * BLK), 1)
@@ -213,8 +224,6 @@
                 part = part + (u[0] * j[0] + u[1] * j[1] + u[2] * j[2])
                 energy[h] = energy[h] - part * ratio
                 logs[h] = logs[h] + jnp.log2(phi)
-                for k, value in enumerate((*u, us, ratio)):
-                    firsts[h, k, e : e + 1, :] = value[0:1, :]
         return tuple(energy), tuple(logs), tuple(pots)
 
     def reaching(p, _):
@@ -227,13 +236,6 @@
 
     lax.fori_loop(0, EB, reaching, 0)
 
-    def drift(p):
-        for h in range(2):
-            for c in range(3):
-                rows = slice(c * 8, c * 8 + 8)
-                own = (firsts[h, c] - pos[p, h, rows, :] * firsts[h, 3]) * firsts[h, 4]
-                out[p, h, rows, :] = own + grad[p, h, rows, :]
-
     features(0)
     squares(square0, 0, 8)
 
@@ -242,7 +244,6 @@
         for first in range(0, 8, GROUP):
             squares(later, first, GROUP)
             carry = orbitals(p, now, carry, first)
-        drift(p)
         return carry
 
     def some_blocks(t, carry):
@@ -268,46 +269,99 @@
         local.append(e)
     placed = jnp.where(lane == row, numerator, 0.0) + jnp.where(lane == row + 8, denominator, 0.0)
     placed = jnp.broadcast_to(jnp.sum(placed, axis=0, keepdims=True), (8, BLK))
-    for h in range(2):
-        first = jnp.broadcast_to(local[h][0:1, :], (8, BLK))
-        for half in range(2):
-            e = local[h] if half == 0 else roll8(local[h], 4)
-            tile = jnp.where(row < 4, e, jnp.where(row == 4, first, placed))
-            for q in range(8):
-                out[half * 8 + q, h, 24:32, :] = tile
-
-
-def walker_step(whole, spread, table, nuclear, live):
+    firsts = [jnp.broadcast_to(local[h][0:1, :], (8, BLK)) for h in range(2)]
+    rest = jnp.where(row == 0, firsts[0], jnp.where(row == 1, firsts[1], placed))
+    for q in range(EB):
+        low, high = local if q < EB // 2 else (roll8(local[0], 4), roll8(local[1], 4))
+        out[q, 0:8, :] = jnp.where(row < 4, low, roll8(high, 4))
+        out[q, 8:16, :] = rest
+
+
+def pair_step(whole):
+    vmem = pl.BlockSpec(memory_space=pltpu.VMEM)
+    return pl.pallas_call(
+        pair_kernel,
+        out_shape=(
+            jax.ShapeDtypeStruct((EB, 2, 24, BLK), jnp.float32),
+            jax.ShapeDtypeStruct((2, 8, BLK), jnp.float32),
+        ),
+        in_specs=[vmem],
+        out_specs=(vmem, vmem),
+        scratch_shapes=[
+            pltpu.VMEM((EB, 2, 7, 24, BLK), jnp.float32),
+            pltpu.VMEM((EB, 2, 8, 24, BLK), jnp.float32),
+        ],
+        compiler_params=pltpu.CompilerParams(vmem_limit_bytes=16 * 1024 * 1024),
+        cost_estimate=pl.CostEstimate(
+            flops=EB * EB * BLK * 2 * 32 * 32, transcendentals=0, bytes_accessed=1 << 20
+        ),
+        name="pair_step",
+    )(whole)
+
+
+def orbital_step(whole, grad, totals, spread, table, nuclear, live):
     vmem = pl.BlockSpec(memory_space=pltpu.VMEM)
     rows, width = 8 * NA * 8, 2 * BLK
     return pl.pallas_call(
-        walker_kernel,
-        out_shape=jax.ShapeDtypeStruct((EB, 2, 32, BLK), jnp.float32),
-        in_specs=[vmem] * 5,
+        orbital_kernel,
+        out_shape=jax.ShapeDtypeStruct((EB, 16, BLK), jnp.float32),
+        in_specs=[vmem] * 7,
         out_specs=vmem,
         scratch_shapes=[
-            pltpu.VMEM((EB, 2, 8, 24, BLK), jnp.float32),
-            pltpu.VMEM((EB, 2, 8, 24, BLK), jnp.float32),
-            pltpu.VMEM((EB, 2, 24, BLK), jnp.float32),
             pltpu.VMEM((rows, width), jnp.bfloat16),
             pltpu.VMEM((width, width), jnp.float32),
             pltpu.VMEM((rows, width), jnp.float32),
             pltpu.VMEM((rows, width), jnp.float32),
             pltpu.VMEM((EB, 2, 8, BLK), jnp.float32),
-            pltpu.VMEM((2, 5, 8, BLK), jnp.float32),
         ],
-        compiler_params=pltpu.CompilerParams(vmem_limit_bytes=24 * 1024 * 1024),
-        name="walker_step",
-    )(whole, spread, table, nuclear, live)
-
-
-def pack_kernel(picked, returned, base, live, send, energy):
-    sums = returned[0, 29:30, :]
-    for p in range(1, EB):
-        sums = sums + returned[2 * p, 29:30, :]
-    for b in range(2 * EB):
-        energy[:, b * BLK : (b + 1) * BLK] = returned[b, 24:28, :]
-
+        compiler_params=pltpu.CompilerParams(vmem_limit_bytes=16 * 1024 * 1024),
+        cost_estimate=pl.CostEstimate(
+            flops=EB * 8 * NA * NG * BLK * 2 * 32 * 2, transcendentals=0, bytes_accessed=1 << 20
+        ),
+        name="orbital_step",
+    )(whole, grad, totals, spread, table, nuclear, live)
+
+
+def own_kernel(scalars, positions, noise, base):
+    wide = 4 * BLK
+
+    def four(t, _):
+        at = pl.multiple_of(t * wide, wide)
+        r = [positions[c, :, pl.ds(at, wide)] for c in range(3)]
+        phi = jnp.zeros((8, wide), jnp.float32)
+        grad = [phi, phi, phi]
+        for a in range(NA):
+            v = [r[c] - scalars[c, a] for c in range(3)]
+            square = (v[0] * v[0] + v[1] * v[1]) + (v[2] * v[2] + SOFT)
+            inv = lax.rsqrt(square)
+            amp = jnp.exp2(scalars[4, a] - scalars[3, a] * (square * inv))
+            u = amp * inv
+            phi = phi + amp * scalars[5, a]
+            grad = [grad[c] + u * v[c] for c in range(3)]
+        step = TIME_STEP / phi
+        for c in range(3):
+            moved = r[c] + STEP_ROOT * noise[c, :, pl.ds(at, wide)] - step * grad[c]
+            for k in range(4):
+                base[t * 4 + k, c * 8 : c * 8 + 8, :] = moved[:, k * BLK : (k + 1) * BLK]
+        return 0
+
+    lax.fori_loop(0, base.shape[0] // 4, four, 0)
+
+
+def own_step(scalars, positions, noise):
+    vmem = pl.BlockSpec(memory_space=pltpu.VMEM)
+    blocks = positions.shape[2] // BLK
+    return pl.pallas_call(
+        own_kernel,
+        out_shape=jax.ShapeDtypeStruct((blocks, 24, BLK), jnp.float32),
+        in_specs=[pl.BlockSpec(memory_space=pltpu.SMEM), vmem, vmem],
+        out_specs=vmem,
+        compiler_params=pltpu.CompilerParams(vmem_limit_bytes=8 * 1024 * 1024),
+        name="own_step",
+    )(scalars, positions, noise)
+
+
+def blocks_kernel(picked, returned, base, send):
     def one_peer(peer, _):
         for k in range(CAP):
             b = picked[peer * CAP + k]
@@ -315,29 +369,63 @@
                 send[peer, k * 24 + c * 8 : k * 24 + c * 8 + 8, :] = (
                     base[b, c * 8 : c * 8 + 8, :] + TIME_STEP * returned[b, c * 8 : c * 8 + 8, :]
                 )
-            alive = live[pl.ds(b, 1), :]
-            level = returned[b, 28:29, :] - jnp.log(alive)
-            send[peer, 96 + k : 97 + k, :] = jnp.where(alive > 0.0, level, 3.0e38)
-        send[peer, 100:101, :] = sums
-        send[peer, 101:104, :] = jnp.zeros((3, BLK), jnp.float32)
+        send[peer, 96:104, :] = jnp.zeros((8, BLK), jnp.float32)
         return 0
 
     lax.fori_loop(0, send.shape[0], one_peer, 0)
 
 
-def pack_step(picked, returned, base, live, peers):
+def blocks_step(picked, returned, base, peers):
     vmem = pl.BlockSpec(memory_space=pltpu.VMEM)
     return pl.pallas_call(
-        pack_kernel,
+        blocks_kernel,
+        out_shape=jax.ShapeDtypeStruct((peers, PEER_ROWS, BLK), jnp.float32),
+        in_specs=[pl.BlockSpec(memory_space=pltpu.SMEM)] + [vmem] * 2,
+        out_specs=vmem,
+        compiler_params=pltpu.CompilerParams(vmem_limit_bytes=8 * 1024 * 1024),
+        cost_estimate=pl.CostEstimate(flops=1 << 24, transcendentals=0, bytes_accessed=1 << 21),
+        name="blocks_step",
+    )(picked, returned, base)
+
+
+def levels_kernel(picked, energies, live, _, send, energy, tiles, done):
+    sums = energies[0, 10:11, :]
+    for p in range(1, EB):
+        sums = sums + energies[p, 10:11, :]
+    peers = tiles.shape[0]
+    for peer in range(peers):
+        for k in range(CAP):
+            b = picked[peer * CAP + k]
+            alive = live[pl.ds(b, 1), :]
+            level = energies[b // 2, pl.ds(8 + b % 2, 1), :] - jnp.log(alive)
+            tiles[peer, k : k + 1, :] = jnp.where(alive > 0.0, level, 3.0e38)
+        tiles[peer, 4:5, :] = sums
+        tiles[peer, 5:8, :] = jnp.zeros((3, BLK), jnp.float32)
+    copy = pltpu.make_async_copy(tiles, send.at[:, 96:104, :], done)
+    copy.start()
+    for b in range(2 * EB):
+        at = (b % 2) * 4
+        energy[:, b * BLK : (b + 1) * BLK] = energies[b // 2, at : at + 4, :]
+    copy.wait()
+
+
+def levels_step(picked, energies, live, send):
+    vmem = pl.BlockSpec(memory_space=pltpu.VMEM)
+    whole = pl.BlockSpec(memory_space=pl.ANY)
+    peers = send.shape[0]
+    return pl.pallas_call(
+        levels_kernel,
         out_shape=(
-            jax.ShapeDtypeStruct((peers, PEER_ROWS, BLK), jnp.float32),
+            jax.ShapeDtypeStruct(send.shape, jnp.float32),
             jax.ShapeDtypeStruct((NG // 2, 2 * EB * BLK), jnp.float32),
         ),
-        in_specs=[pl.BlockSpec(memory_space=pltpu.SMEM)] + [vmem] * 3,
-        out_specs=(vmem, vmem),
+        in_specs=[pl.BlockSpec(memory_space=pltpu.SMEM), vmem, vmem, whole],
+        out_specs=(whole, vmem),
+        scratch_shapes=[pltpu.VMEM((peers, 8, BLK), jnp.float32), pltpu.SemaphoreType.DMA],
+        input_output_aliases={3: 0},
         compiler_params=pltpu.CompilerParams(vmem_limit_bytes=8 * 1024 * 1024),
-        name="pack_step",
-    )(picked, returned, base, live)
+        name="levels_step",
+    )(picked, energies, live, send)
 
 
 def place_kernel(slots, half, received, moved, weights, estimate):
@@ -446,8 +534,12 @@
     sent = by_blocks(positions)
     whole = lax.all_to_all(sent.reshape(EB, 2, 24, BLK), GZY, 0, 0, tiled=True)
 
-    base = sent + STEP_ROOT * by_blocks(diffusion_noise)
     centers = base_nuclei[None, :, :] + displacements
+    first = centers[0]
+    rate = orbital_decay * LOG2E
+    level = jnp.log2(coefficients * orbital_decay)
+    scalars = jnp.stack([first[:, 0], first[:, 1], first[:, 2], rate, level, 1.0 / orbital_decay])
+    base = own_step(scalars, positions.transpose(1, 0, 2), diffusion_noise.transpose(1, 0, 2))
     spread, table = nucleus_tables(centers, charges, orbital_decay, coefficients)
     nuclear = jnp.broadcast_to(nuclear_repulsion(centers, charges)[:, None], (NG, BLK))
     live = jnp.where(
@@ -479,9 +571,16 @@
     ).astype(jnp.int32)
     slots = source_device * CAP + jnp.sum(before, axis=1)
 
-    out = walker_step(whole, spread, table, nuclear, own_live)
-    returned = lax.all_to_all(out, GZY, 0, 0, tiled=True).reshape(blocks_here, 32, BLK)
-    send, local_energy = pack_step(picked, returned, base, live, peers)
+    whole, base, spread, table, nuclear, own_live, picked = lax.optimization_barrier(
+        (whole, base, spread, table, nuclear, own_live, picked)
+    )
+    grad, totals = pair_step(whole)
+    returned = lax.all_to_all(grad, GZY, 0, 0, tiled=True).reshape(blocks_here, 24, BLK)
+    out = orbital_step(whole, grad, totals, spread, table, nuclear, own_live)
+    returned, out = lax.optimization_barrier((returned, out))
+    energies = lax.all_to_all(out, GZY, 0, 0, tiled=True)
+    send = blocks_step(picked, returned, base, peers)
+    send, local_energy = levels_step(picked, energies, live, send)
     received = lax.all_to_all(send, GX, 0, 0, tiled=True)
     moved, new_weights, estimate = place_step(slots, replica.reshape(1), received)
     return (local_energy, estimate.reshape(NG // 2), moved.transpose(1, 0, 2), new_weights.reshape(blocks_here * BLK))

time: 95.7 us -> 96.9 us (1.013)
  waiting for transfers between devices: 37.8 us -> 28.3 us
  starting transfers between devices: 19.7 us -> 26.8 us
  Pallas kernels: 28.8 us -> 34.4 us
  local copies, waits for them, and re-layouts: 6.48 us -> 4.51 us
    all_to_all x1 -> x2, waiting for transfers between devices: 15.7 us -> 6.5 us  [the longest x1 6.5 us: local(): energies = lax.all_to_all(out, GZY, 0, 0, tiled=True)]
    all_to_all x1 -> x2, starting transfers between devices: 3.98 us -> 11.1 us  [the longest x1 7.23 us: local(): energies = lax.all_to_all(out, GZY, 0, 0, tiled=True)]
    pallas_call x2 -> x5, Pallas kernels: 27.2 us -> 32.8 us  [the longest x1 16.1 us: orbital_step(): pl.pallas_call(orbital_kernel, out_shape=jax.ShapeDtypeStruct((EB, 16, BL...]
    unnamed x26 -> x27, local copies, waits for them, and re-layouts: 2.07 us -> 0.07 us
  transfers between devices with their start and end apart: 3 -> 4, of which waited for: 3 -> 3; matrix products, arithmetic and copies ran while one was open for 4% -> 4% of each run, Pallas kernels for 0% -> 21%
where the time goes in v6:
time: 96.9 us; the launch traced here: 96.3 us
  Pallas kernels  34.4 us (36%)
  waiting for transfers between devices  28.3 us (29%)
  starting transfers between devices  26.8 us (28%)
  local copies, waits for them, and re-layouts  4.51 us (5%)
  other arithmetic  1.31 us (1%)
  between operations  1.01 us (1%)
    pallas_call x1, Pallas kernels, orbital_step(): pl.pallas_call(orbital_kernel, out_shape=jax.ShapeDtypeStruct((EB, 16, BL...  16.1 us
    all_to_all x1, waiting for transfers between devices, local(): received = lax.all_to_all(send, GX, 0, 0, tiled=True)  14.3 us
    pallas_call x1, Pallas kernels, pair_step(): pl.pallas_call(pair_kernel, out_shape=(jax.ShapeDtypeStruct((EB, 2, 24, B...  10.3 us
    all_to_all x1, starting transfers between devices, local(): whole = lax.all_to_all(sent.reshape(EB, 2, 24, BLK), GZY, 0, 0, tiled=True)  8.73 us
    all_to_all x1, waiting for transfers between devices, local(): whole = lax.all_to_all(sent.reshape(EB, 2, 24, BLK), GZY, 0, 0, tiled=True)  7.48 us
    all_to_all x1, starting transfers between devices, local(): energies = lax.all_to_all(out, GZY, 0, 0, tiled=True)  7.23 us
    all_to_all x1, starting transfers between devices, local(): received = lax.all_to_all(send, GX, 0, 0, tiled=True)  7.04 us
    all_to_all x1, waiting for transfers between devices, local(): energies = lax.all_to_all(out, GZY, 0, 0, tiled=True)  6.5 us
  transfers between devices with their start and end apart: 4, of which 3 were waited for; matrix products, arithmetic and copies ran while one was open for 4% of the time, Pallas kernels for 21%

profile of v6, /device:TPU:32, one launch (start us, length us, event | category | flops | bytes accessed | tf_op | source)
XLA Modules:
  0.0 96.3 jit_solution(2342321134879226066)
XLA Ops:
  0.6 1.8 %copy.138 = f32[8,3,32,128]{3,0,1,2:T(8,128)} copy(f32[8,3,32,128]{3,0,2,1:T(8,128)} %bitcast.75) | data formatting | bytes 786432 | tf_op jit(solution)/shard_map/reshape | solution.py:513
  2.5 8.7 %all-to-all-start = ((f32[16,2,24,128]{3,2,1,0:T(8,128)}), f32[16,2,24,128]{3,2,1,0:T(8,128)S(1)}, u32[]{:S(2)}, u32[]{:S(2)}) async-start(f32[16,2,24,128]{3,2,1,0:T(8,128)} %bitcast.2), calls=%async_computation | async-start | bytes 786432 | tf_op jit(solution)/shard_map/all_to_all | solution.py:535
  11.3 0.2 select_reduce_fusion
  11.5 0.2 convert_reduce_fusion.1
  11.7 0.1 select_reduce_fusion.1.picked
  12.5 0.1 stack.106
  12.7 0.1 stack.108
  14.4 2.4 %own_step.1.base = f32[32,24,128]{2,1,0:T(8,128)S(1)} custom-call(f32[6,16]{1,0:T(8,128)S(1)} %stack.93.scalars, f32[3,8,4096]{2,1,0:T(8,128)S(1)} %bitcast.76, f32[3,8,4096]{2,1,0:T(8,128)S(1)} %bitcast.78), custom_call_target="tpu_custom_call" | custom-call | tf_op jit(solution)/shard_map/own_step/pallas_call | solution.py:354
  17.0 0.1 multiply_reduce_fusion
  17.1 0.2 multiply_reduce_fusion.1
  17.3 7.5 %all-to-all-done.pos = f32[16,2,24,128]{3,2,1,0:T(8,128)S(1)} async-done(((f32[16,2,24,128]{3,2,1,0:T(8,128)}), f32[16,2,24,128]{3,2,1,0:T(8,128)S(1)}, u32[]{:S(2)}, u32[]{:S(2)}) %all-to-all-start) | async-done | bytes 393248 | tf_op jit(solution)/shard_map/all_to_all | solution.py:535
  24.8 0.2 broadcast_in_dim.13.table
  25.0 10.3 %pair_step.1 = (f32[16,2,24,128]{3,2,1,0:T(8,128)}, f32[2,8,128]{2,1,0:T(8,128)S(1)}) custom-call(f32[16,2,24,128]{3,2,1,0:T(8,128)S(1)} %all-to-all-done.pos), custom_call_target="tpu_custom_call" | custom-call | flops 67108864 | bytes 1048576 | tf_op jit(solution)/shard_map/pair_step/pallas_call | solution.py:282
  35.3 3.8 %all-to-all-start.1 = ((f32[16,2,24,128]{3,2,1,0:T(8,128)}), f32[16,2,24,128]{3,2,1,0:T(8,128)S(1)}, u32[]{:S(2)}, u32[]{:S(2)}) async-start(f32[16,2,24,128]{3,2,1,0:T(8,128)} %get-tuple-element.22.grad), calls=%async_computation.1 | async-start | bytes 786432 | tf_op jit(solution)/shard_map/all_to_all | solution.py:578
  39.2 0.1 copy.179.spread
  39.3 16.1 %orbital_step.1 = f32[16,16,128]{2,1,0:T(8,128)} custom-call(f32[16,2,24,128]{3,2,1,0:T(8,128)S(1)} %all-to-all-done.pos, f32[16,2,24,128]{3,2,1,0:T(8,128)} %get-tuple-element.22.grad, f32[2,8,128]{2,1,0:T(8,128)S(1)} %get-tuple-element.23.totals, f32[128,256]{1,0:T(8,128)S(1)} %copy.179.spread, f32[7,16,8,128]{3,2,1,0:T(8,128)S(1)} %broadcast_in_dim.13.table, ...), custom_call_target="tpu_custom_call" | custom-call | flops 268435456 | bytes 1048576 | tf_op jit(solution)/shard_map/orbital_step/pallas_call | solution.py:305
  55.3 7.2 %all-to-all-start.2 = ((f32[16,16,128]{2,1,0:T(8,128)}), f32[16,16,128]{2,1,0:T(8,128)S(1)}, u32[]{:S(2)}, u32[]{:S(2)}) async-start(f32[16,16,128]{2,1,0:T(8,128)} %orbital_step.1), calls=%async_computation.2 | async-start | bytes 262144 | tf_op jit(solution)/shard_map/all_to_all | solution.py:581
  62.6 1.7 %blocks_step.1._ = f32[16,104,128]{2,1,0:T(8,128)} custom-call(s32[64]{0:T(128)S(1)} %select_reduce_fusion.1.picked, f32[32,24,128]{2,1,0:T(8,128)S(1)} %bitcast.77, f32[32,24,128]{2,1,0:T(8,128)S(1)} %own_step.1.base), custom_call_target="tpu_custom_call" | custom-call | flops 16777216 | bytes 2097152 | tf_op jit(solution)/shard_map/blocks_step/pallas_call | solution.py:380
  64.3 6.5 %all-to-all-done.2.energies = f32[16,16,128]{2,1,0:T(8,128)S(1)} async-done(((f32[16,16,128]{2,1,0:T(8,128)}), f32[16,16,128]{2,1,0:T(8,128)S(1)}, u32[]{:S(2)}, u32[]{:S(2)}) %all-to-all-start.2) | async-done | bytes 131104 | tf_op jit(solution)/shard_map/all_to_all | solution.py:581
  70.8 2.2 %levels_step.1 = (f32[16,104,128]{2,1,0:T(8,128)}, f32[4,4096]{1,0:T(4,128)}) custom-call(s32[64]{0:T(128)S(1)} %select_reduce_fusion.1.picked, f32[16,16,128]{2,1,0:T(8,128)S(1)} %all-to-all-done.2.energies, f32[32,128]{1,0:T(8,128)S(1)} %bitcast_select_fusion.live, f32[16,104,128]{2,1,0:T(8,128)} %blocks_step.1._), custom_call_target="tpu_custom_call", output_to_operand_aliasing={{0}: (3, {})} | custom-call | tf_op jit(solution)/shard_map/levels_step/pallas_call | solution.py:416
  73.0 7.0 %all-to-all-start.3 = ((f32[16,104,128]{2,1,0:T(8,128)}), f32[16,104,128]{2,1,0:T(8,128)S(1)}, u32[]{:S(2)}, u32[]{:S(2)}) async-start(f32[16,104,128]{2,1,0:T(8,128)} %get-tuple-element.32), calls=%async_computation.3 | async-start | bytes 1703936 | tf_op jit(solution)/shard_map/all_to_all | solution.py:584
  80.1 0.2 convert_reduce_fusion
  80.4 14.3 %all-to-all-done.3.received = f32[16,104,128]{2,1,0:T(8,128)S(1)} async-done(((f32[16,104,128]{2,1,0:T(8,128)}), f32[16,104,128]{2,1,0:T(8,128)S(1)}, u32[]{:S(2)}, u32[]{:S(2)}) %all-to-all-start.3) | async-done | bytes 852000 | tf_op jit(solution)/shard_map/all_to_all | solution.py:584
  94.7 1.6 %place_step.1 = (f32[3,8,4096]{2,1,0:T(8,128)}, f32[32,128]{1,0:T(8,128)}, f32[1,4]{1,0:T(1,128)}) custom-call(s32[32]{0:T(128)S(1)} %multiply_add_fusion.slots, s32[1]{0:T(128)} %bitcast.34.half, f32[16,104,128]{2,1,0:T(8,128)S(1)} %all-to-all-done.3.received), custom_call_target="tpu_custom_call" | custom-call | tf_op jit(solution)/shard_map/place_step/pallas_call | solution.py:454
  (78 shorter events, 2.7 us)
Async XLA Ops:
  2.4 8.8 %copy-start.5 = (s32[512]{0:T(512)S(1)}, s32[512]{0:T(512)}, u32[]{:S(2)}) copy-start(s32[512]{0:T(512)} %param.19) | copy-start | bytes 6148
  2.4 9.3 %copy-start.4 = (f32[16]{0:T(128)S(1)}, f32[16]{0:T(128)}, u32[]{:S(2)}) copy-start(f32[16]{0:T(128)} %param.14) | copy-start | bytes 196
  2.4 9.4 %copy-start.3 = (f32[8,16,3]{1,0,2:T(8,128)S(1)}, f32[8,16,3]{1,0,2:T(8,128)}, u32[]{:S(2)}) copy-start(f32[8,16,3]{1,0,2:T(8,128)} %param.13) | copy-start | bytes 4612
  2.4 9.4 %copy-start.6 = (f32[16,3]{0,1:T(4,128)S(1)}, f32[16,3]{0,1:T(4,128)}, u32[]{:S(2)}) copy-start(f32[16,3]{0,1:T(4,128)} %param.12) | copy-start | bytes 580
  2.4 9.5 %copy-start.8 = (f32[16]{0:T(128)S(1)}, f32[16]{0:T(128)}, u32[]{:S(2)}) copy-start(f32[16]{0:T(128)} %param.15) | copy-start | bytes 196
  2.4 9.5 %copy-start.9 = (f32[16]{0:T(128)S(1)}, f32[16]{0:T(128)}, u32[]{:S(2)}) copy-start(f32[16]{0:T(128)} %param.16) | copy-start | bytes 196
  2.4 9.8 %copy-start.2 = (f32[4096]{0:T(1024)S(1)}, f32[4096]{0:T(1024)}, u32[]{:S(2)}) copy-start(f32[4096]{0:T(1024)} %param.17) | copy-start | bytes 49156
  2.4 9.8 %copy-start.7 = (s32[32]{0:T(128)S(1)}, s32[32]{0:T(128)}, u32[]{:S(2)}) copy-start(s32[32]{0:T(128)} %param.18) | copy-start | bytes 388
  2.5 11.9 %copy-start.1 = (f32[8,3,4096]{2,0,1:T(8,128)S(1)}, f32[8,3,4096]{2,0,1:T(8,128)}, u32[]{:S(2)}) copy-start(f32[8,3,4096]{2,0,1:T(8,128)} %param.11) | copy-start | bytes 1179652
  2.5 22.3 %all-to-all-start = ((f32[16,2,24,128]{3,2,1,0:T(8,128)}), f32[16,2,24,128]{3,2,1,0:T(8,128)S(1)}, u32[]{:S(2)}, u32[]{:S(2)}) async-start(f32[16,2,24,128]{3,2,1,0:T(8,128)} %bitcast.2), calls=%async_computation | async-start | bytes 786432 | tf_op jit(solution)/shard_map/all_to_all | solution.py:535
  11.2 3.2 %copy-start = (f32[8,3,4096]{2,0,1:T(8,128)S(1)}, f32[8,3,4096]{2,0,1:T(8,128)}, u32[]{:S(2)}) copy-start(f32[8,3,4096]{2,0,1:T(8,128)} %param.10) | copy-start | bytes 1179652
  35.3 20.0 %all-to-all-start.1 = ((f32[16,2,24,128]{3,2,1,0:T(8,128)}), f32[16,2,24,128]{3,2,1,0:T(8,128)S(1)}, u32[]{:S(2)}, u32[]{:S(2)}) async-start(f32[16,2,24,128]{3,2,1,0:T(8,128)} %get-tuple-element.22.grad), calls=%async_computation.1 | async-start | bytes 786432 | tf_op jit(solution)/shard_map/all_to_all | solution.py:578
  55.3 15.4 %all-to-all-start.2 = ((f32[16,16,128]{2,1,0:T(8,128)}), f32[16,16,128]{2,1,0:T(8,128)S(1)}, u32[]{:S(2)}, u32[]{:S(2)}) async-start(f32[16,16,128]{2,1,0:T(8,128)} %orbital_step.1), calls=%async_computation.2 | async-start | bytes 262144 | tf_op jit(solution)/shard_map/all_to_all | solution.py:581
  73.0 21.7 %all-to-all-start.3 = ((f32[16,104,128]{2,1,0:T(8,128)}), f32[16,104,128]{2,1,0:T(8,128)S(1)}, u32[]{:S(2)}, u32[]{:S(2)}) async-start(f32[16,104,128]{2,1,0:T(8,128)} %get-tuple-element.32), calls=%async_computation.3 | async-start | bytes 1703936 | tf_op jit(solution)/shard_map/all_to_all | solution.py:584

commit v7 on v5

--- a/solution.py
+++ b/solution.py
@@ -39,10 +39,8 @@
         for h in range(2):
             for c in range(3):
                 x = pos[p, h, c * 8 : c * 8 + 8, :]
-                grad[p, h, c * 8 : c * 8 + 8, :] = zero
-                for s in range(8):
-                    rot[p, h, s, c * 8 : c * 8 + 8, :] = roll8(x, -s)
-                    back[p, h, s, c * 8 : c * 8 + 8, :] = zero
+                for s in range(1, 8):
+                    rot[p, h, s - 1, c * 8 : c * 8 + 8, :] = roll8(x, -s)
         return 0
 
     lax.fori_loop(0, EB, prepare, 0)
@@ -66,30 +64,39 @@
         for c in range(3):
             ref[(*at, slice(c * 8, c * 8 + 8), slice(None))] = values[c]
 
-    def block_pair(i, j, h, xi, gi, sums):
+    def turned(j, h, s):
+        return load3(pos, j, h) if s == 0 else load3(rot, j, h, s - 1)
+
+    def block_pair(i, j, h, xi, gi, sums, fresh=()):
         for s in range(8):
-            f, sums = terms(xi, load3(rot, j, h, s), sums, False)
+            f, sums = terms(xi, turned(j, h, s), sums, False)
             gi = [gi[c] + f[c] for c in range(3)]
-            b = load3(back, j, h, s)
-            store3(back, [b[c] + f[c] for c in range(3)], j, h, s)
+            if s not in fresh:
+                b = load3(back, j, h, s)
+                f = [b[c] + f[c] for c in range(3)]
+            store3(back, f, j, h, s)
         return gi, sums
 
     def inside(t, sums):
         out = []
+        untouched = (0, 4, 5, 6, 7)
         for h in range(2):
             acc = sums[h]
+            own = []
             for i in (2 * t, 2 * t + 1):
-                xi, gi = load3(pos, i, h), load3(grad, i, h)
+                xi, gi = load3(pos, i, h), [zero] * 3
                 for s in range(1, 5):
-                    f, acc = terms(xi, load3(rot, i, h, s), acc, s == 4)
+                    f, acc = terms(xi, turned(i, h, s), acc, s == 4)
                     gi = [gi[c] + f[c] for c in range(3)]
                     if s < 4:
-                        b = load3(back, i, h, s)
-                        store3(back, [b[c] + f[c] for c in range(3)], i, h, s)
-                store3(grad, gi, i, h)
+                        store3(back, f, i, h, s)
+                own.append(gi)
             i, j = 2 * t, 2 * t + 1
-            gi, acc = block_pair(i, j, h, load3(pos, i, h), load3(grad, i, h), acc)
+            for s in untouched:
+                store3(back, [zero] * 3, i, h, s)
+            gi, acc = block_pair(i, j, h, load3(pos, i, h), own[0], acc, untouched)
             store3(grad, gi, i, h)
+            store3(grad, own[1], j, h)
             out.append(acc)
         return tuple(out)
 
@@ -286,7 +293,7 @@
         in_specs=[vmem] * 5,
         out_specs=vmem,
         scratch_shapes=[
-            pltpu.VMEM((EB, 2, 8, 24, BLK), jnp.float32),
+            pltpu.VMEM((EB, 2, 7, 24, BLK), jnp.float32),
             pltpu.VMEM((EB, 2, 8, 24, BLK), jnp.float32),
             pltpu.VMEM((EB, 2, 24, BLK), jnp.float32),
             pltpu.VMEM((rows, width), jnp.bfloat16),
@@ -301,46 +308,55 @@
     )(whole, spread, table, nuclear, live)
 
 
-def pack_kernel(picked, returned, base, live, send, energy):
+def pack_kernel(picked, returned, base, live, send, energy, held, gone):
     sums = returned[0, 29:30, :]
     for p in range(1, EB):
         sums = sums + returned[2 * p, 29:30, :]
-    for b in range(2 * EB):
-        energy[:, b * BLK : (b + 1) * BLK] = returned[b, 24:28, :]
+    peers = held.shape[0]
+
+    def leaving(peer):
+        return pltpu.make_async_copy(held.at[peer], send.at[peer], gone.at[peer])
 
     def one_peer(peer, _):
         for k in range(CAP):
             b = picked[peer * CAP + k]
             for c in range(3):
-                send[peer, k * 24 + c * 8 : k * 24 + c * 8 + 8, :] = (
+                held[peer, k * 24 + c * 8 : k * 24 + c * 8 + 8, :] = (
                     base[b, c * 8 : c * 8 + 8, :] + TIME_STEP * returned[b, c * 8 : c * 8 + 8, :]
                 )
             alive = live[pl.ds(b, 1), :]
             level = returned[b, 28:29, :] - jnp.log(alive)
-            send[peer, 96 + k : 97 + k, :] = jnp.where(alive > 0.0, level, 3.0e38)
-        send[peer, 100:101, :] = sums
-        send[peer, 101:104, :] = jnp.zeros((3, BLK), jnp.float32)
+            held[peer, 96 + k : 97 + k, :] = jnp.where(alive > 0.0, level, 3.0e38)
+        held[peer, 100:101, :] = sums
+        held[peer, 101:104, :] = jnp.zeros((3, BLK), jnp.float32)
+        leaving(peer).start()
         return 0
 
-    lax.fori_loop(0, send.shape[0], one_peer, 0)
+    lax.fori_loop(0, peers, one_peer, 0)
+    for b in range(2 * EB):
+        energy[:, b * BLK : (b + 1) * BLK] = returned[b, 24:28, :]
+    for peer in range(peers):
+        leaving(peer).wait()
 
 
 def pack_step(picked, returned, base, live, peers):
     vmem = pl.BlockSpec(memory_space=pltpu.VMEM)
+    shape = (peers, PEER_ROWS, BLK)
     return pl.pallas_call(
         pack_kernel,
         out_shape=(
-            jax.ShapeDtypeStruct((peers, PEER_ROWS, BLK), jnp.float32),
+            jax.ShapeDtypeStruct(shape, jnp.float32),
             jax.ShapeDtypeStruct((NG // 2, 2 * EB * BLK), jnp.float32),
         ),
         in_specs=[pl.BlockSpec(memory_space=pltpu.SMEM)] + [vmem] * 3,
-        out_specs=(vmem, vmem),
+        out_specs=(pl.BlockSpec(memory_space=pltpu.HBM), vmem),
+        scratch_shapes=[pltpu.VMEM(shape, jnp.float32), pltpu.SemaphoreType.DMA((peers,))],
         compiler_params=pltpu.CompilerParams(vmem_limit_bytes=8 * 1024 * 1024),
         name="pack_step",
     )(picked, returned, base, live)
 
 
-def place_kernel(slots, half, received, moved, weights, estimate):
+def place_kernel(slots, half, received, out, weights, estimate, moved, gone):
     sums = received[0, 100:101, :]
     for peer in range(1, received.shape[0]):
         sums = sums + received[peer, 100:101, :]
@@ -350,6 +366,7 @@
     reference = jnp.sum(jnp.where(lane == 0, ratio, 0.0), axis=1, keepdims=True)[0:1, :]
     own = jnp.where(half[0] == 0, ratio, pltpu.roll(ratio, BLK - 4, axis=1))
     estimate[...] = own[0:1, 0:4]
+    copies, step = [], weights.shape[0] // 4
     for d in range(weights.shape[0]):
         peer, k = slots[d] // CAP, slots[d] % CAP
         for c in range(3):
@@ -357,6 +374,16 @@
             moved[c, :, d * BLK : (d + 1) * BLK] = received[peer, pl.ds(at, 8), :]
         level = received[peer, pl.ds(96 + k, 1), :]
         weights[d : d + 1, :] = jnp.exp(-(level - reference))
+        if (d + 1) % step == 0:
+            part = pl.ds((d + 1 - step) * BLK, step * BLK)
+            copies.append(
+                pltpu.make_async_copy(
+                    moved.at[:, :, part], out.at[:, :, part], gone.at[len(copies)]
+                )
+            )
+            copies[-1].start()
+    for copy in copies:
+        copy.wait()
 
 
 def place_step(slots, half, received):
@@ -371,7 +398,11 @@
             jax.ShapeDtypeStruct((1, NG // 2), jnp.float32),
         ),
         in_specs=[smem, smem, vmem],
-        out_specs=(vmem, vmem, vmem),
+        out_specs=(pl.BlockSpec(memory_space=pltpu.HBM), vmem, vmem),
+        scratch_shapes=[
+            pltpu.VMEM((3, 8, blocks * BLK), jnp.float32),
+            pltpu.SemaphoreType.DMA((4,)),
+        ],
         compiler_params=pltpu.CompilerParams(vmem_limit_bytes=8 * 1024 * 1024),
         name="place_step",
     )(slots, half, received)

time: 95.7 us -> 96.3 us (level)
  no operation moved by 1% of the time
where the time goes in v7:
time: 96.3 us; the launch traced here: 95.8 us
  waiting for transfers between devices  37.8 us (39%)
  Pallas kernels  29.4 us (31%)
  starting transfers between devices  19.7 us (20%)
  local copies, waits for them, and re-layouts  6.48 us (7%)
  other arithmetic  1.37 us (1%)
    pallas_call x1, Pallas kernels, walker_step(): pl.pallas_call(walker_kernel, out_shape=jax.ShapeDtypeStruct((EB, 2, 32,...  25.1 us
    all_to_all x1, waiting for transfers between devices, local(): lax.all_to_all(out, GZY, 0, 0, tiled=True).reshape(blocks_here, 32, BLK)  15.7 us
    all_to_all x1, waiting for transfers between devices, local(): received = lax.all_to_all(send, GX, 0, 0, tiled=True)  13.7 us
    all_to_all x1, starting transfers between devices, local(): whole = lax.all_to_all(sent.reshape(EB, 2, 24, BLK), GZY, 0, 0, tiled=True)  8.72 us
    all_to_all x1, waiting for transfers between devices, local(): whole = lax.all_to_all(sent.reshape(EB, 2, 24, BLK), GZY, 0, 0, tiled=True)  8.39 us
    all_to_all x1, starting transfers between devices, local(): received = lax.all_to_all(send, GX, 0, 0, tiled=True)  7.04 us
    all_to_all x1, starting transfers between devices, local(): lax.all_to_all(out, GZY, 0, 0, tiled=True).reshape(blocks_here, 32, BLK)  3.97 us
    pallas_call x1, Pallas kernels, pack_step(): pl.pallas_call(pack_kernel, out_shape=(jax.ShapeDtypeStruct(shape, jnp.fl...  2.26 us
  transfers between devices with their start and end apart: 3, of which 3 were waited for; matrix products, arithmetic and copies ran while one was open for 4% of the time, Pallas kernels for 0%

profile of v7, /device:TPU:32, one launch (start us, length us, event | category | flops | bytes accessed | tf_op | source)
XLA Modules:
  0.0 95.8 jit_solution(16806851249043265369)
XLA Ops:
  0.6 1.8 %copy.140 = f32[8,3,32,128]{3,0,1,2:T(8,128)} copy(f32[8,3,32,128]{3,0,2,1:T(8,128)} %bitcast.71) | data formatting | bytes 786432 | tf_op jit(solution)/shard_map/reshape | solution.py:456
  2.4 8.7 %all-to-all-start = ((f32[16,2,24,128]{3,2,1,0:T(8,128)}), f32[16,2,24,128]{3,2,1,0:T(8,128)S(1)}, u32[]{:S(2)}, u32[]{:S(2)}) async-start(f32[16,2,24,128]{3,2,1,0:T(8,128)} %bitcast.2), calls=%async_computation | async-start | bytes 786432 | tf_op jit(solution)/shard_map/all_to_all | solution.py:478
  11.2 0.7 copy-done.3
  11.8 0.6 copy-done.4
  12.8 0.1 stack.85
  12.9 0.1 stack.86
  14.4 0.1 stack.90
  14.6 0.1 stack.92
  14.9 0.7 copy-done.2
  15.7 0.1 copy.181.spread
  15.9 0.1 multiply_reduce_fusion
  16.1 0.2 multiply_reduce_fusion.1
  16.3 8.4 %all-to-all-done.pos = f32[16,2,24,128]{3,2,1,0:T(8,128)S(1)} async-done(((f32[16,2,24,128]{3,2,1,0:T(8,128)}), f32[16,2,24,128]{3,2,1,0:T(8,128)S(1)}, u32[]{:S(2)}, u32[]{:S(2)}) %all-to-all-start) | async-done | bytes 393248 | tf_op jit(solution)/shard_map/all_to_all | solution.py:478
  24.7 0.2 broadcast_in_dim.16.table
  24.9 25.1 %walker_step.1 = f32[16,2,32,128]{3,2,1,0:T(8,128)} custom-call(f32[16,2,24,128]{3,2,1,0:T(8,128)S(1)} %all-to-all-done.pos, f32[128,256]{1,0:T(8,128)S(1)} %copy.181.spread, f32[7,16,8,128]{3,2,1,0:T(8,128)S(1)} %broadcast_in_dim.16.table, f32[8,128]{1,0:T(8,128)S(1)} %broadcast_in_dim.17.nuclear, f32[2,128]{1,0:T(2,128)S(1)} %constant_dynamic-slice_fusion.live), custom_call_target="tpu_custom_call" | custom-call | tf_op jit(solution)/shard_map/walker_step/pallas_call | solution.py:290
  50.0 4.0 %all-to-all-start.1 = ((f32[16,2,32,128]{3,2,1,0:T(8,128)}), f32[16,2,32,128]{3,2,1,0:T(8,128)S(1)}, u32[]{:S(2)}, u32[]{:S(2)}) async-start(f32[16,2,32,128]{3,2,1,0:T(8,128)} %walker_step.1), calls=%async_computation.1 | async-start | bytes 1048576 | tf_op jit(solution)/shard_map/all_to_all | solution.py:514
  54.0 0.2 select_reduce_fusion
  54.2 0.2 convert_reduce_fusion.1
  54.5 15.7 %all-to-all-done.1 = f32[16,2,32,128]{3,2,1,0:T(8,128)S(1)} async-done(((f32[16,2,32,128]{3,2,1,0:T(8,128)}), f32[16,2,32,128]{3,2,1,0:T(8,128)S(1)}, u32[]{:S(2)}, u32[]{:S(2)}) %all-to-all-start.1) | async-done | bytes 524320 | tf_op jit(solution)/shard_map/all_to_all | solution.py:514
  70.3 2.3 %pack_step.1 = (f32[16,104,128]{2,1,0:T(8,128)}, f32[4,4096]{1,0:T(4,128)}) custom-call(s32[64]{0:T(128)S(1)} %select_reduce_fusion.1.picked, f32[32,32,128]{2,1,0:T(8,128)S(1)} %bitcast.70, f32[32,24,128]{2,1,0:T(8,128)S(1)} %fusion.base, f32[32,128]{1,0:T(8,128)S(1)} %bitcast_select_fusion.live), custom_call_target="tpu_custom_call" | custom-call | tf_op jit(solution)/shard_map/pack_step/pallas_call | solution.py:345
  72.5 7.0 %all-to-all-start.2 = ((f32[16,104,128]{2,1,0:T(8,128)}), f32[16,104,128]{2,1,0:T(8,128)S(1)}, u32[]{:S(2)}, u32[]{:S(2)}) async-start(f32[16,104,128]{2,1,0:T(8,128)} %get-tuple-element.10), calls=%async_computation.2 | async-start | bytes 1703936 | tf_op jit(solution)/shard_map/all_to_all | solution.py:516
  79.7 0.2 convert_reduce_fusion
  79.9 13.7 %all-to-all-done.2.received = f32[16,104,128]{2,1,0:T(8,128)S(1)} async-done(((f32[16,104,128]{2,1,0:T(8,128)}), f32[16,104,128]{2,1,0:T(8,128)S(1)}, u32[]{:S(2)}, u32[]{:S(2)}) %all-to-all-start.2) | async-done | bytes 852000 | tf_op jit(solution)/shard_map/all_to_all | solution.py:516
  93.7 2.1 %place_step.1 = (f32[3,8,4096]{2,1,0:T(8,128)}, f32[32,128]{1,0:T(8,128)}, f32[1,4]{1,0:T(1,128)}) custom-call(s32[32]{0:T(128)S(1)} %multiply_add_fusion.slots, s32[1]{0:T(128)} %bitcast.29.half, f32[16,104,128]{2,1,0:T(8,128)S(1)} %all-to-all-done.2.received), custom_call_target="tpu_custom_call" | custom-call | tf_op jit(solution)/shard_map/place_step/pallas_call | solution.py:393
  (70 shorter events, 2.6 us)
Async XLA Ops:
  2.4 8.7 %copy-start.6 = (f32[16,3]{0,1:T(4,128)S(1)}, f32[16,3]{0,1:T(4,128)}, u32[]{:S(2)}) copy-start(f32[16,3]{0,1:T(4,128)} %param.12) | copy-start | bytes 580
  2.4 22.3 %all-to-all-start = ((f32[16,2,24,128]{3,2,1,0:T(8,128)}), f32[16,2,24,128]{3,2,1,0:T(8,128)S(1)}, u32[]{:S(2)}, u32[]{:S(2)}) async-start(f32[16,2,24,128]{3,2,1,0:T(8,128)} %bitcast.2), calls=%async_computation | async-start | bytes 786432 | tf_op jit(solution)/shard_map/all_to_all | solution.py:478
  11.1 0.7 copy-start.3
  11.8 0.7 copy-start.4
  11.8 0.7 copy-start.8
  11.8 0.7 copy-start.9
  14.9 0.7 copy-start.2
  14.9 0.7 copy-start.7
  50.0 4.0 %copy-start.5 = (s32[512]{0:T(512)S(1)}, s32[512]{0:T(512)}, u32[]{:S(2)}) copy-start(s32[512]{0:T(512)} %param.19) | copy-start | bytes 6148
  50.0 4.5 %copy-start = (f32[8,3,4096]{2,0,1:T(8,128)S(1)}, f32[8,3,4096]{2,0,1:T(8,128)}, u32[]{:S(2)}) copy-start(f32[8,3,4096]{2,0,1:T(8,128)} %param.10) | copy-start | bytes 1179652
  50.0 4.5 %copy-start.1 = (f32[8,3,4096]{2,0,1:T(8,128)S(1)}, f32[8,3,4096]{2,0,1:T(8,128)}, u32[]{:S(2)}) copy-start(f32[8,3,4096]{2,0,1:T(8,128)} %param.11) | copy-start | bytes 1179652
  50.0 20.3 %all-to-all-start.1 = ((f32[16,2,32,128]{3,2,1,0:T(8,128)}), f32[16,2,32,128]{3,2,1,0:T(8,128)S(1)}, u32[]{:S(2)}, u32[]{:S(2)}) async-start(f32[16,2,32,128]{3,2,1,0:T(8,128)} %walker_step.1), calls=%async_computation.1 | async-start | bytes 1048576 | tf_op jit(solution)/shard_map/all_to_all | solution.py:514
  72.5 21.1 %all-to-all-start.2 = ((f32[16,104,128]{2,1,0:T(8,128)}), f32[16,104,128]{2,1,0:T(8,128)S(1)}, u32[]{:S(2)}, u32[]{:S(2)}) async-start(f32[16,104,128]{2,1,0:T(8,128)} %get-tuple-element.10), calls=%async_computation.2 | async-start | bytes 1703936 | tf_op jit(solution)/shard_map/all_to_all | solution.py:516

commit v8 on v5

--- a/solution.py
+++ b/solution.py
@@ -39,10 +39,8 @@
         for h in range(2):
             for c in range(3):
                 x = pos[p, h, c * 8 : c * 8 + 8, :]
-                grad[p, h, c * 8 : c * 8 + 8, :] = zero
-                for s in range(8):
-                    rot[p, h, s, c * 8 : c * 8 + 8, :] = roll8(x, -s)
-                    back[p, h, s, c * 8 : c * 8 + 8, :] = zero
+                for s in range(1, 8):
+                    rot[p, h, s - 1, c * 8 : c * 8 + 8, :] = roll8(x, -s)
         return 0
 
     lax.fori_loop(0, EB, prepare, 0)
@@ -66,30 +64,39 @@
         for c in range(3):
             ref[(*at, slice(c * 8, c * 8 + 8), slice(None))] = values[c]
 
-    def block_pair(i, j, h, xi, gi, sums):
+    def turned(j, h, s):
+        return load3(pos, j, h) if s == 0 else load3(rot, j, h, s - 1)
+
+    def block_pair(i, j, h, xi, gi, sums, fresh=()):
         for s in range(8):
-            f, sums = terms(xi, load3(rot, j, h, s), sums, False)
+            f, sums = terms(xi, turned(j, h, s), sums, False)
             gi = [gi[c] + f[c] for c in range(3)]
-            b = load3(back, j, h, s)
-            store3(back, [b[c] + f[c] for c in range(3)], j, h, s)
+            if s not in fresh:
+                b = load3(back, j, h, s)
+                f = [b[c] + f[c] for c in range(3)]
+            store3(back, f, j, h, s)
         return gi, sums
 
     def inside(t, sums):
         out = []
+        untouched = (0, 4, 5, 6, 7)
         for h in range(2):
             acc = sums[h]
+            own = []
             for i in (2 * t, 2 * t + 1):
-                xi, gi = load3(pos, i, h), load3(grad, i, h)
+                xi, gi = load3(pos, i, h), [zero] * 3
                 for s in range(1, 5):
-                    f, acc = terms(xi, load3(rot, i, h, s), acc, s == 4)
+                    f, acc = terms(xi, turned(i, h, s), acc, s == 4)
                     gi = [gi[c] + f[c] for c in range(3)]
                     if s < 4:
-                        b = load3(back, i, h, s)
-                        store3(back, [b[c] + f[c] for c in range(3)], i, h, s)
-                store3(grad, gi, i, h)
+                        store3(back, f, i, h, s)
+                own.append(gi)
             i, j = 2 * t, 2 * t + 1
-            gi, acc = block_pair(i, j, h, load3(pos, i, h), load3(grad, i, h), acc)
+            for s in untouched:
+                store3(back, [zero] * 3, i, h, s)
+            gi, acc = block_pair(i, j, h, load3(pos, i, h), own[0], acc, untouched)
             store3(grad, gi, i, h)
+            store3(grad, own[1], j, h)
             out.append(acc)
         return tuple(out)
 
@@ -286,7 +293,7 @@
         in_specs=[vmem] * 5,
         out_specs=vmem,
         scratch_shapes=[
-            pltpu.VMEM((EB, 2, 8, 24, BLK), jnp.float32),
+            pltpu.VMEM((EB, 2, 7, 24, BLK), jnp.float32),
             pltpu.VMEM((EB, 2, 8, 24, BLK), jnp.float32),
             pltpu.VMEM((EB, 2, 24, BLK), jnp.float32),
             pltpu.VMEM((rows, width), jnp.bfloat16),

time: 95.7 us -> 95.4 us (level)
  no operation moved by 1% of the time
where the time goes in v8:
time: 95.4 us; the launch traced here: 94.8 us
  waiting for transfers between devices  37.8 us (40%)
  Pallas kernels  28.5 us (30%)
  starting transfers between devices  19.7 us (21%)
  local copies, waits for them, and re-layouts  6.48 us (7%)
  other arithmetic  1.37 us (1%)
    pallas_call x1, Pallas kernels, walker_step(): pl.pallas_call(walker_kernel, out_shape=jax.ShapeDtypeStruct((EB, 2, 32,...  25.1 us
    all_to_all x1, waiting for transfers between devices, local(): lax.all_to_all(out, GZY, 0, 0, tiled=True).reshape(blocks_here, 32, BLK)  15.7 us
    all_to_all x1, waiting for transfers between devices, local(): received = lax.all_to_all(send, GX, 0, 0, tiled=True)  13.7 us
    all_to_all x1, starting transfers between devices, local(): whole = lax.all_to_all(sent.reshape(EB, 2, 24, BLK), GZY, 0, 0, tiled=True)  8.72 us
    all_to_all x1, waiting for transfers between devices, local(): whole = lax.all_to_all(sent.reshape(EB, 2, 24, BLK), GZY, 0, 0, tiled=True)  8.39 us
    all_to_all x1, starting transfers between devices, local(): received = lax.all_to_all(send, GX, 0, 0, tiled=True)  7.03 us
    all_to_all x1, starting transfers between devices, local(): lax.all_to_all(out, GZY, 0, 0, tiled=True).reshape(blocks_here, 32, BLK)  3.97 us
    unnamed x26, local copies, waits for them, and re-layouts  2.07 us
  transfers between devices with their start and end apart: 3, of which 3 were waited for; matrix products, arithmetic and copies ran while one was open for 4% of the time, Pallas kernels for 0%

profile of v8, /device:TPU:32, one launch (start us, length us, event | category | flops | bytes accessed | tf_op | source)
XLA Modules:
  0.0 94.8 jit_solution(17633499176532436822)
XLA Ops:
  0.6 1.8 %copy.140 = f32[8,3,32,128]{3,0,1,2:T(8,128)} copy(f32[8,3,32,128]{3,0,2,1:T(8,128)} %bitcast.71) | data formatting | bytes 786432 | tf_op jit(solution)/shard_map/reshape | solution.py:432
  2.4 8.7 %all-to-all-start = ((f32[16,2,24,128]{3,2,1,0:T(8,128)}), f32[16,2,24,128]{3,2,1,0:T(8,128)S(1)}, u32[]{:S(2)}, u32[]{:S(2)}) async-start(f32[16,2,24,128]{3,2,1,0:T(8,128)} %bitcast.2), calls=%async_computation | async-start | bytes 786432 | tf_op jit(solution)/shard_map/all_to_all | solution.py:454
  11.2 0.7 copy-done.3
  11.8 0.6 copy-done.4
  12.8 0.1 stack.85
  12.9 0.1 stack.86
  14.4 0.1 stack.90
  14.6 0.1 stack.92
  14.9 0.7 copy-done.2
  15.7 0.1 copy.181.spread
  15.9 0.1 multiply_reduce_fusion
  16.1 0.2 multiply_reduce_fusion.1
  16.3 8.4 %all-to-all-done.pos = f32[16,2,24,128]{3,2,1,0:T(8,128)S(1)} async-done(((f32[16,2,24,128]{3,2,1,0:T(8,128)}), f32[16,2,24,128]{3,2,1,0:T(8,128)S(1)}, u32[]{:S(2)}, u32[]{:S(2)}) %all-to-all-start) | async-done | bytes 393248 | tf_op jit(solution)/shard_map/all_to_all | solution.py:454
  24.7 0.2 broadcast_in_dim.16.table
  24.9 25.1 %walker_step.1 = f32[16,2,32,128]{3,2,1,0:T(8,128)} custom-call(f32[16,2,24,128]{3,2,1,0:T(8,128)S(1)} %all-to-all-done.pos, f32[128,256]{1,0:T(8,128)S(1)} %copy.181.spread, f32[7,16,8,128]{3,2,1,0:T(8,128)S(1)} %broadcast_in_dim.16.table, f32[8,128]{1,0:T(8,128)S(1)} %broadcast_in_dim.17.nuclear, f32[2,128]{1,0:T(2,128)S(1)} %constant_dynamic-slice_fusion.live), custom_call_target="tpu_custom_call" | custom-call | tf_op jit(solution)/shard_map/walker_step/pallas_call | solution.py:290
  50.0 4.0 %all-to-all-start.1 = ((f32[16,2,32,128]{3,2,1,0:T(8,128)}), f32[16,2,32,128]{3,2,1,0:T(8,128)S(1)}, u32[]{:S(2)}, u32[]{:S(2)}) async-start(f32[16,2,32,128]{3,2,1,0:T(8,128)} %walker_step.1), calls=%async_computation.1 | async-start | bytes 1048576 | tf_op jit(solution)/shard_map/all_to_all | solution.py:490
  54.0 0.2 select_reduce_fusion
  54.2 0.2 convert_reduce_fusion.1
  54.5 15.7 %all-to-all-done.1 = f32[16,2,32,128]{3,2,1,0:T(8,128)S(1)} async-done(((f32[16,2,32,128]{3,2,1,0:T(8,128)}), f32[16,2,32,128]{3,2,1,0:T(8,128)S(1)}, u32[]{:S(2)}, u32[]{:S(2)}) %all-to-all-start.1) | async-done | bytes 524320 | tf_op jit(solution)/shard_map/all_to_all | solution.py:490
  70.3 1.8 %pack_step.1 = (f32[16,104,128]{2,1,0:T(8,128)}, f32[4,4096]{1,0:T(4,128)}) custom-call(s32[64]{0:T(128)S(1)} %select_reduce_fusion.1.picked, f32[32,32,128]{2,1,0:T(8,128)S(1)} %bitcast.70, f32[32,24,128]{2,1,0:T(8,128)S(1)} %fusion.base, f32[32,128]{1,0:T(8,128)S(1)} %bitcast_select_fusion.live), custom_call_target="tpu_custom_call" | custom-call | tf_op jit(solution)/shard_map/pack_step/pallas_call | solution.py:337
  72.1 7.0 %all-to-all-start.2 = ((f32[16,104,128]{2,1,0:T(8,128)}), f32[16,104,128]{2,1,0:T(8,128)S(1)}, u32[]{:S(2)}, u32[]{:S(2)}) async-start(f32[16,104,128]{2,1,0:T(8,128)} %get-tuple-element.10), calls=%async_computation.2 | async-start | bytes 1703936 | tf_op jit(solution)/shard_map/all_to_all | solution.py:492
  79.2 0.2 convert_reduce_fusion
  79.5 13.7 %all-to-all-done.2.received = f32[16,104,128]{2,1,0:T(8,128)S(1)} async-done(((f32[16,104,128]{2,1,0:T(8,128)}), f32[16,104,128]{2,1,0:T(8,128)S(1)}, u32[]{:S(2)}, u32[]{:S(2)}) %all-to-all-start.2) | async-done | bytes 852000 | tf_op jit(solution)/shard_map/all_to_all | solution.py:492
  93.2 1.6 %place_step.1 = (f32[3,8,4096]{2,1,0:T(8,128)}, f32[32,128]{1,0:T(8,128)}, f32[1,4]{1,0:T(1,128)}) custom-call(s32[32]{0:T(128)S(1)} %multiply_add_fusion.slots, s32[1]{0:T(128)} %bitcast.29.half, f32[16,104,128]{2,1,0:T(8,128)S(1)} %all-to-all-done.2.received), custom_call_target="tpu_custom_call" | custom-call | tf_op jit(solution)/shard_map/place_step/pallas_call | solution.py:373
  (70 shorter events, 2.6 us)
Async XLA Ops:
  2.4 8.7 %copy-start.6 = (f32[16,3]{0,1:T(4,128)S(1)}, f32[16,3]{0,1:T(4,128)}, u32[]{:S(2)}) copy-start(f32[16,3]{0,1:T(4,128)} %param.12) | copy-start | bytes 580
  2.4 22.3 %all-to-all-start = ((f32[16,2,24,128]{3,2,1,0:T(8,128)}), f32[16,2,24,128]{3,2,1,0:T(8,128)S(1)}, u32[]{:S(2)}, u32[]{:S(2)}) async-start(f32[16,2,24,128]{3,2,1,0:T(8,128)} %bitcast.2), calls=%async_computation | async-start | bytes 786432 | tf_op jit(solution)/shard_map/all_to_all | solution.py:454
  11.1 0.7 copy-start.3
  11.8 0.7 copy-start.4
  11.8 0.7 copy-start.8
  11.8 0.7 copy-start.9
  14.9 0.7 copy-start.2
  14.9 0.7 copy-start.7
  50.0 4.0 %copy-start.5 = (s32[512]{0:T(512)S(1)}, s32[512]{0:T(512)}, u32[]{:S(2)}) copy-start(s32[512]{0:T(512)} %param.19) | copy-start | bytes 6148
  50.0 4.5 %copy-start = (f32[8,3,4096]{2,0,1:T(8,128)S(1)}, f32[8,3,4096]{2,0,1:T(8,128)}, u32[]{:S(2)}) copy-start(f32[8,3,4096]{2,0,1:T(8,128)} %param.10) | copy-start | bytes 1179652
  50.0 4.5 %copy-start.1 = (f32[8,3,4096]{2,0,1:T(8,128)S(1)}, f32[8,3,4096]{2,0,1:T(8,128)}, u32[]{:S(2)}) copy-start(f32[8,3,4096]{2,0,1:T(8,128)} %param.11) | copy-start | bytes 1179652
  50.0 20.3 %all-to-all-start.1 = ((f32[16,2,32,128]{3,2,1,0:T(8,128)}), f32[16,2,32,128]{3,2,1,0:T(8,128)S(1)}, u32[]{:S(2)}, u32[]{:S(2)}) async-start(f32[16,2,32,128]{3,2,1,0:T(8,128)} %walker_step.1), calls=%async_computation.1 | async-start | bytes 1048576 | tf_op jit(solution)/shard_map/all_to_all | solution.py:490
  72.1 21.1 %all-to-all-start.2 = ((f32[16,104,128]{2,1,0:T(8,128)}), f32[16,104,128]{2,1,0:T(8,128)S(1)}, u32[]{:S(2)}, u32[]{:S(2)}) async-start(f32[16,104,128]{2,1,0:T(8,128)} %get-tuple-element.10), calls=%async_computation.2 | async-start | bytes 1703936 | tf_op jit(solution)/shard_map/all_to_all | solution.py:492
